TPU v7x, 32 devices: a whole 2x2x4 slice. The times are simulated.
32 devices in a mesh: grp: 2 (over x), sec: 16 (over z, y, core).
Axes of the slice: x: 2, y: 2, z: 4, core: 2. Of those that a mesh axis runs over, the one named last changes fastest.
Arguments:
- section_tile: bfloat16 [32, 512, 512], P(('grp', 'sec')), parts along dimension 0, may hold values from -8 to 8
- placement: int32 [64, 2], P('grp'), parts along dimension 0, may hold values from 0 to 384
- tissue_mask: int32 [32, 32], P(('grp', 'sec')), parts along dimension 0, may hold values 0 or 1
- level_use: int32 [3, 64], P(None, 'grp'), parts along dimension 1, may hold values 0 or 1
Outputs:
- flow_next: float32 [32, 2, 32], P(('grp', 'sec')), parts along dimension 0
- flow_skip: float32 [32, 2, 32], P(('grp', 'sec')), parts along dimension 0
- position: float32 [32, 2, 32], P(('grp', 'sec')), parts along dimension 0
There are 2 independent parts, one for each index of `grp`. A program takes and returns all parts, laid end to end along the dimension named above; each array names one. Nothing has to cross between parts.
All inputs are finite; a program needn't handle non-finite values. No bound on the sum of `tissue_mask` on one device may be relied on, other than what follows from the above.
Results may differ from a plain program's by a relative error of at most 0.0044.
Values may be sent and summed in bfloat16 or wider, within the bound.
No kernel may reach another device: no remote copies, remote signals or barrier semaphores. Data moves between devices by JAX's collectives and lax.ppermute only.
A program may use at most 128 MiB of HBM per device.

v0:
```python
import jax
import jax.numpy as jnp
from jax import lax
from jax.sharding import PartitionSpec as P

PATCH = 128
LEVELS = 3


def passed_along(block, axis, distance):
    devices = range(lax.axis_size(axis))
    route = [(i - distance, i) for i in devices if i - distance in devices]
    return lax.ppermute(block, axis, route)


def entering(part, axis, combine, identity):
    place = lax.axis_index(axis)
    gathered = lax.all_gather(part, axis)
    state = jnp.zeros_like(part) + jnp.asarray(identity, part.dtype)

    def one(turn, state):
        return combine(state, lax.dynamic_index_in_dim(gathered, turn, 0, False))

    return lax.fori_loop(0, place, one, state)


def dft_tables():
    index = jnp.arange(PATCH, dtype=jnp.int32)
    product = index[:, None] * index[None, :] % PATCH
    angles = product.astype(jnp.float32) * (2.0 * jnp.pi / PATCH)
    return (jnp.cos(angles).astype(jnp.bfloat16), (-jnp.sin(angles)).astype(jnp.bfloat16))


def band_vector(level_number):
    index = jnp.arange(PATCH, dtype=jnp.int32)
    signed_freq = jnp.minimum(index, PATCH - index)
    return (signed_freq < PATCH // 2 ** (level_number + 1)).astype(jnp.bfloat16)


def offset_vector():
    index = jnp.arange(PATCH, dtype=jnp.int32)
    return jnp.where(index < PATCH // 2, index, index - PATCH).astype(jnp.float32)


def extract(plane, placement):

    def one_patch(corner):
        return lax.dynamic_slice(plane, (corner[0], corner[1]), (PATCH, PATCH))

    return jax.vmap(one_patch)(placement)


def matrix_product(form, left, right):
    return jnp.einsum(form, left, right, preferred_element_type=jnp.float32)


def spectrum(patches, cosine_lookup, sine_lookup):
    real_rows = matrix_product("kn,pnm->pkm", cosine_lookup, patches).astype(jnp.bfloat16)
    imag_rows = matrix_product("kn,pnm->pkm", sine_lookup, patches).astype(jnp.bfloat16)
    spec_real = (
        matrix_product("pkm,ml->pkl", real_rows, cosine_lookup)
        - matrix_product("pkm,ml->pkl", imag_rows, sine_lookup)
    ) / PATCH
    spec_imag = (
        matrix_product("pkm,ml->pkl", real_rows, sine_lookup)
        + matrix_product("pkm,ml->pkl", imag_rows, cosine_lookup)
    ) / PATCH
    return (spec_real.astype(jnp.bfloat16), spec_imag.astype(jnp.bfloat16))


def centroid(correl, offsets):
    weights = correl * correl
    total = jnp.sum(weights, axis=(1, 2)) + 1e-06
    along_rows = jnp.sum(weights * offsets[None, :, None], axis=(1, 2)) / total
    along_cols = jnp.sum(weights * offsets[None, None, :], axis=(1, 2)) / total
    return jnp.stack([along_rows, along_cols])


def pair_flow(own_real, own_imag, other_real, other_imag, cosine_lookup, sine_lookup, usage, valid):
    first_real = own_real.astype(jnp.float32)
    first_imag = own_imag.astype(jnp.float32)
    second_real = other_real.astype(jnp.float32)
    second_imag = other_imag.astype(jnp.float32)
    cross_power_real = (first_real * second_real + first_imag * second_imag).astype(jnp.bfloat16)
    cross_power_imaginary = (first_imag * second_real - first_real * second_imag).astype(
        jnp.bfloat16
    )
    offsets = offset_vector()
    estimate = jnp.zeros((2, usage.shape[1]), jnp.float32)
    for level_number in range(LEVELS):
        band_row = band_vector(level_number)
        cosine_left_factor = cosine_lookup * band_row[None, :]
        sine_left_factor = sine_lookup * band_row[None, :]
        cos_right = cosine_lookup * band_row[:, None]
        sin_right = sine_lookup * band_row[:, None]
        partial_real = (
            matrix_product("dt,hts->hds", cosine_left_factor, cross_power_real)
            + matrix_product("dt,hts->hds", sine_left_factor, cross_power_imaginary)
        ).astype(jnp.bfloat16)
        partial_imaginary = (
            matrix_product("dt,hts->hds", cosine_left_factor, cross_power_imaginary)
            - matrix_product("dt,hts->hds", sine_left_factor, cross_power_real)
        ).astype(jnp.bfloat16)
        correl = (
            matrix_product("pkq,ql->pkl", partial_real, cos_right)
            + matrix_product("pkq,ql->pkl", partial_imaginary, sin_right)
        ) / PATCH
        estimate = estimate + usage[level_number][None, :] * centroid(correl, offsets)
    count = jnp.maximum(jnp.sum(usage, axis=0), 1.0)
    return valid[None, :] * estimate / count[None, :]


def add_terms(earlier, later):
    return earlier + later


def on_device(section_tile, placement, tissue_mask, level_use):
    cosine_lookup, sine_lookup = dft_tables()
    own_real, own_imag = spectrum(extract(section_tile[0], placement), cosine_lookup, sine_lookup)
    own_flag = tissue_mask.astype(jnp.bfloat16)
    next_real, next_imag, next_flag = passed_along((own_real, own_imag, own_flag), "sec", -1)
    skip_real, skip_imag, skip_flag = passed_along((own_real, own_imag, own_flag), "sec", -2)
    usage = level_use.astype(jnp.float32)
    self_valid = tissue_mask[0].astype(jnp.float32)
    flow_next = pair_flow(
        own_real,
        own_imag,
        next_real,
        next_imag,
        cosine_lookup,
        sine_lookup,
        usage,
        self_valid * next_flag[0].astype(jnp.float32),
    )[None]
    flow_skip = pair_flow(
        own_real,
        own_imag,
        skip_real,
        skip_imag,
        cosine_lookup,
        sine_lookup,
        usage,
        self_valid * skip_flag[0].astype(jnp.float32),
    )[None]
    earlier = entering(flow_next, "sec", add_terms, jnp.zeros_like(flow_next))
    return (flow_next, flow_skip, earlier + flow_next)


def solution(mesh):
    in_specs = (
        P(("grp", "sec"), None, None),
        P("grp", None),
        P(("grp", "sec"), None),
        P(None, "grp"),
    )
    out_specs = (
        P(("grp", "sec"), None, None),
        P(("grp", "sec"), None, None),
        P(("grp", "sec"), None, None),
    )
    return jax.shard_map(
        on_device, mesh=mesh, in_specs=in_specs, out_specs=out_specs, check_vma=False
    )
```

profile of v0, /device:TPU:0, one launch (start us, length us, event | category | flops | bytes accessed | tf_op | source)
XLA Modules:
  0.0 277.1 jit_solution(1236571950580947353)
XLA Ops:
  1.4 92.6 %while.12 = (s32[]{:T(128)}, bf16[512,512]{1,0:T(8,128)(2,1)}, s32[32,2]{0,1:T(2,128)S(1)}, bf16[32,128,128]{2,1,0:T(8,128)(2,1)S(1)}, s32[]{:T(128)}) while((s32[]{:T(128)}, bf16[512,512]{1,0:T(8,128)(2,1)}, s32[32,2]{0,1:T(2,128)S(1)}, bf16[32,128,128]{2,1,0:T(8,128)(2,1)S(1)}, s32[]{:T(128)}) %tuple.89), condition=%wide.while_cond, body=%wide.while_body.sunk | while | flops 2 | bytes 65653 | solution.py:48
  2.0 2.3 bitcast_dynamic-update-slice_fusion.2
  4.9 2.3 bitcast_dynamic-update-slice_fusion.2
  7.8 2.3 bitcast_dynamic-update-slice_fusion.2
  10.7 2.3 bitcast_dynamic-update-slice_fusion.2
  13.6 2.3 bitcast_dynamic-update-slice_fusion.2
  16.5 2.3 bitcast_dynamic-update-slice_fusion.2
  19.4 2.3 bitcast_dynamic-update-slice_fusion.2
  22.3 2.3 bitcast_dynamic-update-slice_fusion.2
  25.2 2.3 bitcast_dynamic-update-slice_fusion.2
  28.1 2.3 bitcast_dynamic-update-slice_fusion.2
  31.0 2.3 bitcast_dynamic-update-slice_fusion.2
  33.9 2.3 bitcast_dynamic-update-slice_fusion.2
  36.8 2.3 bitcast_dynamic-update-slice_fusion.2
  39.7 2.3 bitcast_dynamic-update-slice_fusion.2
  42.6 2.3 bitcast_dynamic-update-slice_fusion.2
  45.5 2.3 bitcast_dynamic-update-slice_fusion.2
  48.4 2.3 bitcast_dynamic-update-slice_fusion.2
  51.3 2.3 bitcast_dynamic-update-slice_fusion.2
  54.2 2.3 bitcast_dynamic-update-slice_fusion.2
  57.0 2.2 bitcast_dynamic-update-slice_fusion.2
  59.9 2.3 bitcast_dynamic-update-slice_fusion.2
  62.8 2.3 bitcast_dynamic-update-slice_fusion.2
  65.7 2.3 bitcast_dynamic-update-slice_fusion.2
  68.6 2.3 bitcast_dynamic-update-slice_fusion.2
  71.5 2.3 bitcast_dynamic-update-slice_fusion.2
  74.4 2.3 bitcast_dynamic-update-slice_fusion.2
  77.3 2.3 bitcast_dynamic-update-slice_fusion.2
  80.2 2.3 bitcast_dynamic-update-slice_fusion.2
  83.1 2.3 bitcast_dynamic-update-slice_fusion.2
  86.0 2.3 bitcast_dynamic-update-slice_fusion.2
  88.9 2.3 bitcast_dynamic-update-slice_fusion.2
  91.8 2.3 bitcast_dynamic-update-slice_fusion.2
  96.8 1.3 collective-permute-start.2
  98.1 1.3 collective-permute-start.5
  104.9 65.9 %collective-permute-done.3 = bf16[1,32]{1,0:T(2,128)(2,1)S(1)} collective-permute-done((bf16[1,32]{1,0:T(2,128)(2,1)S(1)}, bf16[1,32]{1,0:T(2,128)(2,1)S(1)}, u32[]{:S(2)}, u32[]{:S(2)}) %collective-permute-start.3) | collective-permute-done | bytes 96 | tf_op jit(solution)/shard_map/ppermute | solution.py:13
  170.8 1.5 collective-permute-start
  172.3 1.6 collective-permute-done
  174.8 4.3 %fusion.1 = (bf16[32,128,128]{2,1,0:T(8,128)(2,1)S(1)}, bf16[32,128,128]{2,1,0:T(8,128)(2,1)S(1)}, bf16[32,128,128]{2,1,0:T(8,128)(2,1)S(1)}, bf16[32,128,128]{2,1,0:T(8,128)(2,1)S(1)}) fusion(bf16[32,128,128]{2,1,0:T(8,128)(2,1)} %collective-permute-done.1, bf16[32,128,128]{2,1,0:T(8,128)(2,1)} %copy-done.3, bf16[32,128,128]{2,1,0:T(8,128)(2,1)} %copy-done.4, ...), kind=kLoop, calls=%fused_computation.12 | loop fusion | flops 11534336 | bytes 10485760 | tf_op jit(solution)/shard_map/convert_element_type | solution.py:84
  179.2 2.0 fusion.58
  181.2 2.0 fusion.60
  183.2 2.1 fusion.38
  185.2 2.0 fusion.40
  187.2 2.0 fusion.62
  189.2 2.0 fusion.42
  191.2 1.9 fusion.64
  193.1 2.0 fusion.44
  195.2 2.0 fusion.78
  197.2 2.0 fusion.80
  199.2 2.0 fusion.82
  201.2 2.0 fusion.84
  203.2 3.9 %fusion.14 = f32[32,128,128]{2,1,0:T(8,128)} fusion(f32[32,128,128]{1,2,0:T(8,128)} %fusion.58, bf16[32,128,128]{2,1,0:T(8,128)(2,1)S(1)} %get-tuple-element.88, bf16[128]{0:T(256)(128)(2,1)S(1)} %compare_convert_fusion.1), kind=kOutput, calls=%fused_computation.59 | convolution fusion | flops 270106624 | bytes 5243136 | tf_op jit(solution)/shard_map/pkq,ql->pkl/dot_general | solution.py:54
  207.0 3.9 %fusion.17 = f32[32,128,128]{2,1,0:T(8,128)} fusion(f32[32,128,128]{1,2,0:T(8,128)} %fusion.38, bf16[32,128,128]{2,1,0:T(8,128)(2,1)S(1)} %get-tuple-element.88, bf16[128]{0:T(256)(128)(2,1)S(1)} %compare_convert_fusion), kind=kOutput, calls=%fused_computation.62 | convolution fusion | flops 270106624 | bytes 5243136 | tf_op jit(solution)/shard_map/pkq,ql->pkl/dot_general | solution.py:54
  210.9 3.9 %fusion.23 = f32[32,128,128]{2,1,0:T(8,128)} fusion(f32[32,128,128]{1,2,0:T(8,128)} %fusion.62, bf16[32,128,128]{2,1,0:T(8,128)(2,1)S(1)} %get-tuple-element.93, bf16[128]{0:T(256)(128)(2,1)S(1)} %compare_convert_fusion.1), kind=kOutput, calls=%fused_computation.68 | convolution fusion | flops 270106624 | bytes 5243136 | tf_op jit(solution)/shard_map/pkq,ql->pkl/dot_general | solution.py:54
  214.8 3.8 %fusion.26 = f32[32,128,128]{2,1,0:T(8,128)} fusion(f32[32,128,128]{1,2,0:T(8,128)} %fusion.42, bf16[32,128,128]{2,1,0:T(8,128)(2,1)S(1)} %get-tuple-element.93, bf16[128]{0:T(256)(128)(2,1)S(1)} %compare_convert_fusion), kind=kOutput, calls=%fused_computation.71 | convolution fusion | flops 270106624 | bytes 5243136 | tf_op jit(solution)/shard_map/pkq,ql->pkl/dot_general | solution.py:54
  218.6 4.1 %fusion.11 = f32[32,128,128]{2,1,0:T(8,128)} fusion(f32[32,128,128]{1,2,0:T(8,128)} %fusion.78, bf16[32,128,128]{2,1,0:T(8,128)(2,1)S(1)} %get-tuple-element.88, bf16[128]{0:T(256)(128)(2,1)S(1)} %compare_convert_fusion.2), kind=kOutput, calls=%fused_computation.56 | convolution fusion | flops 270106624 | bytes 5243136 | tf_op jit(solution)/shard_map/pkq,ql->pkl/dot_general | solution.py:54
  222.7 3.9 %fusion.20 = f32[32,128,128]{2,1,0:T(8,128)} fusion(f32[32,128,128]{1,2,0:T(8,128)} %fusion.82, bf16[32,128,128]{2,1,0:T(8,128)(2,1)S(1)} %get-tuple-element.93, bf16[128]{0:T(256)(128)(2,1)S(1)} %compare_convert_fusion.2), kind=kOutput, calls=%fused_computation.65 | convolution fusion | flops 270106624 | bytes 5243136 | tf_op jit(solution)/shard_map/pkq,ql->pkl/dot_general | solution.py:54
  226.6 4.5 %multiply_multiply_fusion.4 = f32[32,128,128]{2,1,0:T(8,128)} fusion(f32[32,128,128]{2,1,0:T(8,128)} %fusion.14, f32[32,128,128]{1,2,0:T(8,128)} %fusion.60, bf16[32,128,128]{2,1,0:T(8,128)(2,1)S(1)} %get-tuple-element.89, bf16[128]{0:T(256)(128)(2,1)S(1)} %compare_convert_fusion.1), kind=kOutput, calls=%fused_computation.41 | convolution fusion | flops 271695872 | bytes 7340288 | tf_op jit(solution)/shard_map/pkq,ql->pkl/dot_general | solution.py:54
  231.1 4.6 %multiply_multiply_fusion.3 = f32[32,128,128]{2,1,0:T(8,128)} fusion(f32[32,128,128]{2,1,0:T(8,128)} %fusion.17, f32[32,128,128]{1,2,0:T(8,128)} %fusion.40, bf16[32,128,128]{2,1,0:T(8,128)(2,1)S(1)} %get-tuple-element.89, bf16[128]{0:T(256)(128)(2,1)S(1)} %compare_convert_fusion), kind=kOutput, calls=%fused_computation.36 | convolution fusion | flops 271695872 | bytes 7340288 | tf_op jit(solution)/shard_map/pkq,ql->pkl/dot_general | solution.py:54
  235.7 4.6 %multiply_multiply_fusion.1 = f32[32,128,128]{2,1,0:T(8,128)} fusion(f32[32,128,128]{2,1,0:T(8,128)} %fusion.23, f32[32,128,128]{1,2,0:T(8,128)} %fusion.64, bf16[32,128,128]{2,1,0:T(8,128)(2,1)S(1)} %copy-done.1, bf16[128]{0:T(256)(128)(2,1)S(1)} %compare_convert_fusion.1), kind=kOutput, calls=%fused_computation.26 | convolution fusion | flops 271695872 | bytes 7340288 | tf_op jit(solution)/shard_map/pkq,ql->pkl/dot_general | solution.py:54
  240.3 4.5 %multiply_multiply_fusion = f32[32,128,128]{2,1,0:T(8,128)} fusion(f32[32,128,128]{2,1,0:T(8,128)} %fusion.26, f32[32,128,128]{1,2,0:T(8,128)} %fusion.44, bf16[32,128,128]{2,1,0:T(8,128)(2,1)S(1)} %copy-done.1, bf16[128]{0:T(256)(128)(2,1)S(1)} %compare_convert_fusion), kind=kOutput, calls=%fused_computation.21 | convolution fusion | flops 271695872 | bytes 7340288 | tf_op jit(solution)/shard_map/pkq,ql->pkl/dot_general | solution.py:54
  244.8 4.5 %multiply_multiply_fusion.5 = f32[32,128,128]{2,1,0:T(8,128)} fusion(f32[32,128,128]{2,1,0:T(8,128)} %fusion.11, f32[32,128,128]{1,2,0:T(8,128)} %fusion.80, bf16[32,128,128]{2,1,0:T(8,128)(2,1)S(1)} %get-tuple-element.89, bf16[128]{0:T(256)(128)(2,1)S(1)} %compare_convert_fusion.2), kind=kOutput, calls=%fused_computation.46 | convolution fusion | flops 271695872 | bytes 7340288 | tf_op jit(solution)/shard_map/pkq,ql->pkl/dot_general | solution.py:54
  249.3 7.3 %multiply_reduce_fusion.5 = (f32[32]{0:T(128)S(1)}, f32[32]{0:T(128)S(1)}, f32[32]{0:T(128)S(1)}, f32[32]{0:T(128)S(1)}, f32[32]{0:T(128)S(1)}, /*index=5*/f32[3...) fusion(f32[128]{0:T(128)S(1)} %fusion.222, ...), kind=kOutput, calls=%fused_computation.30 | convolution fusion | flops 287423936 | bytes 15731712 | tf_op jit(solution)/shard_map/pkq,ql->pkl/dot_general | solution.py:54
  256.7 19.8 %all_gather.3 = f32[16,1,2,32]{3,2,1,0:T(2,128)S(1)} all-gather(f32[1,1,2,32]{3,2,1,0:T(2,128)S(1)} %fusion.219), channel_id=1, replica_groups=mesh['grp'=2,'sec'=16] {'sec'}, dimensions={0}, use_global_device_ids=true | all-gather | bytes 4352 | tf_op jit(solution)/shard_map/all_gather | solution.py:18
  (112 shorter events, 29.5 us)
Async XLA Ops:
  96.8 4.0 %copy-start.2 = (bf16[32,128,128]{2,1,0:T(8,128)(2,1)}, bf16[32,128,128]{2,1,0:T(8,128)(2,1)S(1)}, u32[]{:S(2)}) copy-start(bf16[32,128,128]{2,1,0:T(8,128)(2,1)S(1)} %multiply_convert_fusion) | copy-start | bytes 3145732
  96.8 77.0 %collective-permute-start.2 = (bf16[32,128,128]{2,1,0:T(8,128)(2,1)S(1)}, bf16[32,128,128]{2,1,0:T(8,128)(2,1)S(1)}, u32[]{:S(2)}, u32[]{:S(2)}) collective-permute-start(bf16[32,128,128]{2,1,0:T(8,128)(2,1)S(1)} %multiply_convert_fusion), channel_id=1, source_target_pairs={{1,0},{2,1},{3,2},{4,3},{5,4},{6,5},{7,6},{8,7},{9,8},{10,9},{11,1... | collective-permute-start | bytes 3145736 | tf_op jit(solution)/shard_map/ppermute | solution.py:13
  98.1 75.7 %collective-permute-start.5 = (bf16[32,128,128]{2,1,0:T(8,128)(2,1)S(1)}, bf16[32,128,128]{2,1,0:T(8,128)(2,1)}, u32[]{:S(2)}, u32[]{:S(2)}) collective-permute-start(bf16[32,128,128]{2,1,0:T(8,128)(2,1)S(1)} %multiply_convert_fusion), channel_id=1, source_target_pairs={{2,0},{3,1},{4,2},{5,3},{6,4},{7,5},{8,6},{9,7},{10,8},{11,9},{12,... | collective-permute-start | bytes 3145736 | tf_op jit(solution)/shard_map/ppermute | solution.py:13
  100.1 3.3 %copy-start.6 = (s32[1,32]{1,0:T(1,128)S(1)}, s32[1,32]{1,0:T(1,128)}, u32[]{:S(2)}) copy-start(s32[1,32]{1,0:T(1,128)} %param.8) | copy-start | bytes 388
  100.1 4.7 %copy-start.5 = (s32[3,32]{1,0:T(4,128)S(1)}, s32[3,32]{1,0:T(4,128)}, u32[]{:S(2)}) copy-start(s32[3,32]{1,0:T(4,128)} %param.9) | copy-start | bytes 1156
  100.9 73.0 %copy-start.3 = (bf16[32,128,128]{2,1,0:T(8,128)(2,1)}, bf16[32,128,128]{2,1,0:T(8,128)(2,1)S(1)}, u32[]{:S(2)}) copy-start(bf16[32,128,128]{2,1,0:T(8,128)(2,1)S(1)} %multiply_convert_fusion.1) | copy-start | bytes 3145732
  100.9 73.0 %collective-permute-start.1 = (bf16[32,128,128]{2,1,0:T(8,128)(2,1)S(1)}, bf16[32,128,128]{2,1,0:T(8,128)(2,1)}, u32[]{:S(2)}, u32[]{:S(2)}) collective-permute-start(bf16[32,128,128]{2,1,0:T(8,128)(2,1)S(1)} %multiply_convert_fusion.1), channel_id=1, source_target_pairs={{1,0},{2,1},{3,2},{4,3},{5,4},{6,5},{7,6},{8,7},{9,8},{10,9},{11,1... | collective-permute-start | bytes 3145736 | tf_op jit(solution)/shard_map/ppermute | solution.py:13
  102.2 72.7 %collective-permute-start.4 = (bf16[32,128,128]{2,1,0:T(8,128)(2,1)S(1)}, bf16[32,128,128]{2,1,0:T(8,128)(2,1)}, u32[]{:S(2)}, u32[]{:S(2)}) collective-permute-start(bf16[32,128,128]{2,1,0:T(8,128)(2,1)S(1)} %multiply_convert_fusion.1), channel_id=1, source_target_pairs={{2,0},{3,1},{4,2},{5,3},{6,4},{7,5},{8,6},{9,7},{10,8},{11,9},{12,... | collective-permute-start | bytes 3145736 | tf_op jit(solution)/shard_map/ppermute | solution.py:13
  103.5 67.3 %collective-permute-start.3 = (bf16[1,32]{1,0:T(2,128)(2,1)S(1)}, bf16[1,32]{1,0:T(2,128)(2,1)S(1)}, u32[]{:S(2)}, u32[]{:S(2)}) collective-permute-start(bf16[1,32]{1,0:T(2,128)(2,1)S(1)} %convert_element_type.449), channel_id=1, source_target_pairs={{2,0},{3,1},{4,2},{5,3},{6,4},{7,5},{8,6},{9,7},{10,8},{11,9},{12,... | collective-permute-start | bytes 200 | tf_op jit(solution)/shard_map/ppermute | solution.py:13
  170.8 3.0 %collective-permute-start = (bf16[1,32]{1,0:T(2,128)(2,1)S(1)}, bf16[1,32]{1,0:T(2,128)(2,1)S(1)}, u32[]{:S(2)}, u32[]{:S(2)}) collective-permute-start(bf16[1,32]{1,0:T(2,128)(2,1)S(1)} %convert_element_type.449), channel_id=1, source_target_pairs={{1,0},{2,1},{3,2},{4,3},{5,4},{6,5},{7,6},{8,7},{9,8},{10,9},{11,1... | collective-permute-start | bytes 200 | tf_op jit(solution)/shard_map/ppermute | solution.py:13
  173.9 1.0 copy-start.4
  179.1 20.1 %copy-start = (bf16[32,128,128]{2,1,0:T(8,128)(2,1)}, bf16[32,128,128]{2,1,0:T(8,128)(2,1)S(1)}, u32[]{:S(2)}) copy-start(bf16[32,128,128]{2,1,0:T(8,128)(2,1)S(1)} %get-tuple-element.92) | copy-start | bytes 3145732
  231.1 4.6 %copy-start.1 = (bf16[32,128,128]{2,1,0:T(8,128)(2,1)S(1)}, bf16[32,128,128]{2,1,0:T(8,128)(2,1)}, u32[]{:S(2)}) copy-start(bf16[32,128,128]{2,1,0:T(8,128)(2,1)} %copy-done) | copy-start | bytes 3145732
where the time goes:
time: 280 us; the launch traced here: 277 us
  local copies, waits for them, and re-layouts  93.1 us (33%)
  matrix products  81.6 us (29%)
  waiting for transfers between devices  67.5 us (24%)
  blocking collectives  19.8 us (7%)
  starting transfers between devices  7.92 us (3%)
  other arithmetic  5.77 us (2%)
    gather x96, local copies, waits for them, and re-layouts  92.1 us
    dot_general x30, matrix products, matrix_product(): return jnp.einsum(form, left, right, preferred_element_type=jnp.float32)  81.6 us
    ppermute x6, waiting for transfers between devices, passed_along(): return lax.ppermute(block, axis, route)  67.5 us
    all_gather x1, blocking collectives, entering(): gathered = lax.all_gather(part, axis)  19.8 us
    ppermute x6, starting transfers between devices, passed_along(): return lax.ppermute(block, axis, route)  7.92 us
  transfers between devices with their start and end apart: 6, of which 2 were waited for; matrix products, arithmetic and copies ran while one was open for 1% of the time, Pallas kernels for 0%

commit v1 on v0

v1 whole, which is shorter than its diff:
```python
import functools

import jax
import jax.numpy as jnp
import numpy as np
from jax import lax
from jax.experimental import pallas as pl
from jax.experimental.pallas import tpu as pltpu
from jax.sharding import PartitionSpec as P

PATCH = 128
LEVELS = 3
HALF = PATCH // 2
QUAD = 4


def tables():
    index = np.arange(PATCH)
    angles = ((index[:, None] * index[None, :]) % PATCH).astype(np.float32) * np.float32(2.0 * np.pi / PATCH)
    cosine = np.cos(angles).astype(jnp.bfloat16).astype(np.float32)
    sine = (-np.sin(angles)).astype(jnp.bfloat16).astype(np.float32)
    zero = np.zeros((PATCH, HALF), np.float32)
    window = np.zeros((4, 3 * PATCH, PATCH), np.float32)
    cos_half, sin_half = cosine[:, :HALF], sine[:, :HALF]
    for place, part in enumerate(
        ([cos_half, zero], [sin_half, zero], [zero, cos_half], [zero, sin_half])
    ):
        window[place, PATCH : 2 * PATCH] = np.concatenate(part, axis=1)
    forward = np.concatenate([cosine, sine], axis=1) / PATCH
    inverse_rows = np.zeros((LEVELS * 2 * PATCH, 2 * PATCH), np.float32)
    inverse_cols = np.zeros((LEVELS, 2 * PATCH, 2 * PATCH), np.float32)
    signed = np.minimum(index, PATCH - index)
    twice = np.where(np.arange(HALF) == 0, 1.0, 2.0)[:, None]
    for level in range(LEVELS):
        band = (signed < PATCH // 2 ** (level + 1)).astype(np.float32)
        cos_left, sin_left = cosine * band[None, :], sine * band[None, :]
        top = 2 * PATCH * level
        inverse_rows[top : top + PATCH] = np.concatenate([cos_left, sin_left], axis=1)
        inverse_rows[top + PATCH : top + 2 * PATCH] = np.concatenate([-sin_left, cos_left], axis=1)
        weight = twice * band[:HALF, None] / PATCH
        cos_right, sin_right = cosine[:HALF] * weight, sine[:HALF] * weight
        for member in range(2):
            cols = slice(member * PATCH, (member + 1) * PATCH)
            inverse_cols[level, member * HALF : (member + 1) * HALF, cols] = cos_right
            inverse_cols[level, PATCH + member * HALF : PATCH + (member + 1) * HALF, cols] = sin_right
    offset = np.where(index < HALF, index, index - PATCH).astype(np.float32)
    moments = np.zeros((8, PATCH), np.float32)
    moments[0] = 1.0
    moments[1] = offset
    offset_rows = np.broadcast_to(offset[:, None], (PATCH, PATCH)).copy()
    return (
        jnp.asarray(window),
        jnp.asarray(forward, jnp.bfloat16),
        jnp.asarray(inverse_rows, jnp.bfloat16),
        jnp.asarray(inverse_cols, jnp.bfloat16),
        jnp.asarray(moments),
        jnp.asarray(offset_rows),
    )


def product(left, right):
    return jnp.dot(left, right, preferred_element_type=jnp.float32)


def fill_panels(tile_ref, panels):
    for panel in range(panels.shape[0]):
        panels[panel] = tile_ref[:, panel * PATCH : (panel + 1) * PATCH].astype(jnp.float32)


def pair_spectrum(pair, place_ref, panels, window_ref, forward):
    last = panels.shape[0] - 2
    total = None
    for member in range(2):
        row = place_ref[2 * pair + member, 0]
        col = place_ref[2 * pair + member, 1]
        panel = jnp.minimum(col // PATCH, last)
        shift = col - panel * PATCH
        patch = jnp.concatenate(
            [panels[panel, pl.ds(row, PATCH), :], panels[panel + 1, pl.ds(row, PATCH), :]], axis=1
        ).astype(jnp.bfloat16)
        table = jnp.concatenate(
            [
                window_ref[2 * member, pl.ds(PATCH - shift, 2 * PATCH), :],
                window_ref[2 * member + 1, pl.ds(PATCH - shift, 2 * PATCH), :],
            ],
            axis=1,
        ).astype(jnp.bfloat16)
        term = product(patch, table)
        total = term if total is None else total + term
    cols = total.astype(jnp.bfloat16)
    turned = jnp.concatenate([-cols[:, PATCH:], cols[:, :PATCH]], axis=1)
    return product(forward, jnp.concatenate([cols, turned], axis=0)).astype(jnp.bfloat16)


def spectrum_kernel(place_ref, tile_ref, window_ref, forward_ref, spec_ref, panels):
    fill_panels(tile_ref, panels)
    forward = forward_ref[...]

    def step(pair, carry):
        spec_ref[pair] = pair_spectrum(pair, place_ref, panels, window_ref, forward)
        return carry

    lax.fori_loop(0, spec_ref.shape[0], step, 0)


def estimate(
    place_ref, tile_ref, spec_ref, usage_ref, window_ref, forward_ref, rows_ref, cols_ref, moments_ref,
    offset_ref, panels, col_sums, row_sums,
):
    fill_panels(tile_ref, panels)

    def step(quad, carry):
        forward = forward_ref[...]
        real, imag = [], []
        for pair in range(QUAD // 2):
            other = pair_spectrum(quad * (QUAD // 2) + pair, place_ref, panels, window_ref, forward)
            own = spec_ref[quad * (QUAD // 2) + pair].astype(jnp.float32)
            other = other.astype(jnp.float32)
            own_real, own_imag = own[:, :PATCH], own[:, PATCH:]
            other_real, other_imag = other[:, :PATCH], other[:, PATCH:]
            real.append((own_real * other_real + own_imag * other_imag).astype(jnp.bfloat16))
            imag.append((own_imag * other_real - own_real * other_imag).astype(jnp.bfloat16))
        cross = jnp.concatenate([jnp.concatenate(real, axis=1), jnp.concatenate(imag, axis=1)], axis=0)
        offsets = offset_ref[...]
        offsets = jnp.concatenate([offsets, offsets], axis=1)
        for level in range(LEVELS):
            top = 2 * PATCH * level
            half = product(rows_ref[top : top + 2 * PATCH], cross).astype(jnp.bfloat16)
            for pair in range(QUAD // 2):
                lanes = slice(pair * PATCH, (pair + 1) * PATCH)
                line = jnp.concatenate([half[:PATCH, lanes], half[PATCH:, lanes]], axis=1)
                correl = product(line, cols_ref[level])
                weight = correl * correl
                by_col = jnp.sum(weight, axis=0, keepdims=True)
                by_row = jnp.sum(weight * offsets, axis=0, keepdims=True)
                for member in range(2):
                    place = quad * QUAD + 2 * pair + member
                    part = slice(member * PATCH, (member + 1) * PATCH)
                    col_sums[level, pl.ds(place, 1), :] = by_col[:, part]
                    row_sums[level, pl.ds(place, 1), :] = by_row[:, part]
        return carry

    lax.fori_loop(0, place_ref.shape[0] // QUAD, step, 0)
    usage = usage_ref[...].astype(jnp.float32)
    moments = moments_ref[...]
    across = (((1,), (1,)), ((), ()))
    along_rows, along_cols = 0.0, 0.0
    for level in range(LEVELS):
        col_part = lax.dot_general(
            moments, col_sums[level], across, precision=lax.Precision.HIGHEST,
            preferred_element_type=jnp.float32,
        )
        row_part = lax.dot_general(
            moments, row_sums[level], across, precision=lax.Precision.HIGHEST,
            preferred_element_type=jnp.float32,
        )
        scale = usage[level : level + 1] / (col_part[0:1] + 1e-6)
        along_rows = along_rows + row_part[0:1] * scale
        along_cols = along_cols + col_part[1:2] * scale
    count = jnp.maximum(jnp.sum(usage, axis=0, keepdims=True), 1.0)
    return jnp.concatenate([along_rows, along_cols], axis=0) / count


def next_kernel(*refs):
    ins, out_ref, scratch = refs[:10], refs[10], refs[11:]
    out_ref[...] = estimate(*ins, *scratch)


def skip_kernel(turn_ref, *refs):
    ins, shared_ref, outs, scratch = refs[:10], refs[10], refs[11:14], refs[14:]
    skip = estimate(*ins, *scratch)
    me = turn_ref[0]
    sections = shared_ref.shape[0]

    def mask_of(section):
        held = shared_ref[jnp.minimum(section, sections - 1), 2:3, :]
        return jnp.where(section < sections, held, jnp.zeros_like(held))

    def flow_of(section):
        return shared_ref[section, 0:2, :] * (mask_of(section) * mask_of(section + 1))

    flow_next = flow_of(me)
    outs[0][0] = flow_next
    outs[1][0] = skip * (mask_of(me) * mask_of(me + 2))
    outs[2][0] = lax.fori_loop(
        0, me, lambda section, held: held + flow_of(section), jnp.zeros_like(flow_next)
    ) + flow_next


def passed_along(block, axis, distance):
    devices = range(lax.axis_size(axis))
    route = [(i - distance, i) for i in devices if i - distance in devices]
    return lax.ppermute(block, axis, route)


def on_device(section_tile, placement, tissue_mask, level_use):
    window, forward, inverse_rows, inverse_cols, moments, offset_rows = tables()
    patches = placement.shape[0]
    side = section_tile.shape[1]
    tile = section_tile[0]
    sections = lax.axis_size("sec")
    vmem = pl.BlockSpec(memory_space=pltpu.VMEM)
    smem = pl.BlockSpec(memory_space=pltpu.SMEM)
    panels = pltpu.VMEM((side // PATCH, side, PATCH), jnp.float32)
    sums = pltpu.VMEM((LEVELS, patches, PATCH), jnp.float32)
    params = pltpu.CompilerParams(vmem_limit_bytes=24 * 2**20)

    next_tile = passed_along(tile, "sec", -1)
    own_spec = pl.pallas_call(
        spectrum_kernel,
        out_shape=jax.ShapeDtypeStruct((patches // 2, PATCH, 2 * PATCH), jnp.bfloat16),
        in_specs=[smem, vmem, vmem, vmem],
        out_specs=vmem,
        scratch_shapes=[panels],
        compiler_params=params,
        cost_estimate=pl.CostEstimate(flops=4 * 10**9, bytes_accessed=3 * 2**20, transcendentals=0),
        name="own_spectrum",
    )(placement, tile, window, forward)
    skip_tile = passed_along(next_tile, "sec", -1)

    kernel_cost = pl.CostEstimate(flops=8 * 10**9, bytes_accessed=4 * 2**20, transcendentals=0)
    shared_ins = (level_use, window, forward, inverse_rows, inverse_cols, moments, offset_rows)
    specs = [smem] + [vmem] * 9
    flow = pl.pallas_call(
        next_kernel,
        out_shape=jax.ShapeDtypeStruct((2, patches), jnp.float32),
        in_specs=specs,
        out_specs=vmem,
        scratch_shapes=[panels, sums, sums],
        compiler_params=params,
        cost_estimate=kernel_cost,
        name="flow_next",
    )(placement, next_tile, own_spec, *shared_ins)
    message = jnp.concatenate([flow, tissue_mask.astype(jnp.float32)], axis=0)
    shared = lax.all_to_all(jnp.broadcast_to(message, (sections,) + message.shape), "sec", 0, 0)
    turn = jnp.reshape(lax.axis_index("sec"), (1,)).astype(jnp.int32)
    out = jax.ShapeDtypeStruct((1, 2, patches), jnp.float32)
    return pl.pallas_call(
        skip_kernel,
        out_shape=(out, out, out),
        in_specs=[smem] + specs + [vmem],
        out_specs=(vmem, vmem, vmem),
        scratch_shapes=[panels, sums, sums],
        compiler_params=params,
        cost_estimate=kernel_cost,
        name="flow_skip",
    )(turn, placement, skip_tile, own_spec, *shared_ins, shared)


def solution(mesh):
    in_specs = (
        P(("grp", "sec"), None, None),
        P("grp", None),
        P(("grp", "sec"), None),
        P(None, "grp"),
    )
    out_specs = (
        P(("grp", "sec"), None, None),
        P(("grp", "sec"), None, None),
        P(("grp", "sec"), None, None),
    )
    return jax.shard_map(
        on_device, mesh=mesh, in_specs=in_specs, out_specs=out_specs, check_vma=False
    )
```

time: 280 us -> 53.3 us (0.19)
  local copies, waits for them, and re-layouts: 93.1 us -> 4.99 us
  matrix products: 81.6 us -> 0 us
  waiting for transfers between devices: 67.5 us -> 6.63 us
  Pallas kernels: 0 us -> 28.4 us
  blocking collectives: 19.8 us -> 0 us
  other arithmetic: 5.77 us -> 0.01 us
  starting transfers between devices: 7.92 us -> 12 us
    gather x96 -> x0, local copies, waits for them, and re-layouts: 92.1 us -> none
    dot_general x30 -> x0, matrix products: 81.6 us -> none  [matrix_product(): return jnp.einsum(form, left, right, preferred_element_type=jnp.float32)]
    ppermute x6 -> x2, waiting for transfers between devices: 67.5 us -> 0.01 us  [passed_along(): return lax.ppermute(block, axis, route)]
    pallas_call x0 -> x3, Pallas kernels: none -> 28.4 us  [the longest x1 10.9 us: on_device(): pl.pallas_call(skip_kernel, out_shape=(out, out, out), in_specs=[smem] +...]
    all_gather x1 -> x0, blocking collectives: 19.8 us -> none  [entering(): gathered = lax.all_gather(part, axis)]
    all_to_all x0 -> x1, starting transfers between devices: none -> 9.27 us  [on_device(): lax.all_to_all(jnp.broadcast_to(message, (sections,) + message.shape), 's...]
    all_to_all x0 -> x1, waiting for transfers between devices: none -> 6.63 us  [on_device(): lax.all_to_all(jnp.broadcast_to(message, (sections,) + message.shape), 's...]
    ppermute x6 -> x2, starting transfers between devices: 7.92 us -> 2.72 us  [passed_along(): return lax.ppermute(block, axis, route)]
  transfers between devices with their start and end apart: 6 -> 3, of which waited for: 2 -> 1; matrix products, arithmetic and copies ran while one was open for 1% -> 1% of each run, Pallas kernels for 0% -> 33%
where the time goes in v1:
time: 53.3 us; the launch traced here: 52.9 us
  Pallas kernels  28.4 us (53%)
  starting transfers between devices  12 us (23%)
  waiting for transfers between devices  6.63 us (12%)
  local copies, waits for them, and re-layouts  4.99 us (9%)
  between operations  0.83 us (2%)
    pallas_call x1, Pallas kernels, on_device(): pl.pallas_call(skip_kernel, out_shape=(out, out, out), in_specs=[smem] +...  10.9 us
    pallas_call x1, Pallas kernels, on_device(): pl.pallas_call(next_kernel, out_shape=jax.ShapeDtypeStruct((2, patches),...  10.3 us
    all_to_all x1, starting transfers between devices, on_device(): lax.all_to_all(jnp.broadcast_to(message, (sections,) + message.shape), 's...  9.27 us
    pallas_call x1, Pallas kernels, on_device(): pl.pallas_call(spectrum_kernel, out_shape=jax.ShapeDtypeStruct((patches /...  7.24 us
    all_to_all x1, waiting for transfers between devices, on_device(): lax.all_to_all(jnp.broadcast_to(message, (sections,) + message.shape), 's...  6.63 us
    unnamed x29, local copies, waits for them, and re-layouts  4.39 us
    ppermute x2, starting transfers between devices, passed_along(): return lax.ppermute(block, axis, route)  2.72 us
  transfers between devices with their start and end apart: 3, of which 1 were waited for; matrix products, arithmetic and copies ran while one was open for 1% of the time, Pallas kernels for 33%

profile of v1, /device:TPU:0, one launch (start us, length us, event | category | flops | bytes accessed | tf_op | source)
XLA Modules:
  0.0 52.9 jit_solution(7177636904790963808)
XLA Ops:
  0.6 0.0 copy-start.13
  0.6 0.0 copy-start.12
  0.7 1.4 %collective-permute-start = (bf16[512,512]{1,0:T(8,128)(2,1)}, bf16[512,512]{1,0:T(8,128)(2,1)S(1)}, u32[]{:S(2)}, u32[]{:S(2)}) collective-permute-start(bf16[512,512]{1,0:T(8,128)(2,1)} %bitcast.2), channel_id=1, source_target_pairs={{1,0},{2,1},{3,2},{4,3},{5,4},{6,5},{7,6},{8,7},{9,8},{10,9},{11,1... | collective-permute-start | bytes 1572872 | tf_op jit(solution)/shard_map/ppermute | solution.py:193
  2.1 0.0 copy-done.13
  2.1 0.0 copy-done.12
  2.1 0.1 copy.15.place_ref.refs_0_
  2.2 0.0 copy-start
  2.2 1.0 %copy-done = bf16[1,512,512]{2,1,0:T(8,128)(2,1)S(1)} copy-done((bf16[1,512,512]{2,1,0:T(8,128)(2,1)S(1)}, bf16[1,512,512]{2,1,0:T(8,128)(2,1)}, u32[]{:S(2)}) %copy-start) | copy-done | bytes 524312
  3.2 0.0 copy-start.2
  3.2 1.1 %copy-done.2 = f32[4,384,128]{2,1,0:T(8,128)S(1)} copy-done((f32[4,384,128]{2,1,0:T(8,128)S(1)}, f32[4,384,128]{2,1,0:T(8,128)}, u32[]{:S(2)}) %copy-start.2) | copy-done | bytes 786456
  4.4 0.0 copy-start.6
  4.4 0.8 %copy-done.6 = bf16[128,256]{1,0:T(8,128)(2,1)S(1)} copy-done((bf16[128,256]{1,0:T(8,128)(2,1)S(1)}, bf16[128,256]{1,0:T(8,128)(2,1)}, u32[]{:S(2)}) %copy-start.6) | copy-done | bytes 65560
  5.2 0.0 copy-start.1
  5.2 0.0 copy-start.3
  5.2 0.0 copy-start.4
  5.2 0.0 copy-start.5
  5.2 0.0 copy-start.7
  5.2 0.0 copy-start.8
  5.3 0.0 copy-start.9
  5.3 7.2 %own_spectrum.1.refs_2_ = bf16[16,128,256]{2,1,0:T(8,128)(2,1)S(1)} custom-call(s32[32,2]{1,0:T(8,128)S(1)} %copy.15.place_ref.refs_0_, bf16[512,512]{1,0:T(8,128)(2,1)S(1)} %bitcast.3, f32[4,384,128]{2,1,0:T(8,128)S(1)} %copy-done.2, bf16[128,256]{1,0:T(8,128)(2,1)S(1)} %copy-done.6), custom_call_target="tpu_custom_call" | custom-call | flops 4000000000 | bytes 3145728 | tf_op jit(solution)/shard_map/own_spectrum/pallas_call | solution.py:209
  12.5 0.0 copy-start.10
  12.5 0.0 collective-permute-done.refs_1_
  12.5 1.3 %collective-permute-start.1 = (bf16[512,512]{1,0:T(8,128)(2,1)S(1)}, bf16[512,512]{1,0:T(8,128)(2,1)S(1)}, u32[]{:S(2)}, u32[]{:S(2)}) collective-permute-start(bf16[512,512]{1,0:T(8,128)(2,1)S(1)} %collective-permute-done.refs_1_), channel_id=1, source_target_pairs={{1,0},{2,1},{3,2},{4,3},{5,4},{6,5},{7,6},{8,7},{9,8},{10,9},{11,1... | collective-permute-start | bytes 1572872 | tf_op jit(solution)/shard_map/ppermute | solution.py:193
  13.8 0.0 copy-done.1
  13.8 0.0 copy-done.3
  13.9 0.0 copy-done.4
  13.9 0.0 copy-done.5
  13.9 0.0 copy-done.7
  13.9 0.0 copy-done.8
  13.9 0.0 copy-done.9
  13.9 10.3 %flow_next.1 = f32[2,32]{1,0:T(2,128)S(1)} custom-call(s32[32,2]{1,0:T(8,128)S(1)} %copy.15.place_ref.refs_0_, bf16[512,512]{1,0:T(8,128)(2,1)S(1)} %collective-permute-done.refs_1_, bf16[16,128,256]{2,1,0:T(8,128)(2,1)S(1)} %own_spectrum.1.refs_2_, s32[3,32]{1,0:T(4,128)S(1)} %copy-done.1, f32[4,384,128]{2,1,0:T(8,128)S(1)} %copy-done.3, ...), custom_call_target="tpu_custom_call" | custom-call | flops 8000000000 | bytes 4194304 | tf_op jit(solution)/shard_map/flow_next/pallas_call | solution.py:224
  24.2 0.0 copy-done.10
  24.2 0.6 %broadcast_in_dim.3 = f32[16,3,32]{2,1,0:T(4,128)} broadcast(f32[3,32]{1,0:T(4,128)S(1)} %pad_maximum_fusion), dimensions={1,2} | broadcast | bytes 6528 | tf_op jit(solution)/shard_map/broadcast_in_dim | solution.py:235
  24.9 9.3 %all-to-all-start = ((f32[16,3,32]{2,1,0:T(4,128)}), f32[16,3,32]{2,1,0:T(4,128)S(1)}, u32[]{:S(2)}, u32[]{:S(2)}) async-start(f32[16,3,32]{2,1,0:T(4,128)} %broadcast_in_dim.3), calls=%async_computation | async-start | bytes 65536 | tf_op jit(solution)/shard_map/all_to_all | solution.py:235
  34.1 6.6 %all-to-all-done.refs_10_ = f32[16,3,32]{2,1,0:T(4,128)S(1)} async-done(((f32[16,3,32]{2,1,0:T(4,128)}), f32[16,3,32]{2,1,0:T(4,128)S(1)}, u32[]{:S(2)}, u32[]{:S(2)}) %all-to-all-start) | async-done | bytes 6176 | tf_op jit(solution)/shard_map/all_to_all | solution.py:235
  40.8 0.0 collective-permute-done.1.refs_1_
  40.8 0.0 copy-start.11
  40.8 1.2 %copy-done.11 = bf16[16,128,256]{2,1,0:T(8,128)(2,1)S(1)} copy-done((bf16[16,128,256]{2,1,0:T(8,128)(2,1)S(1)}, bf16[16,128,256]{2,1,0:T(8,128)(2,1)}, u32[]{:S(2)}) %copy-start.11) | copy-done | bytes 1048600
  42.0 10.9 %flow_skip.1 = (f32[1,2,32]{2,1,0:T(2,128)}, f32[1,2,32]{2,1,0:T(2,128)}, f32[1,2,32]{2,1,0:T(2,128)}) custom-call(s32[1]{0:T(128)} %bitcast.turn_ref, s32[32,2]{1,0:T(8,128)S(1)} %copy.15.place_ref.refs_0_, bf16[512,512]{1,0:T(8,128)(2,1)S(1)} %collective-permute-done.1.refs_1_, bf16[16,128,256]{2,1,0:T(8,128)(2,1)S(1)} %copy-done.11, ...), custom_call_target="tpu_custom_call" | custom-call | flops 8000000000 | bytes 4194304 | tf_op jit(solution)/shard_map/flow_skip/pallas_call | solution.py:238
  (2 shorter events, 0.0 us)
Async XLA Ops:
  0.6 1.5 %copy-start.13 = (s32[1,32]{1,0:T(1,128)S(1)}, s32[1,32]{1,0:T(1,128)}, u32[]{:S(2)}) copy-start(s32[1,32]{1,0:T(1,128)} %param.12) | copy-start | bytes 388
  0.6 1.5 %copy-start.12 = (s32[32,2]{0,1:T(2,128)S(1)}, s32[32,2]{0,1:T(2,128)}, u32[]{:S(2)}) copy-start(s32[32,2]{0,1:T(2,128)} %param.11) | copy-start | bytes 772
  0.7 11.9 %collective-permute-start = (bf16[512,512]{1,0:T(8,128)(2,1)}, bf16[512,512]{1,0:T(8,128)(2,1)S(1)}, u32[]{:S(2)}, u32[]{:S(2)}) collective-permute-start(bf16[512,512]{1,0:T(8,128)(2,1)} %bitcast.2), channel_id=1, source_target_pairs={{1,0},{2,1},{3,2},{4,3},{5,4},{6,5},{7,6},{8,7},{9,8},{10,9},{11,1... | collective-permute-start | bytes 1572872 | tf_op jit(solution)/shard_map/ppermute | solution.py:193
  2.2 1.0 %copy-start = (bf16[1,512,512]{2,1,0:T(8,128)(2,1)S(1)}, bf16[1,512,512]{2,1,0:T(8,128)(2,1)}, u32[]{:S(2)}) copy-start(bf16[1,512,512]{2,1,0:T(8,128)(2,1)} %param.10) | copy-start | bytes 1572868
  3.2 1.1 %copy-start.2 = (f32[4,384,128]{2,1,0:T(8,128)S(1)}, f32[4,384,128]{2,1,0:T(8,128)}, u32[]{:S(2)}) copy-start(f32[4,384,128]{2,1,0:T(8,128)} %constant.16.clone.window_ref.refs_4_) | copy-start | bytes 2359300
  4.4 0.8 %copy-start.6 = (bf16[128,256]{1,0:T(8,128)(2,1)S(1)}, bf16[128,256]{1,0:T(8,128)(2,1)}, u32[]{:S(2)}) copy-start(bf16[128,256]{1,0:T(8,128)(2,1)} %constant.17.clone.forward_ref.refs_5_) | copy-start | bytes 196612
  5.2 8.6 %copy-start.1 = (s32[3,32]{1,0:T(4,128)S(1)}, s32[3,32]{1,0:T(4,128)}, u32[]{:S(2)}) copy-start(s32[3,32]{1,0:T(4,128)} %refs_3_.3) | copy-start | bytes 1156
  5.2 8.6 %copy-start.3 = (f32[4,384,128]{2,1,0:T(8,128)S(1)}, f32[4,384,128]{2,1,0:T(8,128)}, u32[]{:S(2)}) copy-start(f32[4,384,128]{2,1,0:T(8,128)} %constant.16.clone.window_ref.refs_4_) | copy-start | bytes 2359300
  5.2 8.6 %copy-start.4 = (bf16[3,256,256]{2,1,0:T(8,128)(2,1)S(1)}, bf16[3,256,256]{2,1,0:T(8,128)(2,1)}, u32[]{:S(2)}) copy-start(bf16[3,256,256]{2,1,0:T(8,128)(2,1)} %constant.19.clone.refs_7_) | copy-start | bytes 1179652
  5.2 8.6 %copy-start.5 = (bf16[768,256]{1,0:T(8,128)(2,1)S(1)}, bf16[768,256]{1,0:T(8,128)(2,1)}, u32[]{:S(2)}) copy-start(bf16[768,256]{1,0:T(8,128)(2,1)} %constant.18.clone.refs_6_) | copy-start | bytes 1179652
  5.2 8.6 %copy-start.7 = (bf16[128,256]{1,0:T(8,128)(2,1)S(1)}, bf16[128,256]{1,0:T(8,128)(2,1)}, u32[]{:S(2)}) copy-start(bf16[128,256]{1,0:T(8,128)(2,1)} %constant.17.clone.forward_ref.refs_5_) | copy-start | bytes 196612
  5.2 8.6 %copy-start.8 = (f32[128,128]{1,0:T(8,128)S(1)}, f32[128,128]{1,0:T(8,128)}, u32[]{:S(2)}) copy-start(f32[128,128]{1,0:T(8,128)} %constant.21.clone.refs_9_) | copy-start | bytes 196612
  5.3 8.6 %copy-start.9 = (f32[8,128]{1,0:T(8,128)S(1)}, f32[8,128]{1,0:T(8,128)}, u32[]{:S(2)}) copy-start(f32[8,128]{1,0:T(8,128)} %constant.20.clone.refs_8_) | copy-start | bytes 12292
  12.5 11.7 %copy-start.10 = (bf16[16,128,256]{2,1,0:T(8,128)(2,1)}, bf16[16,128,256]{2,1,0:T(8,128)(2,1)S(1)}, u32[]{:S(2)}) copy-start(bf16[16,128,256]{2,1,0:T(8,128)(2,1)S(1)} %own_spectrum.1.refs_2_) | copy-start | bytes 3145732
  12.5 28.2 %collective-permute-start.1 = (bf16[512,512]{1,0:T(8,128)(2,1)S(1)}, bf16[512,512]{1,0:T(8,128)(2,1)S(1)}, u32[]{:S(2)}, u32[]{:S(2)}) collective-permute-start(bf16[512,512]{1,0:T(8,128)(2,1)S(1)} %collective-permute-done.refs_1_), channel_id=1, source_target_pairs={{1,0},{2,1},{3,2},{4,3},{5,4},{6,5},{7,6},{8,7},{9,8},{10,9},{11,1... | collective-permute-start | bytes 1572872 | tf_op jit(solution)/shard_map/ppermute | solution.py:193
  24.9 15.9 %all-to-all-start = ((f32[16,3,32]{2,1,0:T(4,128)}), f32[16,3,32]{2,1,0:T(4,128)S(1)}, u32[]{:S(2)}, u32[]{:S(2)}) async-start(f32[16,3,32]{2,1,0:T(4,128)} %broadcast_in_dim.3), calls=%async_computation | async-start | bytes 65536 | tf_op jit(solution)/shard_map/all_to_all | solution.py:235
  40.8 1.2 %copy-start.11 = (bf16[16,128,256]{2,1,0:T(8,128)(2,1)S(1)}, bf16[16,128,256]{2,1,0:T(8,128)(2,1)}, u32[]{:S(2)}) copy-start(bf16[16,128,256]{2,1,0:T(8,128)(2,1)} %copy-done.10) | copy-start | bytes 3145732

commit v2 on v1

--- a/solution.py
+++ b/solution.py
@@ -47,14 +47,12 @@
     moments = np.zeros((8, PATCH), np.float32)
     moments[0] = 1.0
     moments[1] = offset
-    offset_rows = np.broadcast_to(offset[:, None], (PATCH, PATCH)).copy()
     return (
         jnp.asarray(window),
         jnp.asarray(forward, jnp.bfloat16),
         jnp.asarray(inverse_rows, jnp.bfloat16),
         jnp.asarray(inverse_cols, jnp.bfloat16),
         jnp.asarray(moments),
-        jnp.asarray(offset_rows),
     )
 
 
@@ -105,54 +103,70 @@
 
 def estimate(
     place_ref, tile_ref, spec_ref, usage_ref, window_ref, forward_ref, rows_ref, cols_ref, moments_ref,
-    offset_ref, panels, col_sums, row_sums,
+    panels, cross_ref, half_ref, plain, nested,
 ):
     fill_panels(tile_ref, panels)
-
-    def step(quad, carry):
+    quads = place_ref.shape[0] // QUAD
+
+    def cross_stage(quad, slot):
         forward = forward_ref[...]
-        real, imag = [], []
         for pair in range(QUAD // 2):
-            other = pair_spectrum(quad * (QUAD // 2) + pair, place_ref, panels, window_ref, forward)
-            own = spec_ref[quad * (QUAD // 2) + pair].astype(jnp.float32)
-            other = other.astype(jnp.float32)
+            place = quad * (QUAD // 2) + pair
+            other = pair_spectrum(place, place_ref, panels, window_ref, forward).astype(jnp.float32)
+            own = spec_ref[place].astype(jnp.float32)
             own_real, own_imag = own[:, :PATCH], own[:, PATCH:]
             other_real, other_imag = other[:, :PATCH], other[:, PATCH:]
-            real.append((own_real * other_real + own_imag * other_imag).astype(jnp.bfloat16))
-            imag.append((own_imag * other_real - own_real * other_imag).astype(jnp.bfloat16))
-        cross = jnp.concatenate([jnp.concatenate(real, axis=1), jnp.concatenate(imag, axis=1)], axis=0)
-        offsets = offset_ref[...]
-        offsets = jnp.concatenate([offsets, offsets], axis=1)
+            lanes = slice(pair * PATCH, (pair + 1) * PATCH)
+            cross_ref[slot, :PATCH, lanes] = (own_real * other_real + own_imag * other_imag).astype(jnp.bfloat16)
+            cross_ref[slot, PATCH:, lanes] = (own_imag * other_real - own_real * other_imag).astype(jnp.bfloat16)
+
+    def half_stage(slot):
+        half_ref[slot] = product(rows_ref[...], cross_ref[slot]).astype(jnp.bfloat16)
+
+    def sums_stage(quad, slot):
         for level in range(LEVELS):
             top = 2 * PATCH * level
-            half = product(rows_ref[top : top + 2 * PATCH], cross).astype(jnp.bfloat16)
+            lines = [
+                jnp.concatenate(
+                    [
+                        half_ref[slot, top : top + PATCH, pair * PATCH : (pair + 1) * PATCH],
+                        half_ref[slot, top + PATCH : top + 2 * PATCH, pair * PATCH : (pair + 1) * PATCH],
+                    ],
+                    axis=1,
+                )
+                for pair in range(QUAD // 2)
+            ]
+            correl = product(jnp.concatenate(lines, axis=0), cols_ref[level])
             for pair in range(QUAD // 2):
-                lanes = slice(pair * PATCH, (pair + 1) * PATCH)
-                line = jnp.concatenate([half[:PATCH, lanes], half[PATCH:, lanes]], axis=1)
-                correl = product(line, cols_ref[level])
-                weight = correl * correl
-                by_col = jnp.sum(weight, axis=0, keepdims=True)
-                by_row = jnp.sum(weight * offsets, axis=0, keepdims=True)
+                running, ladder = None, None
+                for turn in range(PATCH // 8):
+                    row = pair * PATCH + (turn * 8 + HALF) % PATCH
+                    block = correl[row : row + 8]
+                    weight = block * block
+                    running = weight if running is None else running + weight
+                    ladder = running if ladder is None else ladder + running
                 for member in range(2):
                     place = quad * QUAD + 2 * pair + member
                     part = slice(member * PATCH, (member + 1) * PATCH)
-                    col_sums[level, pl.ds(place, 1), :] = by_col[:, part]
-                    row_sums[level, pl.ds(place, 1), :] = by_row[:, part]
-        return carry
-
-    lax.fori_loop(0, place_ref.shape[0] // QUAD, step, 0)
+                    plain[level, place] = running[:, part]
+                    nested[level, place] = ladder[:, part]
+
+    schedule(quads, cross_stage, half_stage, sums_stage)
     usage = usage_ref[...].astype(jnp.float32)
     moments = moments_ref[...]
     across = (((1,), (1,)), ((), ()))
     along_rows, along_cols = 0.0, 0.0
     for level in range(LEVELS):
+        by_col, by_row = 0.0, 0.0
+        for sublane in range(8):
+            part = plain[level, :, sublane, :]
+            by_col = by_col + part
+            by_row = by_row + ((HALF + sublane) * part - 8.0 * nested[level, :, sublane, :])
         col_part = lax.dot_general(
-            moments, col_sums[level], across, precision=lax.Precision.HIGHEST,
-            preferred_element_type=jnp.float32,
+            moments, by_col, across, precision=lax.Precision.HIGHEST, preferred_element_type=jnp.float32
         )
         row_part = lax.dot_general(
-            moments, row_sums[level], across, precision=lax.Precision.HIGHEST,
-            preferred_element_type=jnp.float32,
+            moments, by_row, across, precision=lax.Precision.HIGHEST, preferred_element_type=jnp.float32
         )
         scale = usage[level : level + 1] / (col_part[0:1] + 1e-6)
         along_rows = along_rows + row_part[0:1] * scale
@@ -161,14 +175,22 @@
     return jnp.concatenate([along_rows, along_cols], axis=0) / count
 
 
-def next_kernel(*refs):
-    ins, out_ref, scratch = refs[:10], refs[10], refs[11:]
+def schedule(quads, cross_stage, half_stage, sums_stage):
+    for turn in range(quads + 2):
+        if turn >= 2:
+            sums_stage(turn - 2, turn % 2)
+        if 1 <= turn <= quads:
+            half_stage((turn - 1) % 2)
+        if turn < quads:
+            cross_stage(turn, turn % 2)
+
+
+def flow_kernel(*refs):
+    ins, out_ref, scratch = refs[:9], refs[9], refs[10:]
     out_ref[...] = estimate(*ins, *scratch)
 
 
-def skip_kernel(turn_ref, *refs):
-    ins, shared_ref, outs, scratch = refs[:10], refs[10], refs[11:14], refs[14:]
-    skip = estimate(*ins, *scratch)
+def combine_kernel(turn_ref, shared_ref, skip_ref, *outs):
     me = turn_ref[0]
     sections = shared_ref.shape[0]
 
@@ -181,7 +203,7 @@
 
     flow_next = flow_of(me)
     outs[0][0] = flow_next
-    outs[1][0] = skip * (mask_of(me) * mask_of(me + 2))
+    outs[1][0] = skip_ref[...] * (mask_of(me) * mask_of(me + 2))
     outs[2][0] = lax.fori_loop(
         0, me, lambda section, held: held + flow_of(section), jnp.zeros_like(flow_next)
     ) + flow_next
@@ -194,7 +216,7 @@
 
 
 def on_device(section_tile, placement, tissue_mask, level_use):
-    window, forward, inverse_rows, inverse_cols, moments, offset_rows = tables()
+    window, forward, inverse_rows, inverse_cols, moments = tables()
     patches = placement.shape[0]
     side = section_tile.shape[1]
     tile = section_tile[0]
@@ -202,7 +224,7 @@
     vmem = pl.BlockSpec(memory_space=pltpu.VMEM)
     smem = pl.BlockSpec(memory_space=pltpu.SMEM)
     panels = pltpu.VMEM((side // PATCH, side, PATCH), jnp.float32)
-    sums = pltpu.VMEM((LEVELS, patches, PATCH), jnp.float32)
+    sums = pltpu.VMEM((LEVELS, patches, 8, PATCH), jnp.float32)
     params = pltpu.CompilerParams(vmem_limit_bytes=24 * 2**20)
 
     next_tile = passed_along(tile, "sec", -1)
@@ -218,33 +240,37 @@
     )(placement, tile, window, forward)
     skip_tile = passed_along(next_tile, "sec", -1)
 
-    kernel_cost = pl.CostEstimate(flops=8 * 10**9, bytes_accessed=4 * 2**20, transcendentals=0)
-    shared_ins = (level_use, window, forward, inverse_rows, inverse_cols, moments, offset_rows)
-    specs = [smem] + [vmem] * 9
-    flow = pl.pallas_call(
-        next_kernel,
-        out_shape=jax.ShapeDtypeStruct((2, patches), jnp.float32),
-        in_specs=specs,
-        out_specs=vmem,
-        scratch_shapes=[panels, sums, sums],
-        compiler_params=params,
-        cost_estimate=kernel_cost,
-        name="flow_next",
-    )(placement, next_tile, own_spec, *shared_ins)
-    message = jnp.concatenate([flow, tissue_mask.astype(jnp.float32)], axis=0)
+    def flow(other_tile, name):
+        return pl.pallas_call(
+            flow_kernel,
+            out_shape=jax.ShapeDtypeStruct((2, patches), jnp.float32),
+            in_specs=[smem] + [vmem] * 8,
+            out_specs=vmem,
+            scratch_shapes=[
+                panels,
+                pltpu.VMEM((2, 2 * PATCH, 2 * PATCH), jnp.bfloat16),
+                pltpu.VMEM((2, LEVELS * 2 * PATCH, 2 * PATCH), jnp.bfloat16),
+                sums,
+                sums,
+            ],
+            compiler_params=params,
+            cost_estimate=pl.CostEstimate(flops=8 * 10**9, bytes_accessed=4 * 2**20, transcendentals=0),
+            name=name,
+        )(placement, other_tile, own_spec, level_use, window, forward, inverse_rows, inverse_cols, moments)
+
+    flow_next = flow(next_tile, "flow_next")
+    message = jnp.concatenate([flow_next, tissue_mask.astype(jnp.float32)], axis=0)
     shared = lax.all_to_all(jnp.broadcast_to(message, (sections,) + message.shape), "sec", 0, 0)
+    flow_skip = flow(skip_tile, "flow_skip")
     turn = jnp.reshape(lax.axis_index("sec"), (1,)).astype(jnp.int32)
     out = jax.ShapeDtypeStruct((1, 2, patches), jnp.float32)
     return pl.pallas_call(
-        skip_kernel,
+        combine_kernel,
         out_shape=(out, out, out),
-        in_specs=[smem] + specs + [vmem],
+        in_specs=[smem, vmem, vmem],
         out_specs=(vmem, vmem, vmem),
-        scratch_shapes=[panels, sums, sums],
-        compiler_params=params,
-        cost_estimate=kernel_cost,
-        name="flow_skip",
-    )(turn, placement, skip_tile, own_spec, *shared_ins, shared)
+        name="combine",
+    )(turn, shared, flow_skip)
 
 
 def solution(mesh):

time: 53.3 us -> 41.3 us (0.77)
  Pallas kernels: 28.4 us -> 20.6 us
  waiting for transfers between devices: 6.63 us -> 0.01 us
  local copies, waits for them, and re-layouts: 4.99 us -> 7.52 us
    pallas_call x2 -> x3, Pallas kernels: 21.2 us -> 13.4 us  [the longest x2 12 us: flow(): pl.pallas_call(flow_kernel, out_shape=jax.ShapeDtypeStruct((2, patches),...]
    all_to_all x1, waiting for transfers between devices: 6.63 us -> 0.01 us  [on_device(): lax.all_to_all(jnp.broadcast_to(message, (sections,) + message.shape), 's...]
    unnamed x29 -> x31, local copies, waits for them, and re-layouts: 4.39 us -> 6.9 us
  transfers between devices with their start and end apart: 3 -> 3, of which waited for: 1 -> 0; matrix products, arithmetic and copies ran while one was open for 1% -> 2% of each run, Pallas kernels for 33% -> 47%
where the time goes in v2:
time: 41.3 us; the launch traced here: 40.8 us
  Pallas kernels  20.6 us (50%)
  starting transfers between devices  11.9 us (29%)
  local copies, waits for them, and re-layouts  7.52 us (18%)
  between operations  0.81 us (2%)
    pallas_call x2, Pallas kernels, flow(): pl.pallas_call(flow_kernel, out_shape=jax.ShapeDtypeStruct((2, patches),...  12 us
    all_to_all x1, starting transfers between devices, on_device(): lax.all_to_all(jnp.broadcast_to(message, (sections,) + message.shape), 's...  9.27 us
    pallas_call x1, Pallas kernels, on_device(): pl.pallas_call(spectrum_kernel, out_shape=jax.ShapeDtypeStruct((patches /...  7.23 us
    unnamed x31, local copies, waits for them, and re-layouts  6.9 us
    ppermute x2, starting transfers between devices, passed_along(): return lax.ppermute(block, axis, route)  2.58 us
    pallas_call x1, Pallas kernels, on_device(): pl.pallas_call(combine_kernel, out_shape=(out, out, out), in_specs=[smem,...  1.34 us
  transfers between devices with their start and end apart: 3, of which 0 were waited for; matrix products, arithmetic and copies ran while one was open for 2% of the time, Pallas kernels for 47%

profile of v2, /device:TPU:0, one launch (start us, length us, event | category | flops | bytes accessed | tf_op | source)
XLA Modules:
  0.0 40.8 jit_solution(7916026617768903592)
XLA Ops:
  0.6 1.3 %collective-permute-start = (bf16[512,512]{1,0:T(8,128)(2,1)}, bf16[512,512]{1,0:T(8,128)(2,1)S(1)}, u32[]{:S(2)}, u32[]{:S(2)}) collective-permute-start(bf16[512,512]{1,0:T(8,128)(2,1)} %bitcast.2), channel_id=1, source_target_pairs={{1,0},{2,1},{3,2},{4,3},{5,4},{6,5},{7,6},{8,7},{9,8},{10,9},{11,1... | collective-permute-start | bytes 1572872 | tf_op jit(solution)/shard_map/ppermute | solution.py:215
  1.9 0.0 copy-start.14
  1.9 0.6 %copy-done.14 = s32[1,32]{1,0:T(1,128)S(1)} copy-done((s32[1,32]{1,0:T(1,128)S(1)}, s32[1,32]{1,0:T(1,128)}, u32[]{:S(2)}) %copy-start.14) | copy-done | bytes 152
  2.6 0.0 copy-start.13
  2.6 0.7 %copy-done.13 = s32[32,2]{0,1:T(2,128)S(1)} copy-done((s32[32,2]{0,1:T(2,128)S(1)}, s32[32,2]{0,1:T(2,128)}, u32[]{:S(2)}) %copy-start.13) | copy-done | bytes 280
  3.3 0.1 copy.13.place_ref.refs_0_
  3.4 0.0 copy-start.1
  3.4 1.0 %copy-done.1 = bf16[1,512,512]{2,1,0:T(8,128)(2,1)S(1)} copy-done((bf16[1,512,512]{2,1,0:T(8,128)(2,1)S(1)}, bf16[1,512,512]{2,1,0:T(8,128)(2,1)}, u32[]{:S(2)}) %copy-start.1) | copy-done | bytes 524312
  4.4 0.0 copy-start.3
  4.4 1.1 %copy-done.3 = f32[4,384,128]{2,1,0:T(8,128)S(1)} copy-done((f32[4,384,128]{2,1,0:T(8,128)S(1)}, f32[4,384,128]{2,1,0:T(8,128)}, u32[]{:S(2)}) %copy-start.3) | copy-done | bytes 786456
  5.5 0.0 copy-start.7
  5.5 0.8 %copy-done.7 = bf16[128,256]{1,0:T(8,128)(2,1)S(1)} copy-done((bf16[128,256]{1,0:T(8,128)(2,1)S(1)}, bf16[128,256]{1,0:T(8,128)(2,1)}, u32[]{:S(2)}) %copy-start.7) | copy-done | bytes 65560
  6.4 0.0 copy-start.2
  6.4 0.0 copy-start.4
  6.4 0.0 copy-start.5
  6.4 0.0 copy-start.6
  6.4 0.0 copy-start.8
  6.4 0.0 copy-start.9
  6.4 7.2 %own_spectrum.1.refs_2_ = bf16[16,128,256]{2,1,0:T(8,128)(2,1)S(1)} custom-call(s32[32,2]{1,0:T(8,128)S(1)} %copy.13.place_ref.refs_0_, bf16[512,512]{1,0:T(8,128)(2,1)S(1)} %bitcast.3, f32[4,384,128]{2,1,0:T(8,128)S(1)} %copy-done.3, bf16[128,256]{1,0:T(8,128)(2,1)S(1)} %copy-done.7), custom_call_target="tpu_custom_call" | custom-call | flops 4000000000 | bytes 3145728 | tf_op jit(solution)/shard_map/own_spectrum/pallas_call | solution.py:231
  13.6 0.0 copy-start.10
  13.7 0.0 collective-permute-done.refs_1_
  13.7 1.3 %collective-permute-start.1 = (bf16[512,512]{1,0:T(8,128)(2,1)S(1)}, bf16[512,512]{1,0:T(8,128)(2,1)S(1)}, u32[]{:S(2)}, u32[]{:S(2)}) collective-permute-start(bf16[512,512]{1,0:T(8,128)(2,1)S(1)} %collective-permute-done.refs_1_), channel_id=1, source_target_pairs={{1,0},{2,1},{3,2},{4,3},{5,4},{6,5},{7,6},{8,7},{9,8},{10,9},{11,1... | collective-permute-start | bytes 1572872 | tf_op jit(solution)/shard_map/ppermute | solution.py:215
  15.0 0.0 copy-done.2
  15.0 0.0 copy-done.4
  15.0 0.0 copy-done.5
  15.0 0.0 copy-done.6
  15.0 0.0 copy-done.8
  15.0 0.0 copy-done.9
  15.0 6.0 %flow_next.1 = f32[2,32]{1,0:T(2,128)S(1)} custom-call(s32[32,2]{1,0:T(8,128)S(1)} %copy.13.place_ref.refs_0_, bf16[512,512]{1,0:T(8,128)(2,1)S(1)} %collective-permute-done.refs_1_, bf16[16,128,256]{2,1,0:T(8,128)(2,1)S(1)} %own_spectrum.1.refs_2_, s32[3,32]{1,0:T(4,128)S(1)} %copy-done.2, f32[4,384,128]{2,1,0:T(8,128)S(1)} %copy-done.4, ...), custom_call_target="tpu_custom_call" | custom-call | flops 8000000000 | bytes 4194304 | tf_op jit(solution)/shard_map/flow_next/pallas_call | solution.py:244
  21.1 0.0 copy-done.10
  21.1 0.6 %broadcast_in_dim.3 = f32[16,3,32]{2,1,0:T(4,128)} broadcast(f32[3,32]{1,0:T(4,128)S(1)} %pad_maximum_fusion), dimensions={1,2} | broadcast | bytes 6528 | tf_op jit(solution)/shard_map/broadcast_in_dim | solution.py:263
  21.7 9.3 %all-to-all-start = ((f32[16,3,32]{2,1,0:T(4,128)}), f32[16,3,32]{2,1,0:T(4,128)S(1)}, u32[]{:S(2)}, u32[]{:S(2)}) async-start(f32[16,3,32]{2,1,0:T(4,128)} %broadcast_in_dim.3), calls=%async_computation | async-start | bytes 65536 | tf_op jit(solution)/shard_map/all_to_all | solution.py:263
  31.0 0.0 collective-permute-done.1.refs_1_
  31.0 0.0 copy-start.11
  31.0 1.2 %copy-done.11 = bf16[16,128,256]{2,1,0:T(8,128)(2,1)S(1)} copy-done((bf16[16,128,256]{2,1,0:T(8,128)(2,1)S(1)}, bf16[16,128,256]{2,1,0:T(8,128)(2,1)}, u32[]{:S(2)}) %copy-start.11) | copy-done | bytes 1048600
  32.2 6.0 %flow_skip.1.skip_ref = f32[2,32]{1,0:T(2,128)S(1)} custom-call(s32[32,2]{1,0:T(8,128)S(1)} %copy.13.place_ref.refs_0_, bf16[512,512]{1,0:T(8,128)(2,1)S(1)} %collective-permute-done.1.refs_1_, bf16[16,128,256]{2,1,0:T(8,128)(2,1)S(1)} %copy-done.11, s32[3,32]{1,0:T(4,128)S(1)} %copy-done.2, f32[4,384,128]{2,1,0:T(8,128)S(1)} %copy-done.4, ...), custom_call_target="tpu_custom_call" | custom-call | flops 8000000000 | bytes 4194304 | tf_op jit(solution)/shard_map/flow_skip/pallas_call | solution.py:244
  38.2 0.0 copy-start
  38.3 0.6 %copy-done = f32[2,32]{1,0:T(2,128)} copy-done((f32[2,32]{1,0:T(2,128)}, f32[2,32]{1,0:T(2,128)S(1)}, u32[]{:S(2)}) %copy-start) | copy-done | bytes 280
  38.9 0.0 all-to-all-done.shared_ref
  38.9 0.0 copy-start.12
  38.9 0.6 %copy-done.12 = f32[16,3,32]{2,1,0:T(4,128)} copy-done((f32[16,3,32]{2,1,0:T(4,128)}, f32[16,3,32]{2,1,0:T(4,128)S(1)}, u32[]{:S(2)}) %copy-start.12) | copy-done | bytes 6168
  39.5 1.3 %combine.1 = (f32[1,2,32]{2,1,0:T(2,128)}, f32[1,2,32]{2,1,0:T(2,128)}, f32[1,2,32]{2,1,0:T(2,128)}) custom-call(s32[1]{0:T(128)} %bitcast.turn_ref, f32[16,3,32]{2,1,0:T(4,128)} %copy-done.12, f32[2,32]{1,0:T(2,128)} %copy-done), custom_call_target="tpu_custom_call" | custom-call | tf_op jit(solution)/shard_map/combine/pallas_call | solution.py:267
  (2 shorter events, 0.0 us)
Async XLA Ops:
  0.6 13.0 %collective-permute-start = (bf16[512,512]{1,0:T(8,128)(2,1)}, bf16[512,512]{1,0:T(8,128)(2,1)S(1)}, u32[]{:S(2)}, u32[]{:S(2)}) collective-permute-start(bf16[512,512]{1,0:T(8,128)(2,1)} %bitcast.2), channel_id=1, source_target_pairs={{1,0},{2,1},{3,2},{4,3},{5,4},{6,5},{7,6},{8,7},{9,8},{10,9},{11,1... | collective-permute-start | bytes 1572872 | tf_op jit(solution)/shard_map/ppermute | solution.py:215
  1.9 0.7 %copy-start.14 = (s32[1,32]{1,0:T(1,128)S(1)}, s32[1,32]{1,0:T(1,128)}, u32[]{:S(2)}) copy-start(s32[1,32]{1,0:T(1,128)} %param.11) | copy-start | bytes 388
  2.6 0.7 %copy-start.13 = (s32[32,2]{0,1:T(2,128)S(1)}, s32[32,2]{0,1:T(2,128)}, u32[]{:S(2)}) copy-start(s32[32,2]{0,1:T(2,128)} %param.10) | copy-start | bytes 772
  3.4 1.0 %copy-start.1 = (bf16[1,512,512]{2,1,0:T(8,128)(2,1)S(1)}, bf16[1,512,512]{2,1,0:T(8,128)(2,1)}, u32[]{:S(2)}) copy-start(bf16[1,512,512]{2,1,0:T(8,128)(2,1)} %param.9) | copy-start | bytes 1572868
  4.4 1.1 %copy-start.3 = (f32[4,384,128]{2,1,0:T(8,128)S(1)}, f32[4,384,128]{2,1,0:T(8,128)}, u32[]{:S(2)}) copy-start(f32[4,384,128]{2,1,0:T(8,128)} %constant.14.clone.window_ref.refs_4_) | copy-start | bytes 2359300
  5.5 0.8 %copy-start.7 = (bf16[128,256]{1,0:T(8,128)(2,1)S(1)}, bf16[128,256]{1,0:T(8,128)(2,1)}, u32[]{:S(2)}) copy-start(bf16[128,256]{1,0:T(8,128)(2,1)} %constant.15.clone.forward_ref.refs_5_) | copy-start | bytes 196612
  6.4 8.6 %copy-start.2 = (s32[3,32]{1,0:T(4,128)S(1)}, s32[3,32]{1,0:T(4,128)}, u32[]{:S(2)}) copy-start(s32[3,32]{1,0:T(4,128)} %refs_3_.3) | copy-start | bytes 1156
  6.4 8.6 %copy-start.4 = (f32[4,384,128]{2,1,0:T(8,128)S(1)}, f32[4,384,128]{2,1,0:T(8,128)}, u32[]{:S(2)}) copy-start(f32[4,384,128]{2,1,0:T(8,128)} %constant.14.clone.window_ref.refs_4_) | copy-start | bytes 2359300
  6.4 8.6 %copy-start.5 = (bf16[3,256,256]{2,1,0:T(8,128)(2,1)S(1)}, bf16[3,256,256]{2,1,0:T(8,128)(2,1)}, u32[]{:S(2)}) copy-start(bf16[3,256,256]{2,1,0:T(8,128)(2,1)} %constant.17.clone.refs_7_) | copy-start | bytes 1179652
  6.4 8.6 %copy-start.6 = (bf16[768,256]{1,0:T(8,128)(2,1)S(1)}, bf16[768,256]{1,0:T(8,128)(2,1)}, u32[]{:S(2)}) copy-start(bf16[768,256]{1,0:T(8,128)(2,1)} %constant.16.clone.refs_6_) | copy-start | bytes 1179652
  6.4 8.6 %copy-start.8 = (bf16[128,256]{1,0:T(8,128)(2,1)S(1)}, bf16[128,256]{1,0:T(8,128)(2,1)}, u32[]{:S(2)}) copy-start(bf16[128,256]{1,0:T(8,128)(2,1)} %constant.15.clone.forward_ref.refs_5_) | copy-start | bytes 196612
  6.4 8.6 %copy-start.9 = (f32[8,128]{1,0:T(8,128)S(1)}, f32[8,128]{1,0:T(8,128)}, u32[]{:S(2)}) copy-start(f32[8,128]{1,0:T(8,128)} %constant.18.clone.refs_8_) | copy-start | bytes 12292
  13.6 7.4 %copy-start.10 = (bf16[16,128,256]{2,1,0:T(8,128)(2,1)}, bf16[16,128,256]{2,1,0:T(8,128)(2,1)S(1)}, u32[]{:S(2)}) copy-start(bf16[16,128,256]{2,1,0:T(8,128)(2,1)S(1)} %own_spectrum.1.refs_2_) | copy-start | bytes 3145732
  13.7 17.3 %collective-permute-start.1 = (bf16[512,512]{1,0:T(8,128)(2,1)S(1)}, bf16[512,512]{1,0:T(8,128)(2,1)S(1)}, u32[]{:S(2)}, u32[]{:S(2)}) collective-permute-start(bf16[512,512]{1,0:T(8,128)(2,1)S(1)} %collective-permute-done.refs_1_), channel_id=1, source_target_pairs={{1,0},{2,1},{3,2},{4,3},{5,4},{6,5},{7,6},{8,7},{9,8},{10,9},{11,1... | collective-permute-start | bytes 1572872 | tf_op jit(solution)/shard_map/ppermute | solution.py:215
  21.7 17.2 %all-to-all-start = ((f32[16,3,32]{2,1,0:T(4,128)}), f32[16,3,32]{2,1,0:T(4,128)S(1)}, u32[]{:S(2)}, u32[]{:S(2)}) async-start(f32[16,3,32]{2,1,0:T(4,128)} %broadcast_in_dim.3), calls=%async_computation | async-start | bytes 65536 | tf_op jit(solution)/shard_map/all_to_all | solution.py:263
  31.0 1.2 %copy-start.11 = (bf16[16,128,256]{2,1,0:T(8,128)(2,1)S(1)}, bf16[16,128,256]{2,1,0:T(8,128)(2,1)}, u32[]{:S(2)}) copy-start(bf16[16,128,256]{2,1,0:T(8,128)(2,1)} %copy-done.10) | copy-start | bytes 3145732
  38.2 0.6 %copy-start = (f32[2,32]{1,0:T(2,128)}, f32[2,32]{1,0:T(2,128)S(1)}, u32[]{:S(2)}) copy-start(f32[2,32]{1,0:T(2,128)S(1)} %flow_skip.1.skip_ref) | copy-start | bytes 772
  38.9 0.6 %copy-start.12 = (f32[16,3,32]{2,1,0:T(4,128)}, f32[16,3,32]{2,1,0:T(4,128)S(1)}, u32[]{:S(2)}) copy-start(f32[16,3,32]{2,1,0:T(4,128)S(1)} %all-to-all-done.shared_ref) | copy-start | bytes 18436

commit v3 on v2

v3 whole, which is shorter than its diff:
```python
import functools

import jax
import jax.numpy as jnp
import numpy as np
from jax import lax
from jax.experimental import pallas as pl
from jax.experimental.pallas import tpu as pltpu
from jax.sharding import PartitionSpec as P

PATCH = 128
LEVELS = 3
HALF = PATCH // 2
PAIRS = 4
GROUP = 2 * PAIRS


def tables():
    index = np.arange(PATCH)
    angles = ((index[:, None] * index[None, :]) % PATCH).astype(np.float32) * np.float32(2.0 * np.pi / PATCH)
    cosine = np.cos(angles).astype(jnp.bfloat16).astype(np.float32)
    sine = (-np.sin(angles)).astype(jnp.bfloat16).astype(np.float32)
    signed = np.minimum(index, PATCH - index)
    bands = [(signed < PATCH // 2 ** (level + 1)).astype(np.float32) for level in range(LEVELS)]
    offset = np.where(index < HALF, index, index - PATCH).astype(np.float64)

    zero = np.zeros((PATCH, HALF), np.float32)
    cos_half, sin_half = cosine[:, :HALF], sine[:, :HALF]
    window = np.stack(
        [
            np.tile(np.concatenate(part, axis=1), (2, 1))
            for part in ([cos_half, zero], [sin_half, zero], [zero, cos_half], [zero, sin_half])
        ]
    )
    forward = np.concatenate([cosine, sine], axis=1) / PATCH

    def inverse_rows(level, kept, points):
        left = (cosine * bands[level])[points][:, kept], (sine * bands[level])[points][:, kept]
        return np.block([[left[0], left[1]], [-left[1], left[0]]])

    def inverse_cols(level, width, lanes, members, points):
        twice = np.where(np.arange(width) == 0, 1.0, 2.0)[:, None] * bands[level][:width, None] / PATCH
        table = np.zeros((2 * PATCH, 2 * PATCH), np.float32)
        for turn, patch in enumerate(members):
            group = lanes.index(patch) * width
            cols = slice(turn * len(points), (turn + 1) * len(points))
            table[group : group + width, cols] = cosine[:width][:, points] * twice
            table[PATCH + group : PATCH + group + width, cols] = sine[:width][:, points] * twice
        return table

    quarter, eighth = PATCH // 4, PATCH // 8
    kept = [index, np.r_[:quarter, PATCH - quarter : PATCH], np.r_[:eighth, PATCH - eighth : PATCH]]
    coarse = index[::2]
    rows = [
        inverse_rows(0, kept[0], index),
        inverse_rows(1, kept[1], index),
        inverse_rows(2, kept[2], coarse),
    ]
    by_eighth = [0, 4, 2, 6, 1, 5, 3, 7]
    cols = np.stack(
        [
            inverse_cols(0, HALF, [0, 1], [0, 1], index),
            inverse_cols(1, quarter, [0, 2, 1, 3], [0, 1], index),
            inverse_cols(1, quarter, [0, 2, 1, 3], [2, 3], index),
            inverse_cols(2, eighth, by_eighth, [0, 1, 2, 3], coarse),
            inverse_cols(2, eighth, by_eighth, [4, 5, 6, 7], coarse),
        ]
    )

    spectrum = np.fft.fft(offset)
    spectrum[np.minimum(index, PATCH - index) >= quarter] = 0.0
    smooth = 2.0 * np.real(np.fft.ifft(spectrum))[::2]
    moments = np.zeros((2, 8, PATCH), np.float32)
    moments[0, 0], moments[0, 1], moments[0, 2] = 1.0, offset, 1.0
    moments[1, 0], moments[1, 1], moments[1, 2] = 4.0, 2.0 * np.tile(smooth, 2), 2.0
    slopes = np.broadcast_to(smooth[:, None], (HALF, PATCH)).astype(np.float32)
    return (
        jnp.asarray(window),
        jnp.asarray(forward, jnp.bfloat16),
        *(jnp.asarray(table, jnp.bfloat16) for table in rows),
        jnp.asarray(cols, jnp.bfloat16),
        jnp.asarray(moments),
        jnp.asarray(slopes),
    )


def product(left, right):
    return jnp.dot(left, right, preferred_element_type=jnp.float32)


def fill_panels(tile_ref, panels):
    for panel in range(panels.shape[0]):
        panels[panel] = tile_ref[:, panel * PATCH : (panel + 1) * PATCH].astype(jnp.float32)


def pair_spectrum(pair, place_ref, panels, window_ref, forward):
    last = panels.shape[0] - 1
    lane = lax.broadcasted_iota(jnp.int32, (PATCH, PATCH), 1)
    turned, table = [], []
    for member in range(2):
        row = place_ref[0, 2 * pair + member]
        col = place_ref[1, 2 * pair + member]
        panel = lax.shift_right_logical(col, PATCH.bit_length() - 1)
        shift = col & (PATCH - 1)
        here = panels[panel, pl.ds(row, PATCH), :]
        beside = panels[jnp.minimum(panel + 1, last), pl.ds(row, PATCH), :]
        turned.append(jnp.where(lane >= shift, here, beside).astype(jnp.bfloat16))
        start = PATCH - shift
        table.append(
            jnp.concatenate(
                [
                    window_ref[2 * member, pl.ds(start, PATCH), :],
                    window_ref[2 * member + 1, pl.ds(start, PATCH), :],
                ],
                axis=1,
            ).astype(jnp.bfloat16)
        )
    cols = product(jnp.concatenate(turned, axis=1), jnp.concatenate(table, axis=0)).astype(jnp.bfloat16)
    crossed = jnp.concatenate([-cols[:, PATCH:], cols[:, :PATCH]], axis=1)
    return product(forward, jnp.concatenate([cols, crossed], axis=0)).astype(jnp.bfloat16)


def own_kernel(place_ref, tile_ref, window_ref, forward_ref, spec_ref, started_ref, panels):
    started_ref[...] = jnp.zeros_like(started_ref)
    fill_panels(tile_ref, panels)
    forward = forward_ref[...]
    for pair in range(spec_ref.shape[0]):
        spec_ref[pair] = pair_spectrum(pair, place_ref, panels, window_ref, forward)


def estimate(
    place_ref, tile_ref, spec_ref, usage_ref, window_ref, forward_ref, rows0_ref, rows1_ref, rows2_ref, cols_ref,
    moments_ref, slopes_ref, panels, cross0, cross1, cross2, half0, half1, half2, plain, nested,
):
    fill_panels(tile_ref, panels)
    groups = place_ref.shape[1] // GROUP
    quarter, eighth = PATCH // 4, PATCH // 8

    def packed(even, odd, width):
        lane = lax.broadcasted_iota(jnp.int32, even.shape, 1)
        return jnp.where((lane & (2 * width - 1)) < width, even, pltpu.roll(odd, width, 1))

    def cross_stage(group, slot):
        forward = forward_ref[...]
        inner = []
        for pair in range(PAIRS):
            place = group * PAIRS + pair
            other = pair_spectrum(place, place_ref, panels, window_ref, forward).astype(jnp.float32)
            own = spec_ref[place].astype(jnp.float32)
            own_real, own_imag = own[:, :PATCH], own[:, PATCH:]
            other_real, other_imag = other[:, :PATCH], other[:, PATCH:]
            real = own_real * other_real + own_imag * other_imag
            imag = own_imag * other_real - own_real * other_imag
            lanes = slice(pair % 2 * PATCH, (pair % 2 + 1) * PATCH)
            cross0[slot, pair // 2, :PATCH, lanes] = real.astype(jnp.bfloat16)
            cross0[slot, pair // 2, PATCH:, lanes] = imag.astype(jnp.bfloat16)
            inner.append(
                jnp.concatenate([real[:quarter], real[-quarter:], imag[:quarter], imag[-quarter:]], axis=0)
            )
        middle = [packed(inner[2 * turn], inner[2 * turn + 1], quarter) for turn in range(PAIRS // 2)]
        for turn in range(PAIRS // 2):
            cross1[slot, :, turn * PATCH : (turn + 1) * PATCH] = middle[turn].astype(jnp.bfloat16)
        inner = [
            jnp.concatenate(
                [part[:eighth], part[HALF - eighth : HALF], part[HALF : HALF + eighth], part[-eighth:]], axis=0
            )
            for part in middle
        ]
        cross2[slot] = packed(inner[0], inner[1], eighth).astype(jnp.bfloat16)

    def half_stage(slot):
        for turn in range(PAIRS // 2):
            half0[slot, turn] = product(rows0_ref[...], cross0[slot, turn]).astype(jnp.bfloat16)
        half1[slot] = product(rows1_ref[...], cross1[slot]).astype(jnp.bfloat16)
        half2[slot] = product(rows2_ref[...], cross2[slot]).astype(jnp.bfloat16)

    def lines(half, tile):
        lanes = slice(tile * PATCH, (tile + 1) * PATCH)
        middle = half.shape[0] // 2
        return jnp.concatenate([half[:middle, lanes], half[middle:, lanes]], axis=1)

    def keep_ladder(level, group, members, correl):
        running, ladder = None, None
        for turn in range(PATCH // 8):
            row = (turn * 8 + HALF) % PATCH
            block = correl[row : row + 8]
            weight = block * block
            running = weight if running is None else running + weight
            ladder = running if ladder is None else ladder + running
        for turn, member in enumerate(members):
            lanes = slice(turn * PATCH, (turn + 1) * PATCH)
            plain[level, group * GROUP + member] = running[:, lanes]
            nested[level, group * GROUP + member] = ladder[:, lanes]

    def sums_stage(group, slot):
        correl = product(
            jnp.concatenate([lines(half0.at[slot, pair // 2], pair % 2) for pair in range(PAIRS)], axis=0), cols_ref[0]
        )
        for pair in range(PAIRS):
            keep_ladder(0, group, (2 * pair, 2 * pair + 1), correl[pair * PATCH : (pair + 1) * PATCH])
        line = jnp.concatenate([lines(half1.at[slot], turn) for turn in range(PAIRS // 2)], axis=0)
        for part in range(2):
            correl = product(line, cols_ref[1 + part])
            for turn in range(PAIRS // 2):
                pair = 2 * turn + part
                keep_ladder(1, group, (2 * pair, 2 * pair + 1), correl[turn * PATCH : (turn + 1) * PATCH])
        line = lines(half2.at[slot], 0)
        for part in range(2):
            correl = product(line, cols_ref[3 + part])
            for turn in range(2):
                total, slope = None, None
                for row in range(0, HALF, 8):
                    block = correl[row : row + 8, turn * PATCH : (turn + 1) * PATCH]
                    weight = block * block
                    sloped = weight * slopes_ref[row : row + 8]
                    total = weight if total is None else total + weight
                    slope = sloped if slope is None else slope + sloped
                for member in range(2):
                    place = group * GROUP + 4 * part + 2 * turn + member
                    plain[2, place] = total
                    nested[2, place] = slope

    for turn in range(groups + 2):
        if turn >= 2:
            sums_stage(turn - 2, turn % 2)
        if 1 <= turn <= groups:
            half_stage((turn - 1) % 2)
        if turn < groups:
            cross_stage(turn, turn % 2)

    usage = usage_ref[...].astype(jnp.float32)
    across = (((1,), (1,)), ((), ()))
    shape = plain.shape[1], PATCH
    own_lanes = (lax.broadcasted_iota(jnp.int32, shape, 1) >= HALF) == (
        (lax.broadcasted_iota(jnp.int32, shape, 0) & 1) == 1
    )
    along_rows, along_cols = 0.0, 0.0
    for level in range(LEVELS):
        by_col, by_row = 0.0, 0.0
        for sublane in range(8):
            part = plain[level, :, sublane, :]
            by_col = by_col + part
            if level < 2:
                by_row = by_row + ((HALF + sublane) * part - 8.0 * nested[level, :, sublane, :])
            else:
                by_row = by_row + nested[level, :, sublane, :]
        if level == 2:
            by_col = jnp.where(own_lanes, by_col, 0.0)
            by_row = jnp.where(own_lanes, by_row, 0.0)
        col_part, row_part = (
            lax.dot_general(
                moments_ref[level // 2], part, across, precision=lax.Precision.HIGHEST,
                preferred_element_type=jnp.float32,
            )
            for part in (by_col, by_row)
        )
        scale = usage[level : level + 1] / (col_part[0:1] + 1e-6)
        along_rows = along_rows + row_part[2:3] * scale
        along_cols = along_cols + col_part[1:2] * scale
    count = jnp.maximum(jnp.sum(usage, axis=0, keepdims=True), 1.0)
    return jnp.concatenate([along_rows, along_cols], axis=0) / count


INS = 12


def next_kernel(*refs):
    ins, mask_ref, out_ref, scratch = refs[:INS], refs[INS], refs[INS + 1], refs[INS + 2 :]
    message = jnp.concatenate([estimate(*ins, *scratch), mask_ref[...].astype(jnp.float32)], axis=0)
    for section in range(out_ref.shape[0]):
        out_ref[section] = message


def skip_kernel(*refs):
    ins, out_ref, scratch = refs[:INS], refs[INS], refs[INS + 1 :]
    out_ref[...] = estimate(*ins, *scratch)


def combine_kernel(shared_ref, skip_ref, *outs):
    me = lax.axis_index("sec")
    sections = shared_ref.shape[0]

    def mask_of(section):
        held = shared_ref[jnp.minimum(section, sections - 1), 2:3, :]
        return jnp.where(section < sections, held, jnp.zeros_like(held))

    def flow_of(section):
        return shared_ref[section, 0:2, :] * (mask_of(section) * mask_of(section + 1))

    flow_next = flow_of(me)
    outs[0][0] = flow_next
    outs[1][0] = skip_ref[...] * (mask_of(me) * mask_of(me + 2))
    outs[2][0] = lax.fori_loop(
        0, me, lambda section, held: held + flow_of(section), jnp.zeros_like(flow_next)
    ) + flow_next


def passed_along(block, axis, distance):
    devices = range(lax.axis_size(axis))
    route = [(i - distance, i) for i in devices if i - distance in devices]
    return lax.ppermute(block, axis, route)


def on_device(section_tile, placement, tissue_mask, level_use):
    window, forward, *rest = tables()
    patches = placement.shape[0]
    side = section_tile.shape[1]
    tile = section_tile[0]
    sections = lax.axis_size("sec")
    vmem = pl.BlockSpec(memory_space=pltpu.VMEM)
    smem = pl.BlockSpec(memory_space=pltpu.SMEM)
    panels = pltpu.VMEM((side // PATCH, side, PATCH), jnp.float32)
    sums = pltpu.VMEM((LEVELS, patches, 8, PATCH), jnp.float32)
    corners = placement.T

    def limit(mebibytes):
        return pltpu.CompilerParams(vmem_limit_bytes=mebibytes * 2**20)

    next_tile = passed_along(tile, "sec", -1)
    own_spec, started = pl.pallas_call(
        own_kernel,
        out_shape=(
            jax.ShapeDtypeStruct((patches // 2, PATCH, 2 * PATCH), jnp.bfloat16),
            jax.ShapeDtypeStruct((8, PATCH), jnp.float32),
        ),
        in_specs=[smem, vmem, vmem, vmem],
        out_specs=(vmem, vmem),
        scratch_shapes=[panels],
        compiler_params=limit(8),
        cost_estimate=pl.CostEstimate(flops=4 * 10**9, bytes_accessed=3 * 2**20, transcendentals=0),
        name="own_spectrum",
    )(corners, tile, window, forward)
    later_tile, own_spec, _ = lax.optimization_barrier((tile, own_spec, started))
    skip_tile = passed_along(later_tile, "sec", -2)

    def flow(kernel, out_shape, other_tile, name, *more):
        return pl.pallas_call(
            kernel,
            out_shape=jax.ShapeDtypeStruct(out_shape, jnp.float32),
            in_specs=[smem] + [vmem] * (INS - 1 + len(more)),
            out_specs=vmem,
            scratch_shapes=[
                panels,
                pltpu.VMEM((2, PAIRS // 2, 2 * PATCH, 2 * PATCH), jnp.bfloat16),
                pltpu.VMEM((2, PATCH, 2 * PATCH), jnp.bfloat16),
                pltpu.VMEM((2, HALF, PATCH), jnp.bfloat16),
                pltpu.VMEM((2, PAIRS // 2, 2 * PATCH, 2 * PATCH), jnp.bfloat16),
                pltpu.VMEM((2, 2 * PATCH, 2 * PATCH), jnp.bfloat16),
                pltpu.VMEM((2, PATCH, PATCH), jnp.bfloat16),
                sums,
                sums,
            ],
            compiler_params=limit(12),
            cost_estimate=pl.CostEstimate(flops=8 * 10**9, bytes_accessed=4 * 2**20, transcendentals=0),
            name=name,
        )(corners, other_tile, own_spec, level_use, window, forward, *rest, *more)

    message = flow(next_kernel, (sections, 3, patches), next_tile, "flow_next", tissue_mask)
    shared = lax.all_to_all(message, "sec", 0, 0)
    flow_skip = flow(skip_kernel, (2, patches), skip_tile, "flow_skip")
    out = jax.ShapeDtypeStruct((1, 2, patches), jnp.float32)
    return pl.pallas_call(
        combine_kernel,
        out_shape=(out, out, out),
        in_specs=[vmem, vmem],
        out_specs=(vmem, vmem, vmem),
        compiler_params=limit(2),
        name="combine",
    )(shared, flow_skip)


def solution(mesh):
    in_specs = (
        P(("grp", "sec"), None, None),
        P("grp", None),
        P(("grp", "sec"), None),
        P(None, "grp"),
    )
    out_specs = (
        P(("grp", "sec"), None, None),
        P(("grp", "sec"), None, None),
        P(("grp", "sec"), None, None),
    )
    return jax.shard_map(
        on_device, mesh=mesh, in_specs=in_specs, out_specs=out_specs, check_vma=False
    )
```

time: 41.3 us -> 30.6 us (0.74)
  Pallas kernels: 20.6 us -> 12.3 us
  local copies, waits for them, and re-layouts: 7.52 us -> 1.93 us
  waiting for transfers between devices: 0.01 us -> 2.46 us
  starting transfers between devices: 11.9 us -> 12.7 us
    pallas_call x4, Pallas kernels: 20.6 us -> 12.3 us  [the longest x2 8.98 us: flow(): pl.pallas_call(kernel, out_shape=jax.ShapeDtypeStruct(out_shape, jnp.floa...]
    unnamed x31 -> x26, local copies, waits for them, and re-layouts: 6.9 us -> 1.93 us
    ppermute x2, waiting for transfers between devices: 0.01 us -> 2.08 us  [passed_along(): return lax.ppermute(block, axis, route)]
    all_to_all x1, starting transfers between devices: 9.27 us -> 10 us  [on_device(): shared = lax.all_to_all(message, 'sec', 0, 0)]
    broadcast_in_dim x1 -> x0, local copies, waits for them, and re-layouts: 0.62 us -> none  [on_device(): jnp.broadcast_to(message, (sections,) + message.shape)]
  transfers between devices with their start and end apart: 3 -> 3, of which waited for: 0 -> 2; matrix products, arithmetic and copies ran while one was open for 2% -> 0% of each run, Pallas kernels for 47% -> 39%
where the time goes in v3:
time: 30.6 us; the launch traced here: 30.3 us
  starting transfers between devices  12.7 us (42%)
  Pallas kernels  12.3 us (40%)
  waiting for transfers between devices  2.46 us (8%)
  local copies, waits for them, and re-layouts  1.93 us (6%)
  between operations  0.81 us (3%)
    all_to_all x1, starting transfers between devices, on_device(): shared = lax.all_to_all(message, 'sec', 0, 0)  10 us
    pallas_call x2, Pallas kernels, flow(): pl.pallas_call(kernel, out_shape=jax.ShapeDtypeStruct(out_shape, jnp.floa...  8.98 us
    pallas_call x1, Pallas kernels, on_device(): pl.pallas_call(own_kernel, out_shape=(jax.ShapeDtypeStruct((patches // 2,...  2.76 us
    ppermute x2, starting transfers between devices, passed_along(): return lax.ppermute(block, axis, route)  2.7 us
    ppermute x2, waiting for transfers between devices, passed_along(): return lax.ppermute(block, axis, route)  2.08 us
    unnamed x26, local copies, waits for them, and re-layouts  1.93 us
  transfers between devices with their start and end apart: 3, of which 2 were waited for; matrix products, arithmetic and copies ran while one was open for 0% of the time, Pallas kernels for 39%

profile of v3, /device:TPU:0, one launch (start us, length us, event | category | flops | bytes accessed | tf_op | source)
XLA Modules:
  0.0 30.3 jit_solution(11747335515700788972)
XLA Ops:
  0.6 0.0 copy-start.1
  0.6 1.3 %collective-permute-start = (bf16[512,512]{1,0:T(8,128)(2,1)}, bf16[512,512]{1,0:T(8,128)(2,1)S(1)}, u32[]{:S(2)}, u32[]{:S(2)}) collective-permute-start(bf16[512,512]{1,0:T(8,128)(2,1)} %bitcast.1.tile_ref), channel_id=1, source_target_pairs={{1,0},{2,1},{3,2},{4,3},{5,4},{6,5},{7,6},{8,7},{9,8},{10,9},{11,1... | collective-permute-start | bytes 1572872 | tf_op jit(solution)/shard_map/ppermute | solution.py:301
  1.9 0.0 copy-done.1
  1.9 0.0 copy-start.4
  2.0 1.0 %copy-done.4 = f32[4,256,128]{2,1,0:T(8,128)S(1)} copy-done((f32[4,256,128]{2,1,0:T(8,128)S(1)}, f32[4,256,128]{2,1,0:T(8,128)}, u32[]{:S(2)}) %copy-start.4) | copy-done | bytes 524312
  3.0 0.0 copy-start.7
  3.0 0.8 %copy-done.7 = bf16[128,256]{1,0:T(8,128)(2,1)S(1)} copy-done((bf16[128,256]{1,0:T(8,128)(2,1)S(1)}, bf16[128,256]{1,0:T(8,128)(2,1)}, u32[]{:S(2)}) %copy-start.7) | copy-done | bytes 65560
  3.8 0.0 copy-start
  3.8 0.0 copy-start.3
  3.8 0.0 copy-start.5
  3.8 0.0 copy-start.6
  3.8 0.0 copy-start.8
  3.9 0.0 copy-start.9
  3.9 0.0 copy-start.10
  3.9 0.0 copy-start.11
  3.9 0.0 copy-start.12
  3.9 2.8 %own_spectrum.1 = (bf16[16,128,256]{2,1,0:T(8,128)(2,1)S(1)}, f32[8,128]{1,0:T(8,128)}) custom-call(s32[2,32]{1,0:T(2,128)S(1)} %bitcast.2, bf16[512,512]{1,0:T(8,128)(2,1)} %bitcast.1.tile_ref, f32[4,256,128]{2,1,0:T(8,128)S(1)} %copy-done.4, bf16[128,256]{1,0:T(8,128)(2,1)S(1)} %copy-done.7), custom_call_target="tpu_custom_call" | custom-call | flops 4000000000 | bytes 3145728 | tf_op jit(solution)/shard_map/own_spectrum/pallas_call | solution.py:320
  6.7 0.0 copy-start.2
  6.7 1.4 %collective-permute-start.1 = (bf16[512,512]{1,0:T(8,128)(2,1)}, bf16[512,512]{1,0:T(8,128)(2,1)S(1)}, u32[]{:S(2)}, u32[]{:S(2)}) collective-permute-start(bf16[512,512]{1,0:T(8,128)(2,1)} %bitcast.1.tile_ref), channel_id=1, source_target_pairs={{2,0},{3,1},{4,2},{5,3},{6,4},{7,5},{8,6},{9,7},{10,8},{11,9},{12,... | collective-permute-start | bytes 1572872 | tf_op jit(solution)/shard_map/ppermute | solution.py:301
  8.1 0.0 collective-permute-done.refs_1_
  8.1 0.0 copy-done
  8.1 0.0 copy-done.3
  8.1 0.0 copy-done.5
  8.1 0.0 copy-done.6
  8.1 0.0 copy-done.8
  8.2 0.0 copy-done.9
  8.2 0.0 copy-done.10
  8.2 0.0 copy-done.11
  8.2 0.0 copy-done.12
  8.2 0.0 copy-done.2
  8.2 4.8 %flow_next.1 = f32[16,3,32]{2,1,0:T(4,128)} custom-call(s32[2,32]{1,0:T(2,128)S(1)} %bitcast.3, bf16[512,512]{1,0:T(8,128)(2,1)S(1)} %collective-permute-done.refs_1_, bf16[16,128,256]{2,1,0:T(8,128)(2,1)S(1)} %get-tuple-element.7.refs_2_, s32[3,32]{1,0:T(4,128)S(1)} %copy-done, f32[4,256,128]{2,1,0:T(8,128)S(1)} %copy-done.5, ...), custom_call_target="tpu_custom_call" | custom-call | flops 8000000000 | bytes 4194304 | tf_op jit(solution)/shard_map/flow_next/pallas_call | solution.py:337
  13.0 10.0 %all-to-all-start = ((f32[16,3,32]{2,1,0:T(4,128)}), f32[16,3,32]{2,1,0:T(4,128)S(1)}, u32[]{:S(2)}, u32[]{:S(2)}) async-start(f32[16,3,32]{2,1,0:T(4,128)} %flow_next.1), calls=%async_computation | async-start | bytes 65536 | tf_op jit(solution)/shard_map/all_to_all | solution.py:359
  23.0 2.1 %collective-permute-done.1.refs_1_ = bf16[512,512]{1,0:T(8,128)(2,1)S(1)} collective-permute-done((bf16[512,512]{1,0:T(8,128)(2,1)}, bf16[512,512]{1,0:T(8,128)(2,1)S(1)}, u32[]{:S(2)}, u32[]{:S(2)}) %collective-permute-start.1) | collective-permute-done | bytes 524320 | tf_op jit(solution)/shard_map/ppermute | solution.py:301
  25.1 4.2 %flow_skip.1.skip_ref = f32[2,32]{1,0:T(2,128)S(1)} custom-call(s32[2,32]{1,0:T(2,128)S(1)} %bitcast.4, bf16[512,512]{1,0:T(8,128)(2,1)S(1)} %collective-permute-done.1.refs_1_, bf16[16,128,256]{2,1,0:T(8,128)(2,1)S(1)} %get-tuple-element.7.refs_2_, s32[3,32]{1,0:T(4,128)S(1)} %copy-done, f32[4,256,128]{2,1,0:T(8,128)S(1)} %copy-done.5, ...), custom_call_target="tpu_custom_call" | custom-call | flops 8000000000 | bytes 4194304 | tf_op jit(solution)/shard_map/flow_skip/pallas_call | solution.py:337
  29.3 0.4 %all-to-all-done.shared_ref = f32[16,3,32]{2,1,0:T(4,128)S(1)} async-done(((f32[16,3,32]{2,1,0:T(4,128)}), f32[16,3,32]{2,1,0:T(4,128)S(1)}, u32[]{:S(2)}, u32[]{:S(2)}) %all-to-all-start) | async-done | bytes 6176 | tf_op jit(solution)/shard_map/all_to_all | solution.py:359
  29.7 0.6 %combine.1 = (f32[1,2,32]{2,1,0:T(2,128)}, f32[1,2,32]{2,1,0:T(2,128)}, f32[1,2,32]{2,1,0:T(2,128)}) custom-call(f32[16,3,32]{2,1,0:T(4,128)S(1)} %all-to-all-done.shared_ref, f32[2,32]{1,0:T(2,128)S(1)} %flow_skip.1.skip_ref), custom_call_target="tpu_custom_call" | custom-call | tf_op jit(solution)/shard_map/combine/pallas_call | solution.py:362
Async XLA Ops:
  0.6 1.3 %copy-start.1 = (s32[32,2]{0,1:T(2,128)S(1)}, s32[32,2]{0,1:T(2,128)}, u32[]{:S(2)}) copy-start(s32[32,2]{0,1:T(2,128)} %param.13) | copy-start | bytes 772
  0.6 7.5 %collective-permute-start = (bf16[512,512]{1,0:T(8,128)(2,1)}, bf16[512,512]{1,0:T(8,128)(2,1)S(1)}, u32[]{:S(2)}, u32[]{:S(2)}) collective-permute-start(bf16[512,512]{1,0:T(8,128)(2,1)} %bitcast.1.tile_ref), channel_id=1, source_target_pairs={{1,0},{2,1},{3,2},{4,3},{5,4},{6,5},{7,6},{8,7},{9,8},{10,9},{11,1... | collective-permute-start | bytes 1572872 | tf_op jit(solution)/shard_map/ppermute | solution.py:301
  1.9 1.0 %copy-start.4 = (f32[4,256,128]{2,1,0:T(8,128)S(1)}, f32[4,256,128]{2,1,0:T(8,128)}, u32[]{:S(2)}) copy-start(f32[4,256,128]{2,1,0:T(8,128)} %constant.16.clone.window_ref.refs_4_) | copy-start | bytes 1572868
  3.0 0.8 %copy-start.7 = (bf16[128,256]{1,0:T(8,128)(2,1)S(1)}, bf16[128,256]{1,0:T(8,128)(2,1)}, u32[]{:S(2)}) copy-start(bf16[128,256]{1,0:T(8,128)(2,1)} %constant.17.clone.forward_ref.refs_5_) | copy-start | bytes 196612
  3.8 4.3 %copy-start = (s32[3,32]{1,0:T(4,128)S(1)}, s32[3,32]{1,0:T(4,128)}, u32[]{:S(2)}) copy-start(s32[3,32]{1,0:T(4,128)} %refs_3_.3) | copy-start | bytes 1156
  3.8 4.3 %copy-start.3 = (bf16[5,256,256]{2,1,0:T(8,128)(2,1)S(1)}, bf16[5,256,256]{2,1,0:T(8,128)(2,1)}, u32[]{:S(2)}) copy-start(bf16[5,256,256]{2,1,0:T(8,128)(2,1)} %constant.21.clone.refs_9_) | copy-start | bytes 1966084
  3.8 4.3 %copy-start.5 = (f32[4,256,128]{2,1,0:T(8,128)S(1)}, f32[4,256,128]{2,1,0:T(8,128)}, u32[]{:S(2)}) copy-start(f32[4,256,128]{2,1,0:T(8,128)} %constant.16.clone.window_ref.refs_4_) | copy-start | bytes 1572868
  3.8 4.3 %copy-start.6 = (bf16[256,256]{1,0:T(8,128)(2,1)S(1)}, bf16[256,256]{1,0:T(8,128)(2,1)}, u32[]{:S(2)}) copy-start(bf16[256,256]{1,0:T(8,128)(2,1)} %constant.18.clone.refs_6_) | copy-start | bytes 393220
  3.8 4.3 %copy-start.8 = (bf16[128,256]{1,0:T(8,128)(2,1)S(1)}, bf16[128,256]{1,0:T(8,128)(2,1)}, u32[]{:S(2)}) copy-start(bf16[128,256]{1,0:T(8,128)(2,1)} %constant.17.clone.forward_ref.refs_5_) | copy-start | bytes 196612
  3.9 4.3 %copy-start.9 = (bf16[256,128]{1,0:T(8,128)(2,1)S(1)}, bf16[256,128]{1,0:T(8,128)(2,1)}, u32[]{:S(2)}) copy-start(bf16[256,128]{1,0:T(8,128)(2,1)} %constant.19.clone.refs_7_) | copy-start | bytes 196612
  3.9 4.3 %copy-start.10 = (bf16[128,64]{1,0:T(8,128)(2,1)S(1)}, bf16[128,64]{1,0:T(8,128)(2,1)}, u32[]{:S(2)}) copy-start(bf16[128,64]{1,0:T(8,128)(2,1)} %constant.20.clone.refs_8_) | copy-start | bytes 49156
  3.9 4.3 %copy-start.11 = (f32[64,128]{1,0:T(8,128)S(1)}, f32[64,128]{1,0:T(8,128)}, u32[]{:S(2)}) copy-start(f32[64,128]{1,0:T(8,128)} %constant.23.clone.refs_11_) | copy-start | bytes 98308
  3.9 4.3 %copy-start.12 = (f32[2,8,128]{2,1,0:T(8,128)S(1)}, f32[2,8,128]{2,1,0:T(8,128)}, u32[]{:S(2)}) copy-start(f32[2,8,128]{2,1,0:T(8,128)} %constant.22.clone.refs_10_) | copy-start | bytes 24580
  6.7 1.5 %copy-start.2 = (s32[1,32]{1,0:T(1,128)S(1)}, s32[1,32]{1,0:T(1,128)}, u32[]{:S(2)}) copy-start(s32[1,32]{1,0:T(1,128)} %refs_12_.1) | copy-start | bytes 388
  6.7 18.4 %collective-permute-start.1 = (bf16[512,512]{1,0:T(8,128)(2,1)}, bf16[512,512]{1,0:T(8,128)(2,1)S(1)}, u32[]{:S(2)}, u32[]{:S(2)}) collective-permute-start(bf16[512,512]{1,0:T(8,128)(2,1)} %bitcast.1.tile_ref), channel_id=1, source_target_pairs={{2,0},{3,1},{4,2},{5,3},{6,4},{7,5},{8,6},{9,7},{10,8},{11,9},{12,... | collective-permute-start | bytes 1572872 | tf_op jit(solution)/shard_map/ppermute | solution.py:301
  13.0 16.7 %all-to-all-start = ((f32[16,3,32]{2,1,0:T(4,128)}), f32[16,3,32]{2,1,0:T(4,128)S(1)}, u32[]{:S(2)}, u32[]{:S(2)}) async-start(f32[16,3,32]{2,1,0:T(4,128)} %flow_next.1), calls=%async_computation | async-start | bytes 65536 | tf_op jit(solution)/shard_map/all_to_all | solution.py:359

commit v4 on v3

--- a/solution.py
+++ b/solution.py
@@ -7,6 +7,7 @@
 from jax.experimental import pallas as pl
 from jax.experimental.pallas import tpu as pltpu
 from jax.sharding import PartitionSpec as P
+
 
 PATCH = 128
 LEVELS = 3
@@ -24,15 +25,14 @@
     bands = [(signed < PATCH // 2 ** (level + 1)).astype(np.float32) for level in range(LEVELS)]
     offset = np.where(index < HALF, index, index - PATCH).astype(np.float64)
 
-    zero = np.zeros((PATCH, HALF), np.float32)
     cos_half, sin_half = cosine[:, :HALF], sine[:, :HALF]
-    window = np.stack(
+    forward = np.concatenate(
         [
             np.tile(np.concatenate(part, axis=1), (2, 1))
-            for part in ([cos_half, zero], [sin_half, zero], [zero, cos_half], [zero, sin_half])
+            for part in ([cos_half, sin_half], [sin_half, cos_half])
         ]
-    )
-    forward = np.concatenate([cosine, sine], axis=1) / PATCH
+        + [cosine / PATCH, sine / PATCH]
+    )
 
     def inverse_rows(level, kept, points):
         left = (cosine * bands[level])[points][:, kept], (sine * bands[level])[points][:, kept]
@@ -75,8 +75,7 @@
     moments[1, 0], moments[1, 1], moments[1, 2] = 4.0, 2.0 * np.tile(smooth, 2), 2.0
     slopes = np.broadcast_to(smooth[:, None], (HALF, PATCH)).astype(np.float32)
     return (
-        jnp.asarray(window),
-        jnp.asarray(forward, jnp.bfloat16),
+        jnp.asarray(forward),
         *(jnp.asarray(table, jnp.bfloat16) for table in rows),
         jnp.asarray(cols, jnp.bfloat16),
         jnp.asarray(moments),
@@ -93,7 +92,13 @@
         panels[panel] = tile_ref[:, panel * PATCH : (panel + 1) * PATCH].astype(jnp.float32)
 
 
-def pair_spectrum(pair, place_ref, panels, window_ref, forward):
+def transform_of(forward_ref):
+    first = forward_ref.shape[0] - 2 * PATCH
+    parts = [forward_ref[first + turn * PATCH : first + (turn + 1) * PATCH] for turn in range(2)]
+    return jnp.concatenate(parts, axis=1).astype(jnp.bfloat16)
+
+
+def pair_spectrum(pair, place_ref, panels, forward_ref, forward):
     last = panels.shape[0] - 1
     lane = lax.broadcasted_iota(jnp.int32, (PATCH, PATCH), 1)
     turned, table = [], []
@@ -105,34 +110,53 @@
         here = panels[panel, pl.ds(row, PATCH), :]
         beside = panels[jnp.minimum(panel + 1, last), pl.ds(row, PATCH), :]
         turned.append(jnp.where(lane >= shift, here, beside).astype(jnp.bfloat16))
-        start = PATCH - shift
-        table.append(
-            jnp.concatenate(
-                [
-                    window_ref[2 * member, pl.ds(start, PATCH), :],
-                    window_ref[2 * member + 1, pl.ds(start, PATCH), :],
-                ],
-                axis=1,
-            ).astype(jnp.bfloat16)
-        )
+        mine = (lane >= HALF) == (member == 1)
+        parts = [
+            jnp.where(mine, forward_ref[pl.ds((2 * order + 1) * PATCH - shift, PATCH), :], 0.0)
+            for order in (member, 1 - member)
+        ]
+        table.append(jnp.concatenate(parts, axis=1).astype(jnp.bfloat16))
     cols = product(jnp.concatenate(turned, axis=1), jnp.concatenate(table, axis=0)).astype(jnp.bfloat16)
     crossed = jnp.concatenate([-cols[:, PATCH:], cols[:, :PATCH]], axis=1)
     return product(forward, jnp.concatenate([cols, crossed], axis=0)).astype(jnp.bfloat16)
 
 
-def own_kernel(place_ref, tile_ref, window_ref, forward_ref, spec_ref, started_ref, panels):
+def with_corners(corners_ref, place_ref, sem, work):
+    copy = pltpu.make_async_copy(corners_ref, place_ref, sem)
+    copy.start()
+    work()
+    copy.wait()
+
+
+def own_kernel(corners_ref, tile_ref, forward_ref, spec_ref, started_ref, held, panels, place_ref, sems):
+    fetch = pltpu.make_async_copy(tile_ref, held, sems.at[0])
+    fetch.start()
     started_ref[...] = jnp.zeros_like(started_ref)
-    fill_panels(tile_ref, panels)
-    forward = forward_ref[...]
+
+    def fill():
+        fetch.wait()
+        fill_panels(held, panels)
+
+    with_corners(corners_ref, place_ref, sems.at[1], fill)
+    forward = transform_of(forward_ref)
     for pair in range(spec_ref.shape[0]):
-        spec_ref[pair] = pair_spectrum(pair, place_ref, panels, window_ref, forward)
+        spec_ref[pair] = pair_spectrum(pair, place_ref, panels, forward_ref, forward)
 
 
 def estimate(
-    place_ref, tile_ref, spec_ref, usage_ref, window_ref, forward_ref, rows0_ref, rows1_ref, rows2_ref, cols_ref,
-    moments_ref, slopes_ref, panels, cross0, cross1, cross2, half0, half1, half2, plain, nested,
+    tile_refs, corners_ref, spec_ref, usage_ref, forward_ref, rows0_ref, rows1_ref, rows2_ref, cols_ref,
+     moments_ref, slopes_ref, panels, place_ref, sem, cross0, cross1, cross2, half0, half1, half2, plain,
+    nested,
 ):
-    fill_panels(tile_ref, panels)
+    def fill():
+        if len(tile_refs) == 1:
+            fill_panels(tile_refs[0], panels)
+        else:
+            odd = lax.axis_index("sec") & 1
+            for parity, tile_ref in enumerate(tile_refs):
+                pl.when(odd == parity)(functools.partial(fill_panels, tile_ref, panels))
+
+    with_corners(corners_ref, place_ref, sem, fill)
     groups = place_ref.shape[1] // GROUP
     quarter, eighth = PATCH // 4, PATCH // 8
 
@@ -141,11 +165,11 @@
         return jnp.where((lane & (2 * width - 1)) < width, even, pltpu.roll(odd, width, 1))
 
     def cross_stage(group, slot):
-        forward = forward_ref[...]
+        forward = transform_of(forward_ref)
         inner = []
         for pair in range(PAIRS):
             place = group * PAIRS + pair
-            other = pair_spectrum(place, place_ref, panels, window_ref, forward).astype(jnp.float32)
+            other = pair_spectrum(place, place_ref, panels, forward_ref, forward).astype(jnp.float32)
             own = spec_ref[place].astype(jnp.float32)
             own_real, own_imag = own[:, :PATCH], own[:, PATCH:]
             other_real, other_imag = other[:, :PATCH], other[:, PATCH:]
@@ -221,12 +245,12 @@
                     nested[2, place] = slope
 
     for turn in range(groups + 2):
+        if turn < groups:
+            cross_stage(turn, turn % 2)
+        if 1 <= turn <= groups:
+            half_stage((turn - 1) % 2)
         if turn >= 2:
             sums_stage(turn - 2, turn % 2)
-        if 1 <= turn <= groups:
-            half_stage((turn - 1) % 2)
-        if turn < groups:
-            cross_stage(turn, turn % 2)
 
     usage = usage_ref[...].astype(jnp.float32)
     across = (((1,), (1,)), ((), ()))
@@ -261,19 +285,19 @@
     return jnp.concatenate([along_rows, along_cols], axis=0) / count
 
 
-INS = 12
+INS = 10
 
 
 def next_kernel(*refs):
-    ins, mask_ref, out_ref, scratch = refs[:INS], refs[INS], refs[INS + 1], refs[INS + 2 :]
-    message = jnp.concatenate([estimate(*ins, *scratch), mask_ref[...].astype(jnp.float32)], axis=0)
+    ins, (tile_ref, mask_ref, out_ref), scratch = refs[:INS], refs[INS : INS + 3], refs[INS + 3 :]
+    message = jnp.concatenate([estimate([tile_ref], *ins, *scratch), mask_ref[...].astype(jnp.float32)], axis=0)
     for section in range(out_ref.shape[0]):
         out_ref[section] = message
 
 
 def skip_kernel(*refs):
-    ins, out_ref, scratch = refs[:INS], refs[INS], refs[INS + 1 :]
-    out_ref[...] = estimate(*ins, *scratch)
+    ins, tile_refs, out_ref, scratch = refs[:INS], refs[INS : INS + 2], refs[INS + 2], refs[INS + 3 :]
+    out_ref[...] = estimate(tile_refs, *ins, *scratch)
 
 
 def combine_kernel(shared_ref, skip_ref, *outs):
@@ -295,52 +319,57 @@
     ) + flow_next
 
 
-def passed_along(block, axis, distance):
+def moved(block, axis, distance, receivers=(0, 1)):
     devices = range(lax.axis_size(axis))
-    route = [(i - distance, i) for i in devices if i - distance in devices]
+    route = [(i + distance, i) for i in devices if i + distance in devices and i % 2 in receivers]
     return lax.ppermute(block, axis, route)
 
 
 def on_device(section_tile, placement, tissue_mask, level_use):
-    window, forward, *rest = tables()
+    forward, *rest = tables()
     patches = placement.shape[0]
     side = section_tile.shape[1]
     tile = section_tile[0]
     sections = lax.axis_size("sec")
     vmem = pl.BlockSpec(memory_space=pltpu.VMEM)
-    smem = pl.BlockSpec(memory_space=pltpu.SMEM)
-    panels = pltpu.VMEM((side // PATCH, side, PATCH), jnp.float32)
+    panels = (side // PATCH, side, PATCH)
+    corners = placement.T
+    corner_scratch = [pltpu.SMEM(corners.shape, corners.dtype), pltpu.SemaphoreType.DMA]
+    spec = jax.ShapeDtypeStruct((patches // 2, PATCH, 2 * PATCH), jnp.bfloat16)
     sums = pltpu.VMEM((LEVELS, patches, 8, PATCH), jnp.float32)
-    corners = placement.T
 
     def limit(mebibytes):
         return pltpu.CompilerParams(vmem_limit_bytes=mebibytes * 2**20)
 
-    next_tile = passed_along(tile, "sec", -1)
+    next_tile = moved(tile, "sec", 1)
+    even_tile = moved(tile, "sec", 2, (0,))
     own_spec, started = pl.pallas_call(
         own_kernel,
-        out_shape=(
-            jax.ShapeDtypeStruct((patches // 2, PATCH, 2 * PATCH), jnp.bfloat16),
-            jax.ShapeDtypeStruct((8, PATCH), jnp.float32),
-        ),
-        in_specs=[smem, vmem, vmem, vmem],
+        out_shape=(spec, jax.ShapeDtypeStruct((8, PATCH), jnp.float32)),
+        in_specs=[vmem, pl.BlockSpec(memory_space=pltpu.HBM), vmem],
         out_specs=(vmem, vmem),
-        scratch_shapes=[panels],
+        scratch_shapes=[
+            pltpu.VMEM(tile.shape, tile.dtype),
+            pltpu.VMEM(panels, jnp.float32),
+            corner_scratch[0],
+            pltpu.SemaphoreType.DMA((2,)),
+        ],
         compiler_params=limit(8),
         cost_estimate=pl.CostEstimate(flops=4 * 10**9, bytes_accessed=3 * 2**20, transcendentals=0),
         name="own_spectrum",
-    )(corners, tile, window, forward)
+    )(corners, tile, forward)
     later_tile, own_spec, _ = lax.optimization_barrier((tile, own_spec, started))
-    skip_tile = passed_along(later_tile, "sec", -2)
-
-    def flow(kernel, out_shape, other_tile, name, *more):
+    odd_tile = moved(later_tile, "sec", 2, (1,))
+
+    def flow(kernel, out_shape, *more):
         return pl.pallas_call(
             kernel,
             out_shape=jax.ShapeDtypeStruct(out_shape, jnp.float32),
-            in_specs=[smem] + [vmem] * (INS - 1 + len(more)),
+            in_specs=[vmem] * (INS + len(more)),
             out_specs=vmem,
             scratch_shapes=[
-                panels,
+                pltpu.VMEM(panels, jnp.float32),
+                *corner_scratch,
                 pltpu.VMEM((2, PAIRS // 2, 2 * PATCH, 2 * PATCH), jnp.bfloat16),
                 pltpu.VMEM((2, PATCH, 2 * PATCH), jnp.bfloat16),
                 pltpu.VMEM((2, HALF, PATCH), jnp.bfloat16),
@@ -352,12 +381,11 @@
             ],
             compiler_params=limit(12),
             cost_estimate=pl.CostEstimate(flops=8 * 10**9, bytes_accessed=4 * 2**20, transcendentals=0),
-            name=name,
-        )(corners, other_tile, own_spec, level_use, window, forward, *rest, *more)
-
-    message = flow(next_kernel, (sections, 3, patches), next_tile, "flow_next", tissue_mask)
+        )(corners, own_spec, level_use, forward, *rest, *more)
+
+    message = flow(next_kernel, (sections, 3, patches), next_tile, tissue_mask)
     shared = lax.all_to_all(message, "sec", 0, 0)
-    flow_skip = flow(skip_kernel, (2, patches), skip_tile, "flow_skip")
+    flow_skip = flow(skip_kernel, (2, patches), even_tile, odd_tile)
     out = jax.ShapeDtypeStruct((1, 2, patches), jnp.float32)
     return pl.pallas_call(
         combine_kernel,
@@ -381,6 +409,5 @@
         P(("grp", "sec"), None, None),
         P(("grp", "sec"), None, None),
     )
-    return jax.shard_map(
-        on_device, mesh=mesh, in_specs=in_specs, out_specs=out_specs, check_vma=False
-    )
+
+    return jax.shard_map(on_device, mesh=mesh, in_specs=in_specs, out_specs=out_specs, check_vma=False)

time: 30.6 us -> 30.1 us (0.984)
  Pallas kernels: 12.3 us -> 11.3 us
  starting transfers between devices: 12.7 us -> 13.7 us
  local copies, waits for them, and re-layouts: 1.93 us -> 1.04 us
  waiting for transfers between devices: 2.46 us -> 2.87 us
    all_to_all x1, waiting for transfers between devices: 0.38 us -> 1.79 us  [on_device(): shared = lax.all_to_all(message, 'sec', 0, 0)]
    ppermute x2 -> x3, waiting for transfers between devices: 2.08 us -> 1.08 us  [moved(): return lax.ppermute(block, axis, route)]
    unnamed x26 -> x22, local copies, waits for them, and re-layouts: 1.93 us -> 1.04 us
    pallas_call x2, Pallas kernels: 8.98 us -> 8.12 us  [flow(): pl.pallas_call(kernel, out_shape=jax.ShapeDtypeStruct(out_shape, jnp.floa...]
    ppermute x2 -> x3, starting transfers between devices: 2.7 us -> 3.28 us  [moved(): return lax.ppermute(block, axis, route)]
    all_to_all x1, starting transfers between devices: 10 us -> 10.5 us  [on_device(): shared = lax.all_to_all(message, 'sec', 0, 0)]
  transfers between devices with their start and end apart: 3 -> 4, of which waited for: 2 -> 2; matrix products, arithmetic and copies ran while one was open for 0% -> 0% of each run, Pallas kernels for 39% -> 36%
where the time goes in v4:
time: 30.1 us; the launch traced here: 29.8 us
  starting transfers between devices  13.7 us (46%)
  Pallas kernels  11.3 us (38%)
  waiting for transfers between devices  2.87 us (10%)
  local copies, waits for them, and re-layouts  1.04 us (3%)
  between operations  0.84 us (3%)
    all_to_all x1, starting transfers between devices, on_device(): shared = lax.all_to_all(message, 'sec', 0, 0)  10.5 us
    pallas_call x2, Pallas kernels, flow(): pl.pallas_call(kernel, out_shape=jax.ShapeDtypeStruct(out_shape, jnp.floa...  8.12 us
    ppermute x3, starting transfers between devices, moved(): return lax.ppermute(block, axis, route)  3.28 us
    pallas_call x1, Pallas kernels, on_device(): pl.pallas_call(own_kernel, out_shape=(spec, jax.ShapeDtypeStruct((8, PATC...  2.59 us
    all_to_all x1, waiting for transfers between devices, on_device(): shared = lax.all_to_all(message, 'sec', 0, 0)  1.79 us
    ppermute x3, waiting for transfers between devices, moved(): return lax.ppermute(block, axis, route)  1.08 us
    unnamed x22, local copies, waits for them, and re-layouts  1.04 us
  transfers between devices with their start and end apart: 4, of which 2 were waited for; matrix products, arithmetic and copies ran while one was open for 0% of the time, Pallas kernels for 36%

profile of v4, /device:TPU:0, one launch (start us, length us, event | category | flops | bytes accessed | tf_op | source)
XLA Modules:
  0.0 29.8 jit_solution(17645988607714034359)
XLA Ops:
  0.6 0.0 copy-start.1
  0.6 1.3 %collective-permute-start = (bf16[512,512]{1,0:T(8,128)(2,1)}, bf16[512,512]{1,0:T(8,128)(2,1)S(1)}, u32[]{:S(2)}, u32[]{:S(2)}) collective-permute-start(bf16[512,512]{1,0:T(8,128)(2,1)} %bitcast.1.tile_ref), channel_id=1, source_target_pairs={{1,0},{2,1},{3,2},{4,3},{5,4},{6,5},{7,6},{8,7},{9,8},{10,9},{11,1... | collective-permute-start | bytes 1572872 | tf_op jit(solution)/shard_map/ppermute | solution.py:325
  1.9 1.3 %collective-permute-start.1 = (bf16[512,512]{1,0:T(8,128)(2,1)}, bf16[512,512]{1,0:T(8,128)(2,1)S(1)}, u32[]{:S(2)}, u32[]{:S(2)}) collective-permute-start(bf16[512,512]{1,0:T(8,128)(2,1)} %bitcast.1.tile_ref), channel_id=1, source_target_pairs={{2,0},{4,2},{6,4},{8,6},{10,8},{12,10},{14,12},{18,16},{20,18},{22... | collective-permute-start | bytes 1572872 | tf_op jit(solution)/shard_map/ppermute | solution.py:325
  3.2 0.0 copy-done.1
  3.2 0.0 copy-start.4
  3.3 1.0 %copy-done.4 = f32[768,128]{1,0:T(8,128)S(1)} copy-done((f32[768,128]{1,0:T(8,128)S(1)}, f32[768,128]{1,0:T(8,128)}, u32[]{:S(2)}) %copy-start.4) | copy-done | bytes 393240
  4.2 0.0 copy-start
  4.3 0.0 copy-start.3
  4.3 0.0 copy-start.5
  4.3 0.0 copy-start.6
  4.3 0.0 copy-start.7
  4.3 0.0 copy-start.8
  4.3 0.0 copy-start.9
  4.3 0.0 copy-start.10
  4.3 2.6 %own_spectrum.1 = (bf16[16,128,256]{2,1,0:T(8,128)(2,1)S(1)}, f32[8,128]{1,0:T(8,128)}) custom-call(s32[2,32]{1,0:T(2,128)S(1)} %bitcast.2, bf16[512,512]{1,0:T(8,128)(2,1)} %bitcast.1.tile_ref, f32[768,128]{1,0:T(8,128)S(1)} %copy-done.4), custom_call_target="tpu_custom_call" | custom-call | flops 4000000000 | bytes 3145728 | tf_op jit(solution)/shard_map/own_spectrum/pallas_call | solution.py:346
  6.9 0.0 copy-start.2
  6.9 0.7 %collective-permute-start.2 = (bf16[512,512]{1,0:T(8,128)(2,1)}, bf16[512,512]{1,0:T(8,128)(2,1)S(1)}, u32[]{:S(2)}, u32[]{:S(2)}) collective-permute-start(bf16[512,512]{1,0:T(8,128)(2,1)} %bitcast.1.tile_ref), channel_id=1, source_target_pairs={{3,1},{5,3},{7,5},{9,7},{11,9},{13,11},{15,13},{19,17},{21,19},{23... | collective-permute-start | bytes 1572872 | tf_op jit(solution)/shard_map/ppermute | solution.py:325
  7.6 0.0 collective-permute-done.refs_10_
  7.6 0.0 copy-done
  7.6 0.0 copy-done.3
  7.7 0.0 copy-done.5
  7.7 0.0 copy-done.6
  7.7 0.0 copy-done.7
  7.7 0.0 copy-done.8
  7.7 0.0 copy-done.9
  7.7 0.0 copy-done.10
  7.7 0.0 copy-done.2
  7.7 4.4 %shard_map.130 = f32[16,3,32]{2,1,0:T(4,128)} custom-call(s32[2,32]{1,0:T(2,128)S(1)} %bitcast.3, bf16[16,128,256]{2,1,0:T(8,128)(2,1)S(1)} %get-tuple-element.7.refs_1_, s32[3,32]{1,0:T(4,128)S(1)} %copy-done, f32[768,128]{1,0:T(8,128)S(1)} %copy-done.5, bf16[256,256]{1,0:T(8,128)(2,1)S(1)} %copy-done.6, bf16[256,128]{1,0:T(8,128)(2,1)S(1)} %copy-done.7, ...), custom_call_target="tpu_custom_call" | custom-call | flops 8000000000 | bytes 4194304 | tf_op jit(solution)/shard_map/pallas_call | solution.py:365
  12.1 10.5 %all-to-all-start = ((f32[16,3,32]{2,1,0:T(4,128)}), f32[16,3,32]{2,1,0:T(4,128)S(1)}, u32[]{:S(2)}, u32[]{:S(2)}) async-start(f32[16,3,32]{2,1,0:T(4,128)} %shard_map.130), calls=%async_computation | async-start | bytes 65536 | tf_op jit(solution)/shard_map/all_to_all | solution.py:387
  22.6 0.0 collective-permute-done.2.refs_11_
  22.6 1.1 %collective-permute-done.1.refs_10_ = bf16[512,512]{1,0:T(8,128)(2,1)S(1)} collective-permute-done((bf16[512,512]{1,0:T(8,128)(2,1)}, bf16[512,512]{1,0:T(8,128)(2,1)S(1)}, u32[]{:S(2)}, u32[]{:S(2)}) %collective-permute-start.1) | collective-permute-done | bytes 524320 | tf_op jit(solution)/shard_map/ppermute | solution.py:325
  23.6 3.8 %shard_map.131.skip_ref = f32[2,32]{1,0:T(2,128)S(1)} custom-call(s32[2,32]{1,0:T(2,128)S(1)} %bitcast.4, bf16[16,128,256]{2,1,0:T(8,128)(2,1)S(1)} %get-tuple-element.7.refs_1_, s32[3,32]{1,0:T(4,128)S(1)} %copy-done, f32[768,128]{1,0:T(8,128)S(1)} %copy-done.5, bf16[256,256]{1,0:T(8,128)(2,1)S(1)} %copy-done.6, bf16[256,128]{1,0:T(8,128)(2,1)S(1)} %copy-done.7, ...), custom_call_target="tpu_custom_call" | custom-call | flops 8000000000 | bytes 4194304 | tf_op jit(solution)/shard_map/pallas_call | solution.py:365
  27.4 1.8 %all-to-all-done.shared_ref = f32[16,3,32]{2,1,0:T(4,128)S(1)} async-done(((f32[16,3,32]{2,1,0:T(4,128)}), f32[16,3,32]{2,1,0:T(4,128)S(1)}, u32[]{:S(2)}, u32[]{:S(2)}) %all-to-all-start) | async-done | bytes 6176 | tf_op jit(solution)/shard_map/all_to_all | solution.py:387
  29.2 0.6 %combine.1 = (f32[1,2,32]{2,1,0:T(2,128)}, f32[1,2,32]{2,1,0:T(2,128)}, f32[1,2,32]{2,1,0:T(2,128)}) custom-call(f32[16,3,32]{2,1,0:T(4,128)S(1)} %all-to-all-done.shared_ref, f32[2,32]{1,0:T(2,128)S(1)} %shard_map.131.skip_ref), custom_call_target="tpu_custom_call" | custom-call | tf_op jit(solution)/shard_map/combine/pallas_call | solution.py:390
Async XLA Ops:
  0.6 2.6 %copy-start.1 = (s32[32,2]{0,1:T(2,128)S(1)}, s32[32,2]{0,1:T(2,128)}, u32[]{:S(2)}) copy-start(s32[32,2]{0,1:T(2,128)} %param.12) | copy-start | bytes 772
  0.6 7.0 %collective-permute-start = (bf16[512,512]{1,0:T(8,128)(2,1)}, bf16[512,512]{1,0:T(8,128)(2,1)S(1)}, u32[]{:S(2)}, u32[]{:S(2)}) collective-permute-start(bf16[512,512]{1,0:T(8,128)(2,1)} %bitcast.1.tile_ref), channel_id=1, source_target_pairs={{1,0},{2,1},{3,2},{4,3},{5,4},{6,5},{7,6},{8,7},{9,8},{10,9},{11,1... | collective-permute-start | bytes 1572872 | tf_op jit(solution)/shard_map/ppermute | solution.py:325
  1.9 21.7 %collective-permute-start.1 = (bf16[512,512]{1,0:T(8,128)(2,1)}, bf16[512,512]{1,0:T(8,128)(2,1)S(1)}, u32[]{:S(2)}, u32[]{:S(2)}) collective-permute-start(bf16[512,512]{1,0:T(8,128)(2,1)} %bitcast.1.tile_ref), channel_id=1, source_target_pairs={{2,0},{4,2},{6,4},{8,6},{10,8},{12,10},{14,12},{18,16},{20,18},{22... | collective-permute-start | bytes 1572872 | tf_op jit(solution)/shard_map/ppermute | solution.py:325
  3.2 1.0 %copy-start.4 = (f32[768,128]{1,0:T(8,128)S(1)}, f32[768,128]{1,0:T(8,128)}, u32[]{:S(2)}) copy-start(f32[768,128]{1,0:T(8,128)} %constant.14.clone.forward_ref.refs_3_) | copy-start | bytes 1179652
  4.2 3.4 %copy-start = (s32[3,32]{1,0:T(4,128)S(1)}, s32[3,32]{1,0:T(4,128)}, u32[]{:S(2)}) copy-start(s32[3,32]{1,0:T(4,128)} %refs_2_.3) | copy-start | bytes 1156
  4.3 3.4 %copy-start.3 = (bf16[5,256,256]{2,1,0:T(8,128)(2,1)S(1)}, bf16[5,256,256]{2,1,0:T(8,128)(2,1)}, u32[]{:S(2)}) copy-start(bf16[5,256,256]{2,1,0:T(8,128)(2,1)} %constant.18.clone.refs_7_) | copy-start | bytes 1966084
  4.3 3.4 %copy-start.5 = (f32[768,128]{1,0:T(8,128)S(1)}, f32[768,128]{1,0:T(8,128)}, u32[]{:S(2)}) copy-start(f32[768,128]{1,0:T(8,128)} %constant.14.clone.forward_ref.refs_3_) | copy-start | bytes 1179652
  4.3 3.4 %copy-start.6 = (bf16[256,256]{1,0:T(8,128)(2,1)S(1)}, bf16[256,256]{1,0:T(8,128)(2,1)}, u32[]{:S(2)}) copy-start(bf16[256,256]{1,0:T(8,128)(2,1)} %constant.15.clone.refs_4_) | copy-start | bytes 393220
  4.3 3.4 %copy-start.7 = (bf16[256,128]{1,0:T(8,128)(2,1)S(1)}, bf16[256,128]{1,0:T(8,128)(2,1)}, u32[]{:S(2)}) copy-start(bf16[256,128]{1,0:T(8,128)(2,1)} %constant.16.clone.refs_5_) | copy-start | bytes 196612
  4.3 3.4 %copy-start.8 = (bf16[128,64]{1,0:T(8,128)(2,1)S(1)}, bf16[128,64]{1,0:T(8,128)(2,1)}, u32[]{:S(2)}) copy-start(bf16[128,64]{1,0:T(8,128)(2,1)} %constant.17.clone.refs_6_) | copy-start | bytes 49156
  4.3 3.4 %copy-start.9 = (f32[64,128]{1,0:T(8,128)S(1)}, f32[64,128]{1,0:T(8,128)}, u32[]{:S(2)}) copy-start(f32[64,128]{1,0:T(8,128)} %constant.20.clone.refs_9_) | copy-start | bytes 98308
  4.3 3.4 %copy-start.10 = (f32[2,8,128]{2,1,0:T(8,128)S(1)}, f32[2,8,128]{2,1,0:T(8,128)}, u32[]{:S(2)}) copy-start(f32[2,8,128]{2,1,0:T(8,128)} %constant.19.clone.refs_8_) | copy-start | bytes 24580
  6.9 0.8 %copy-start.2 = (s32[1,32]{1,0:T(1,128)S(1)}, s32[1,32]{1,0:T(1,128)}, u32[]{:S(2)}) copy-start(s32[1,32]{1,0:T(1,128)} %refs_11_.1) | copy-start | bytes 388
  6.9 15.6 %collective-permute-start.2 = (bf16[512,512]{1,0:T(8,128)(2,1)}, bf16[512,512]{1,0:T(8,128)(2,1)S(1)}, u32[]{:S(2)}, u32[]{:S(2)}) collective-permute-start(bf16[512,512]{1,0:T(8,128)(2,1)} %bitcast.1.tile_ref), channel_id=1, source_target_pairs={{3,1},{5,3},{7,5},{9,7},{11,9},{13,11},{15,13},{19,17},{21,19},{23... | collective-permute-start | bytes 1572872 | tf_op jit(solution)/shard_map/ppermute | solution.py:325
  12.1 17.1 %all-to-all-start = ((f32[16,3,32]{2,1,0:T(4,128)}), f32[16,3,32]{2,1,0:T(4,128)S(1)}, u32[]{:S(2)}, u32[]{:S(2)}) async-start(f32[16,3,32]{2,1,0:T(4,128)} %shard_map.130), calls=%async_computation | async-start | bytes 65536 | tf_op jit(solution)/shard_map/all_to_all | solution.py:387

commit v5 on v4

--- a/solution.py
+++ b/solution.py
@@ -98,25 +98,32 @@
     return jnp.concatenate(parts, axis=1).astype(jnp.bfloat16)
 
 
-def pair_spectrum(pair, place_ref, panels, forward_ref, forward):
-    last = panels.shape[0] - 1
+def pair_table(pair, place_ref, forward_ref):
     lane = lax.broadcasted_iota(jnp.int32, (PATCH, PATCH), 1)
-    turned, table = [], []
+    table = []
     for member in range(2):
-        row = place_ref[0, 2 * pair + member]
-        col = place_ref[1, 2 * pair + member]
-        panel = lax.shift_right_logical(col, PATCH.bit_length() - 1)
-        shift = col & (PATCH - 1)
-        here = panels[panel, pl.ds(row, PATCH), :]
-        beside = panels[jnp.minimum(panel + 1, last), pl.ds(row, PATCH), :]
-        turned.append(jnp.where(lane >= shift, here, beside).astype(jnp.bfloat16))
+        shift = place_ref[1, 2 * pair + member] & (PATCH - 1)
         mine = (lane >= HALF) == (member == 1)
         parts = [
             jnp.where(mine, forward_ref[pl.ds((2 * order + 1) * PATCH - shift, PATCH), :], 0.0)
             for order in (member, 1 - member)
         ]
         table.append(jnp.concatenate(parts, axis=1).astype(jnp.bfloat16))
-    cols = product(jnp.concatenate(turned, axis=1), jnp.concatenate(table, axis=0)).astype(jnp.bfloat16)
+    return jnp.concatenate(table, axis=0)
+
+
+def pair_spectrum(pair, place_ref, panels, table, forward):
+    last = panels.shape[0] - 1
+    lane = lax.broadcasted_iota(jnp.int32, (PATCH, PATCH), 1)
+    turned = []
+    for member in range(2):
+        row = place_ref[0, 2 * pair + member]
+        col = place_ref[1, 2 * pair + member]
+        panel = lax.shift_right_logical(col, PATCH.bit_length() - 1)
+        here = panels[panel, pl.ds(row, PATCH), :]
+        beside = panels[jnp.minimum(panel + 1, last), pl.ds(row, PATCH), :]
+        turned.append(jnp.where(lane >= (col & (PATCH - 1)), here, beside).astype(jnp.bfloat16))
+    cols = product(jnp.concatenate(turned, axis=1), table).astype(jnp.bfloat16)
     crossed = jnp.concatenate([-cols[:, PATCH:], cols[:, :PATCH]], axis=1)
     return product(forward, jnp.concatenate([cols, crossed], axis=0)).astype(jnp.bfloat16)
 
@@ -128,10 +135,9 @@
     copy.wait()
 
 
-def own_kernel(corners_ref, tile_ref, forward_ref, spec_ref, started_ref, held, panels, place_ref, sems):
+def own_kernel(corners_ref, tile_ref, forward_ref, spec_ref, table_ref, held, panels, place_ref, sems):
     fetch = pltpu.make_async_copy(tile_ref, held, sems.at[0])
     fetch.start()
-    started_ref[...] = jnp.zeros_like(started_ref)
 
     def fill():
         fetch.wait()
@@ -140,11 +146,13 @@
     with_corners(corners_ref, place_ref, sems.at[1], fill)
     forward = transform_of(forward_ref)
     for pair in range(spec_ref.shape[0]):
-        spec_ref[pair] = pair_spectrum(pair, place_ref, panels, forward_ref, forward)
+        table = pair_table(pair, place_ref, forward_ref)
+        table_ref[pair] = table
+        spec_ref[pair] = pair_spectrum(pair, place_ref, panels, table, forward)
 
 
 def estimate(
-    tile_refs, corners_ref, spec_ref, usage_ref, forward_ref, rows0_ref, rows1_ref, rows2_ref, cols_ref,
+    tile_refs, table_ref, corners_ref, spec_ref, usage_ref, forward_ref, rows0_ref, rows1_ref, rows2_ref, cols_ref,
      moments_ref, slopes_ref, panels, place_ref, sem, cross0, cross1, cross2, half0, half1, half2, plain,
     nested,
 ):
@@ -169,7 +177,8 @@
         inner = []
         for pair in range(PAIRS):
             place = group * PAIRS + pair
-            other = pair_spectrum(place, place_ref, panels, forward_ref, forward).astype(jnp.float32)
+            table = pair_table(place, place_ref, forward_ref) if table_ref is None else table_ref[place]
+            other = pair_spectrum(place, place_ref, panels, table, forward).astype(jnp.float32)
             own = spec_ref[place].astype(jnp.float32)
             own_real, own_imag = own[:, :PATCH], own[:, PATCH:]
             other_real, other_imag = other[:, :PATCH], other[:, PATCH:]
@@ -211,10 +220,14 @@
             weight = block * block
             running = weight if running is None else running + weight
             ladder = running if ladder is None else ladder + running
+        sublane = lax.broadcasted_iota(jnp.int32, running.shape, 0).astype(jnp.float32)
+        by_col = jnp.sum(running, axis=0, keepdims=True)
+        by_row = jnp.sum((HALF + sublane) * running - 8.0 * ladder, axis=0, keepdims=True)
         for turn, member in enumerate(members):
             lanes = slice(turn * PATCH, (turn + 1) * PATCH)
-            plain[level, group * GROUP + member] = running[:, lanes]
-            nested[level, group * GROUP + member] = ladder[:, lanes]
+            place = group * GROUP + member
+            plain[level, place : place + 1] = by_col[:, lanes]
+            nested[level, place : place + 1] = by_row[:, lanes]
 
     def sums_stage(group, slot):
         correl = product(
@@ -239,10 +252,12 @@
                     sloped = weight * slopes_ref[row : row + 8]
                     total = weight if total is None else total + weight
                     slope = sloped if slope is None else slope + sloped
+                total = jnp.sum(total, axis=0, keepdims=True)
+                slope = jnp.sum(slope, axis=0, keepdims=True)
                 for member in range(2):
                     place = group * GROUP + 4 * part + 2 * turn + member
-                    plain[2, place] = total
-                    nested[2, place] = slope
+                    plain[2, place : place + 1] = total
+                    nested[2, place : place + 1] = slope
 
     for turn in range(groups + 2):
         if turn < groups:
@@ -260,14 +275,7 @@
     )
     along_rows, along_cols = 0.0, 0.0
     for level in range(LEVELS):
-        by_col, by_row = 0.0, 0.0
-        for sublane in range(8):
-            part = plain[level, :, sublane, :]
-            by_col = by_col + part
-            if level < 2:
-                by_row = by_row + ((HALF + sublane) * part - 8.0 * nested[level, :, sublane, :])
-            else:
-                by_row = by_row + nested[level, :, sublane, :]
+        by_col, by_row = plain[level], nested[level]
         if level == 2:
             by_col = jnp.where(own_lanes, by_col, 0.0)
             by_row = jnp.where(own_lanes, by_row, 0.0)
@@ -289,15 +297,15 @@
 
 
 def next_kernel(*refs):
-    ins, (tile_ref, mask_ref, out_ref), scratch = refs[:INS], refs[INS : INS + 3], refs[INS + 3 :]
-    message = jnp.concatenate([estimate([tile_ref], *ins, *scratch), mask_ref[...].astype(jnp.float32)], axis=0)
+    ins, (tile_ref, table_ref, mask_ref, out_ref), scratch = refs[:INS], refs[INS : INS + 4], refs[INS + 4 :]
+    message = jnp.concatenate([estimate([tile_ref], table_ref, *ins, *scratch), mask_ref[...].astype(jnp.float32)], axis=0)
     for section in range(out_ref.shape[0]):
         out_ref[section] = message
 
 
 def skip_kernel(*refs):
     ins, tile_refs, out_ref, scratch = refs[:INS], refs[INS : INS + 2], refs[INS + 2], refs[INS + 3 :]
-    out_ref[...] = estimate(tile_refs, *ins, *scratch)
+    out_ref[...] = estimate(tile_refs, None, *ins, *scratch)
 
 
 def combine_kernel(shared_ref, skip_ref, *outs):
@@ -336,16 +344,16 @@
     corners = placement.T
     corner_scratch = [pltpu.SMEM(corners.shape, corners.dtype), pltpu.SemaphoreType.DMA]
     spec = jax.ShapeDtypeStruct((patches // 2, PATCH, 2 * PATCH), jnp.bfloat16)
-    sums = pltpu.VMEM((LEVELS, patches, 8, PATCH), jnp.float32)
+    sums = pltpu.VMEM((LEVELS, patches, PATCH), jnp.float32)
 
     def limit(mebibytes):
         return pltpu.CompilerParams(vmem_limit_bytes=mebibytes * 2**20)
 
     next_tile = moved(tile, "sec", 1)
     even_tile = moved(tile, "sec", 2, (0,))
-    own_spec, started = pl.pallas_call(
+    own_spec, col_tables = pl.pallas_call(
         own_kernel,
-        out_shape=(spec, jax.ShapeDtypeStruct((8, PATCH), jnp.float32)),
+        out_shape=(spec, jax.ShapeDtypeStruct((patches // 2, 2 * PATCH, 2 * PATCH), jnp.bfloat16)),
         in_specs=[vmem, pl.BlockSpec(memory_space=pltpu.HBM), vmem],
         out_specs=(vmem, vmem),
         scratch_shapes=[
@@ -358,7 +366,7 @@
         cost_estimate=pl.CostEstimate(flops=4 * 10**9, bytes_accessed=3 * 2**20, transcendentals=0),
         name="own_spectrum",
     )(corners, tile, forward)
-    later_tile, own_spec, _ = lax.optimization_barrier((tile, own_spec, started))
+    later_tile, own_spec = lax.optimization_barrier((tile, own_spec))
     odd_tile = moved(later_tile, "sec", 2, (1,))
 
     def flow(kernel, out_shape, *more):
@@ -383,7 +391,7 @@
             cost_estimate=pl.CostEstimate(flops=8 * 10**9, bytes_accessed=4 * 2**20, transcendentals=0),
         )(corners, own_spec, level_use, forward, *rest, *more)
 
-    message = flow(next_kernel, (sections, 3, patches), next_tile, tissue_mask)
+    message = flow(next_kernel, (sections, 3, patches), next_tile, col_tables, tissue_mask)
     shared = lax.all_to_all(message, "sec", 0, 0)
     flow_skip = flow(skip_kernel, (2, patches), even_tile, odd_tile)
     out = jax.ShapeDtypeStruct((1, 2, patches), jnp.float32)

time: 30.1 us -> 29.9 us (level)
  Pallas kernels: 11.3 us -> 10.6 us
  local copies, waits for them, and re-layouts: 1.04 us -> 1.72 us
  starting transfers between devices: 13.7 us -> 13.3 us
    all_to_all x1, waiting for transfers between devices: 1.79 us -> 2.47 us  [on_device(): shared = lax.all_to_all(message, 'sec', 0, 0)]
    unnamed x22 -> x24, local copies, waits for them, and re-layouts: 1.04 us -> 1.72 us
    pallas_call x2, Pallas kernels: 8.12 us -> 7.54 us  [flow(): pl.pallas_call(kernel, out_shape=jax.ShapeDtypeStruct(out_shape, jnp.floa...]
    ppermute x3, waiting for transfers between devices: 1.08 us -> 0.62 us  [moved(): return lax.ppermute(block, axis, route)]
    all_to_all x1, starting transfers between devices: 10.5 us -> 10 us  [on_device(): shared = lax.all_to_all(message, 'sec', 0, 0)]
  transfers between devices with their start and end apart: 4 -> 4, of which waited for: 2 -> 2; matrix products, arithmetic and copies ran while one was open for 0% -> 0% of each run, Pallas kernels for 36% -> 34%
where the time goes in v5:
time: 29.9 us; the launch traced here: 29.6 us
  starting transfers between devices  13.3 us (44%)
  Pallas kernels  10.6 us (35%)
  waiting for transfers between devices  3.09 us (10%)
  local copies, waits for them, and re-layouts  1.72 us (6%)
  between operations  0.84 us (3%)
    all_to_all x1, starting transfers between devices, on_device(): shared = lax.all_to_all(message, 'sec', 0, 0)  10 us
    pallas_call x2, Pallas kernels, flow(): pl.pallas_call(kernel, out_shape=jax.ShapeDtypeStruct(out_shape, jnp.floa...  7.54 us
    ppermute x3, starting transfers between devices, moved(): return lax.ppermute(block, axis, route)  3.28 us
    pallas_call x1, Pallas kernels, on_device(): pl.pallas_call(own_kernel, out_shape=(spec, jax.ShapeDtypeStruct((patches...  2.52 us
    all_to_all x1, waiting for transfers between devices, on_device(): shared = lax.all_to_all(message, 'sec', 0, 0)  2.47 us
    unnamed x24, local copies, waits for them, and re-layouts  1.72 us
    ppermute x3, waiting for transfers between devices, moved(): return lax.ppermute(block, axis, route)  0.62 us
  transfers between devices with their start and end apart: 4, of which 2 were waited for; matrix products, arithmetic and copies ran while one was open for 0% of the time, Pallas kernels for 34%

profile of v5, /device:TPU:0, one launch (start us, length us, event | category | flops | bytes accessed | tf_op | source)
XLA Modules:
  0.0 29.6 jit_solution(17476999243023823225)
XLA Ops:
  0.6 1.3 %collective-permute-start = (bf16[512,512]{1,0:T(8,128)(2,1)}, bf16[512,512]{1,0:T(8,128)(2,1)S(1)}, u32[]{:S(2)}, u32[]{:S(2)}) collective-permute-start(bf16[512,512]{1,0:T(8,128)(2,1)} %bitcast.1.tile_ref), channel_id=1, source_target_pairs={{1,0},{2,1},{3,2},{4,3},{5,4},{6,5},{7,6},{8,7},{9,8},{10,9},{11,1... | collective-permute-start | bytes 1572872 | tf_op jit(solution)/shard_map/ppermute | solution.py:333
  1.9 1.3 %collective-permute-start.1 = (bf16[512,512]{1,0:T(8,128)(2,1)}, bf16[512,512]{1,0:T(8,128)(2,1)S(1)}, u32[]{:S(2)}, u32[]{:S(2)}) collective-permute-start(bf16[512,512]{1,0:T(8,128)(2,1)} %bitcast.1.tile_ref), channel_id=1, source_target_pairs={{2,0},{4,2},{6,4},{8,6},{10,8},{12,10},{14,12},{18,16},{20,18},{22... | collective-permute-start | bytes 1572872 | tf_op jit(solution)/shard_map/ppermute | solution.py:333
  3.2 0.0 copy-start.1
  3.2 0.7 %copy-done.1 = s32[32,2]{0,1:T(2,128)S(1)} copy-done((s32[32,2]{0,1:T(2,128)S(1)}, s32[32,2]{0,1:T(2,128)}, u32[]{:S(2)}) %copy-start.1) | copy-done | bytes 280
  3.9 0.0 copy-start.5
  3.9 1.0 %copy-done.5 = f32[768,128]{1,0:T(8,128)S(1)} copy-done((f32[768,128]{1,0:T(8,128)S(1)}, f32[768,128]{1,0:T(8,128)}, u32[]{:S(2)}) %copy-start.5) | copy-done | bytes 393240
  4.9 0.0 copy-start
  4.9 0.0 copy-start.2
  4.9 0.0 copy-start.3
  4.9 0.0 copy-start.4
  4.9 0.0 copy-start.6
  4.9 0.0 copy-start.7
  4.9 0.0 copy-start.8
  5.0 0.0 copy-start.9
  5.0 0.0 copy-start.10
  5.0 0.0 copy-start.11
  5.0 2.5 %own_spectrum.1 = (bf16[16,128,256]{2,1,0:T(8,128)(2,1)S(1)}, bf16[16,256,256]{2,1,0:T(8,128)(2,1)S(1)}) custom-call(s32[2,32]{1,0:T(2,128)S(1)} %bitcast.2, bf16[512,512]{1,0:T(8,128)(2,1)} %bitcast.1.tile_ref, f32[768,128]{1,0:T(8,128)S(1)} %copy-done.5), custom_call_target="tpu_custom_call" | custom-call | flops 4000000000 | bytes 3145728 | tf_op jit(solution)/shard_map/own_spectrum/pallas_call | solution.py:354
  7.5 0.7 %collective-permute-start.2 = (bf16[512,512]{1,0:T(8,128)(2,1)}, bf16[512,512]{1,0:T(8,128)(2,1)S(1)}, u32[]{:S(2)}, u32[]{:S(2)}) collective-permute-start(bf16[512,512]{1,0:T(8,128)(2,1)} %bitcast.1.tile_ref), channel_id=1, source_target_pairs={{3,1},{5,3},{7,5},{9,7},{11,9},{13,11},{15,13},{19,17},{21,19},{23... | collective-permute-start | bytes 1572872 | tf_op jit(solution)/shard_map/ppermute | solution.py:333
  8.2 0.0 collective-permute-done.refs_10_
  8.2 0.0 copy-done
  8.2 0.0 copy-done.2
  8.3 0.0 copy-done.3
  8.3 0.0 copy-done.4
  8.3 0.0 copy-done.6
  8.3 0.0 copy-done.7
  8.3 0.0 copy-done.8
  8.3 0.0 copy-done.9
  8.3 0.0 copy-done.10
  8.3 0.0 copy-done.11
  8.3 4.0 %shard_map.130 = f32[16,3,32]{2,1,0:T(4,128)} custom-call(s32[2,32]{1,0:T(2,128)S(1)} %bitcast.3, bf16[16,128,256]{2,1,0:T(8,128)(2,1)S(1)} %get-tuple-element.8.refs_1_, s32[3,32]{1,0:T(4,128)S(1)} %copy-done, f32[768,128]{1,0:T(8,128)S(1)} %copy-done.6, bf16[256,256]{1,0:T(8,128)(2,1)S(1)} %copy-done.7, bf16[256,128]{1,0:T(8,128)(2,1)S(1)} %copy-done.8, ...), custom_call_target="tpu_custom_call" | custom-call | flops 8000000000 | bytes 4194304 | tf_op jit(solution)/shard_map/pallas_call | solution.py:373
  12.4 10.0 %all-to-all-start = ((f32[16,3,32]{2,1,0:T(4,128)}), f32[16,3,32]{2,1,0:T(4,128)S(1)}, u32[]{:S(2)}, u32[]{:S(2)}) async-start(f32[16,3,32]{2,1,0:T(4,128)} %shard_map.130), calls=%async_computation | async-start | bytes 65536 | tf_op jit(solution)/shard_map/all_to_all | solution.py:395
  22.4 0.6 %collective-permute-done.1.refs_10_ = bf16[512,512]{1,0:T(8,128)(2,1)S(1)} collective-permute-done((bf16[512,512]{1,0:T(8,128)(2,1)}, bf16[512,512]{1,0:T(8,128)(2,1)S(1)}, u32[]{:S(2)}, u32[]{:S(2)}) %collective-permute-start.1) | collective-permute-done | bytes 524320 | tf_op jit(solution)/shard_map/ppermute | solution.py:333
  23.0 0.0 collective-permute-done.2.refs_11_
  23.0 3.5 %shard_map.131.skip_ref = f32[2,32]{1,0:T(2,128)S(1)} custom-call(s32[2,32]{1,0:T(2,128)S(1)} %bitcast.4, bf16[16,128,256]{2,1,0:T(8,128)(2,1)S(1)} %get-tuple-element.8.refs_1_, s32[3,32]{1,0:T(4,128)S(1)} %copy-done, f32[768,128]{1,0:T(8,128)S(1)} %copy-done.6, bf16[256,256]{1,0:T(8,128)(2,1)S(1)} %copy-done.7, bf16[256,128]{1,0:T(8,128)(2,1)S(1)} %copy-done.8, ...), custom_call_target="tpu_custom_call" | custom-call | flops 8000000000 | bytes 4194304 | tf_op jit(solution)/shard_map/pallas_call | solution.py:373
  26.6 2.5 %all-to-all-done.shared_ref = f32[16,3,32]{2,1,0:T(4,128)S(1)} async-done(((f32[16,3,32]{2,1,0:T(4,128)}), f32[16,3,32]{2,1,0:T(4,128)S(1)}, u32[]{:S(2)}, u32[]{:S(2)}) %all-to-all-start) | async-done | bytes 6176 | tf_op jit(solution)/shard_map/all_to_all | solution.py:395
  29.0 0.6 %combine.1 = (f32[1,2,32]{2,1,0:T(2,128)}, f32[1,2,32]{2,1,0:T(2,128)}, f32[1,2,32]{2,1,0:T(2,128)}) custom-call(f32[16,3,32]{2,1,0:T(4,128)S(1)} %all-to-all-done.shared_ref, f32[2,32]{1,0:T(2,128)S(1)} %shard_map.131.skip_ref), custom_call_target="tpu_custom_call" | custom-call | tf_op jit(solution)/shard_map/combine/pallas_call | solution.py:398
Async XLA Ops:
  0.6 7.6 %collective-permute-start = (bf16[512,512]{1,0:T(8,128)(2,1)}, bf16[512,512]{1,0:T(8,128)(2,1)S(1)}, u32[]{:S(2)}, u32[]{:S(2)}) collective-permute-start(bf16[512,512]{1,0:T(8,128)(2,1)} %bitcast.1.tile_ref), channel_id=1, source_target_pairs={{1,0},{2,1},{3,2},{4,3},{5,4},{6,5},{7,6},{8,7},{9,8},{10,9},{11,1... | collective-permute-start | bytes 1572872 | tf_op jit(solution)/shard_map/ppermute | solution.py:333
  1.9 21.1 %collective-permute-start.1 = (bf16[512,512]{1,0:T(8,128)(2,1)}, bf16[512,512]{1,0:T(8,128)(2,1)S(1)}, u32[]{:S(2)}, u32[]{:S(2)}) collective-permute-start(bf16[512,512]{1,0:T(8,128)(2,1)} %bitcast.1.tile_ref), channel_id=1, source_target_pairs={{2,0},{4,2},{6,4},{8,6},{10,8},{12,10},{14,12},{18,16},{20,18},{22... | collective-permute-start | bytes 1572872 | tf_op jit(solution)/shard_map/ppermute | solution.py:333
  3.2 0.7 %copy-start.1 = (s32[32,2]{0,1:T(2,128)S(1)}, s32[32,2]{0,1:T(2,128)}, u32[]{:S(2)}) copy-start(s32[32,2]{0,1:T(2,128)} %param.12) | copy-start | bytes 772
  3.9 1.0 %copy-start.5 = (f32[768,128]{1,0:T(8,128)S(1)}, f32[768,128]{1,0:T(8,128)}, u32[]{:S(2)}) copy-start(f32[768,128]{1,0:T(8,128)} %constant.14.clone.forward_ref.refs_3_) | copy-start | bytes 1179652
  4.9 3.3 %copy-start = (s32[3,32]{1,0:T(4,128)S(1)}, s32[3,32]{1,0:T(4,128)}, u32[]{:S(2)}) copy-start(s32[3,32]{1,0:T(4,128)} %refs_2_.3) | copy-start | bytes 1156
  4.9 3.3 %copy-start.2 = (s32[32,2]{0,1:T(2,128)S(1)}, s32[32,2]{0,1:T(2,128)}, u32[]{:S(2)}) copy-start(s32[32,2]{0,1:T(2,128)} %param.12) | copy-start | bytes 772
  4.9 3.3 %copy-start.3 = (s32[1,32]{1,0:T(1,128)S(1)}, s32[1,32]{1,0:T(1,128)}, u32[]{:S(2)}) copy-start(s32[1,32]{1,0:T(1,128)} %refs_12_.1) | copy-start | bytes 388
  4.9 3.4 %copy-start.4 = (bf16[5,256,256]{2,1,0:T(8,128)(2,1)S(1)}, bf16[5,256,256]{2,1,0:T(8,128)(2,1)}, u32[]{:S(2)}) copy-start(bf16[5,256,256]{2,1,0:T(8,128)(2,1)} %constant.18.clone.refs_7_) | copy-start | bytes 1966084
  4.9 3.4 %copy-start.6 = (f32[768,128]{1,0:T(8,128)S(1)}, f32[768,128]{1,0:T(8,128)}, u32[]{:S(2)}) copy-start(f32[768,128]{1,0:T(8,128)} %constant.14.clone.forward_ref.refs_3_) | copy-start | bytes 1179652
  4.9 3.4 %copy-start.7 = (bf16[256,256]{1,0:T(8,128)(2,1)S(1)}, bf16[256,256]{1,0:T(8,128)(2,1)}, u32[]{:S(2)}) copy-start(bf16[256,256]{1,0:T(8,128)(2,1)} %constant.15.clone.refs_4_) | copy-start | bytes 393220
  4.9 3.4 %copy-start.8 = (bf16[256,128]{1,0:T(8,128)(2,1)S(1)}, bf16[256,128]{1,0:T(8,128)(2,1)}, u32[]{:S(2)}) copy-start(bf16[256,128]{1,0:T(8,128)(2,1)} %constant.16.clone.refs_5_) | copy-start | bytes 196612
  5.0 3.3 %copy-start.9 = (bf16[128,64]{1,0:T(8,128)(2,1)S(1)}, bf16[128,64]{1,0:T(8,128)(2,1)}, u32[]{:S(2)}) copy-start(bf16[128,64]{1,0:T(8,128)(2,1)} %constant.17.clone.refs_6_) | copy-start | bytes 49156
  5.0 3.3 %copy-start.10 = (f32[64,128]{1,0:T(8,128)S(1)}, f32[64,128]{1,0:T(8,128)}, u32[]{:S(2)}) copy-start(f32[64,128]{1,0:T(8,128)} %constant.20.clone.refs_9_) | copy-start | bytes 98308
  5.0 3.3 %copy-start.11 = (f32[2,8,128]{2,1,0:T(8,128)S(1)}, f32[2,8,128]{2,1,0:T(8,128)}, u32[]{:S(2)}) copy-start(f32[2,8,128]{2,1,0:T(8,128)} %constant.19.clone.refs_8_) | copy-start | bytes 24580
  7.5 15.5 %collective-permute-start.2 = (bf16[512,512]{1,0:T(8,128)(2,1)}, bf16[512,512]{1,0:T(8,128)(2,1)S(1)}, u32[]{:S(2)}, u32[]{:S(2)}) collective-permute-start(bf16[512,512]{1,0:T(8,128)(2,1)} %bitcast.1.tile_ref), channel_id=1, source_target_pairs={{3,1},{5,3},{7,5},{9,7},{11,9},{13,11},{15,13},{19,17},{21,19},{23... | collective-permute-start | bytes 1572872 | tf_op jit(solution)/shard_map/ppermute | solution.py:333
  12.4 16.7 %all-to-all-start = ((f32[16,3,32]{2,1,0:T(4,128)}), f32[16,3,32]{2,1,0:T(4,128)S(1)}, u32[]{:S(2)}, u32[]{:S(2)}) async-start(f32[16,3,32]{2,1,0:T(4,128)} %shard_map.130), calls=%async_computation | async-start | bytes 65536 | tf_op jit(solution)/shard_map/all_to_all | solution.py:395

commit v6 on v5

--- a/solution.py
+++ b/solution.py
@@ -98,6 +98,14 @@
     return jnp.concatenate(parts, axis=1).astype(jnp.bfloat16)
 
 
+class Direct:
+    def __init__(self, corners_ref):
+        self.values = corners_ref[...]
+
+    def __getitem__(self, at):
+        return self.values[at[0], at[1]]
+
+
 def pair_table(pair, place_ref, forward_ref):
     lane = lax.broadcasted_iota(jnp.int32, (PATCH, PATCH), 1)
     table = []
@@ -112,7 +120,7 @@
     return jnp.concatenate(table, axis=0)
 
 
-def pair_spectrum(pair, place_ref, panels, table, forward):
+def turned_patches(pair, place_ref, panels):
     last = panels.shape[0] - 1
     lane = lax.broadcasted_iota(jnp.int32, (PATCH, PATCH), 1)
     turned = []
@@ -123,37 +131,44 @@
         here = panels[panel, pl.ds(row, PATCH), :]
         beside = panels[jnp.minimum(panel + 1, last), pl.ds(row, PATCH), :]
         turned.append(jnp.where(lane >= (col & (PATCH - 1)), here, beside).astype(jnp.bfloat16))
-    cols = product(jnp.concatenate(turned, axis=1), table).astype(jnp.bfloat16)
-    crossed = jnp.concatenate([-cols[:, PATCH:], cols[:, :PATCH]], axis=1)
-    return product(forward, jnp.concatenate([cols, crossed], axis=0)).astype(jnp.bfloat16)
-
-
-def with_corners(corners_ref, place_ref, sem, work):
-    copy = pltpu.make_async_copy(corners_ref, place_ref, sem)
-    copy.start()
-    work()
-    copy.wait()
-
-
-def own_kernel(corners_ref, tile_ref, forward_ref, spec_ref, table_ref, held, panels, place_ref, sems):
-    fetch = pltpu.make_async_copy(tile_ref, held, sems.at[0])
-    fetch.start()
-
-    def fill():
-        fetch.wait()
-        fill_panels(held, panels)
-
-    with_corners(corners_ref, place_ref, sems.at[1], fill)
-    forward = transform_of(forward_ref)
+    return jnp.concatenate(turned, axis=1)
+
+
+def crossed(parts):
+    return jnp.concatenate([-parts[:, PATCH:], parts[:, :PATCH]], axis=1)
+
+
+def spectrum_by_columns(patches, table, forward):
+    cols = product(patches, table).astype(jnp.bfloat16)
+    return product(forward, jnp.concatenate([cols, crossed(cols)], axis=0)).astype(jnp.bfloat16)
+
+
+def spectrum_by_rows(patches, table, stacked):
+    rows = product(stacked, patches).astype(jnp.bfloat16)
+    return (product(rows[:PATCH], table) + product(rows[PATCH:], crossed(table))).astype(jnp.bfloat16)
+
+
+def own_kernel(corners_ref, tile_ref, tables_ref, spec_ref, table_ref, held, panels, forward_ref, corners, sems):
+    copies = [
+        pltpu.make_async_copy(source, target, sems.at[turn])
+        for turn, (source, target) in enumerate(((tile_ref, held), (tables_ref, forward_ref), (corners_ref, corners)))
+    ]
+    for copy in copies:
+        copy.start()
+    for copy in copies:
+        copy.wait()
+    place_ref = Direct(corners)
+    stacked = forward_ref[forward_ref.shape[0] - 2 * PATCH :].astype(jnp.bfloat16)
+    fill_panels(held, panels)
     for pair in range(spec_ref.shape[0]):
         table = pair_table(pair, place_ref, forward_ref)
         table_ref[pair] = table
-        spec_ref[pair] = pair_spectrum(pair, place_ref, panels, table, forward)
+        spec_ref[pair] = spectrum_by_rows(turned_patches(pair, place_ref, panels), table, stacked)
 
 
 def estimate(
     tile_refs, table_ref, corners_ref, spec_ref, usage_ref, forward_ref, rows0_ref, rows1_ref, rows2_ref, cols_ref,
-     moments_ref, slopes_ref, panels, place_ref, sem, cross0, cross1, cross2, half0, half1, half2, plain,
+     moments_ref, slopes_ref, panels, cross0, cross1, cross2, half0, half1, half2, plain,
     nested,
 ):
     def fill():
@@ -164,8 +179,9 @@
             for parity, tile_ref in enumerate(tile_refs):
                 pl.when(odd == parity)(functools.partial(fill_panels, tile_ref, panels))
 
-    with_corners(corners_ref, place_ref, sem, fill)
-    groups = place_ref.shape[1] // GROUP
+    fill()
+    groups = corners_ref.shape[1] // GROUP
+    place_ref = Direct(corners_ref)
     quarter, eighth = PATCH // 4, PATCH // 8
 
     def packed(even, odd, width):
@@ -178,7 +194,7 @@
         for pair in range(PAIRS):
             place = group * PAIRS + pair
             table = pair_table(place, place_ref, forward_ref) if table_ref is None else table_ref[place]
-            other = pair_spectrum(place, place_ref, panels, table, forward).astype(jnp.float32)
+            other = spectrum_by_columns(turned_patches(place, place_ref, panels), table, forward).astype(jnp.float32)
             own = spec_ref[place].astype(jnp.float32)
             own_real, own_imag = own[:, :PATCH], own[:, PATCH:]
             other_real, other_imag = other[:, :PATCH], other[:, PATCH:]
@@ -201,11 +217,11 @@
         ]
         cross2[slot] = packed(inner[0], inner[1], eighth).astype(jnp.bfloat16)
 
-    def half_stage(slot):
+    def half_stage(source, slot):
         for turn in range(PAIRS // 2):
-            half0[slot, turn] = product(rows0_ref[...], cross0[slot, turn]).astype(jnp.bfloat16)
-        half1[slot] = product(rows1_ref[...], cross1[slot]).astype(jnp.bfloat16)
-        half2[slot] = product(rows2_ref[...], cross2[slot]).astype(jnp.bfloat16)
+            half0[slot, turn] = product(rows0_ref[...], cross0[source, turn]).astype(jnp.bfloat16)
+        half1[slot] = product(rows1_ref[...], cross1[source]).astype(jnp.bfloat16)
+        half2[slot] = product(rows2_ref[...], cross2[source]).astype(jnp.bfloat16)
 
     def lines(half, tile):
         lanes = slice(tile * PATCH, (tile + 1) * PATCH)
@@ -259,13 +275,13 @@
                     plain[2, place : place + 1] = total
                     nested[2, place : place + 1] = slope
 
-    for turn in range(groups + 2):
+    for turn in range(groups + 4):
         if turn < groups:
-            cross_stage(turn, turn % 2)
-        if 1 <= turn <= groups:
-            half_stage((turn - 1) % 2)
-        if turn >= 2:
-            sums_stage(turn - 2, turn % 2)
+            cross_stage(turn, turn % 4)
+        if 3 <= turn <= groups + 2:
+            half_stage((turn - 3) % 4, (turn - 1) % 2)
+        if turn >= 4:
+            sums_stage(turn - 4, turn % 2)
 
     usage = usage_ref[...].astype(jnp.float32)
     across = (((1,), (1,)), ((), ()))
@@ -342,7 +358,6 @@
     vmem = pl.BlockSpec(memory_space=pltpu.VMEM)
     panels = (side // PATCH, side, PATCH)
     corners = placement.T
-    corner_scratch = [pltpu.SMEM(corners.shape, corners.dtype), pltpu.SemaphoreType.DMA]
     spec = jax.ShapeDtypeStruct((patches // 2, PATCH, 2 * PATCH), jnp.bfloat16)
     sums = pltpu.VMEM((LEVELS, patches, PATCH), jnp.float32)
 
@@ -354,18 +369,19 @@
     own_spec, col_tables = pl.pallas_call(
         own_kernel,
         out_shape=(spec, jax.ShapeDtypeStruct((patches // 2, 2 * PATCH, 2 * PATCH), jnp.bfloat16)),
-        in_specs=[vmem, pl.BlockSpec(memory_space=pltpu.HBM), vmem],
+        in_specs=[pl.BlockSpec(memory_space=pltpu.HBM)] * 3,
         out_specs=(vmem, vmem),
         scratch_shapes=[
             pltpu.VMEM(tile.shape, tile.dtype),
             pltpu.VMEM(panels, jnp.float32),
-            corner_scratch[0],
-            pltpu.SemaphoreType.DMA((2,)),
+            pltpu.VMEM(forward.shape, forward.dtype),
+            pltpu.VMEM(corners.shape, corners.dtype),
+            pltpu.SemaphoreType.DMA((3,)),
         ],
         compiler_params=limit(8),
         cost_estimate=pl.CostEstimate(flops=4 * 10**9, bytes_accessed=3 * 2**20, transcendentals=0),
         name="own_spectrum",
-    )(corners, tile, forward)
+    )(*(pltpu.with_memory_space_constraint(array, pltpu.HBM) for array in (corners, tile, forward)))
     later_tile, own_spec = lax.optimization_barrier((tile, own_spec))
     odd_tile = moved(later_tile, "sec", 2, (1,))
 
@@ -377,10 +393,9 @@
             out_specs=vmem,
             scratch_shapes=[
                 pltpu.VMEM(panels, jnp.float32),
-                *corner_scratch,
-                pltpu.VMEM((2, PAIRS // 2, 2 * PATCH, 2 * PATCH), jnp.bfloat16),
-                pltpu.VMEM((2, PATCH, 2 * PATCH), jnp.bfloat16),
-                pltpu.VMEM((2, HALF, PATCH), jnp.bfloat16),
+                pltpu.VMEM((4, PAIRS // 2, 2 * PATCH, 2 * PATCH), jnp.bfloat16),
+                pltpu.VMEM((4, PATCH, 2 * PATCH), jnp.bfloat16),
+                pltpu.VMEM((4, HALF, PATCH), jnp.bfloat16),
                 pltpu.VMEM((2, PAIRS // 2, 2 * PATCH, 2 * PATCH), jnp.bfloat16),
                 pltpu.VMEM((2, 2 * PATCH, 2 * PATCH), jnp.bfloat16),
                 pltpu.VMEM((2, PATCH, PATCH), jnp.bfloat16),

time: 29.9 us -> 29 us (0.970)
  local copies, waits for them, and re-layouts: 1.72 us -> 0.06 us
  starting transfers between devices: 13.3 us -> 13.9 us
  waiting for transfers between devices: 3.09 us -> 3.6 us
    unnamed x24 -> x20, local copies, waits for them, and re-layouts: 1.72 us -> 0.06 us
    ppermute x3, waiting for transfers between devices: 0.62 us -> 2.25 us  [moved(): return lax.ppermute(block, axis, route)]
    pallas_call x2, Pallas kernels: 7.54 us -> 6.42 us  [flow(): pl.pallas_call(kernel, out_shape=jax.ShapeDtypeStruct(out_shape, jnp.floa...]
    all_to_all x1, waiting for transfers between devices: 2.47 us -> 1.35 us  [on_device(): shared = lax.all_to_all(message, 'sec', 0, 0)]
    pallas_call x1, Pallas kernels: 2.52 us -> 3.39 us  [on_device(): pl.pallas_call(own_kernel, out_shape=(spec, jax.ShapeDtypeStruct((patches...]
    all_to_all x1, starting transfers between devices: 10 us -> 10.6 us  [on_device(): shared = lax.all_to_all(message, 'sec', 0, 0)]
where the time goes in v6:
time: 29 us; the launch traced here: 28.8 us
  starting transfers between devices  13.9 us (48%)
  Pallas kernels  10.4 us (36%)
  waiting for transfers between devices  3.6 us (12%)
  between operations  0.84 us (3%)
    all_to_all x1, starting transfers between devices, on_device(): shared = lax.all_to_all(message, 'sec', 0, 0)  10.6 us
    pallas_call x2, Pallas kernels, flow(): pl.pallas_call(kernel, out_shape=jax.ShapeDtypeStruct(out_shape, jnp.floa...  6.42 us
    pallas_call x1, Pallas kernels, on_device(): pl.pallas_call(own_kernel, out_shape=(spec, jax.ShapeDtypeStruct((patches...  3.39 us
    ppermute x3, starting transfers between devices, moved(): return lax.ppermute(block, axis, route)  3.28 us
    ppermute x3, waiting for transfers between devices, moved(): return lax.ppermute(block, axis, route)  2.25 us
    all_to_all x1, waiting for transfers between devices, on_device(): shared = lax.all_to_all(message, 'sec', 0, 0)  1.35 us
    pallas_call x1, Pallas kernels, on_device(): pl.pallas_call(combine_kernel, out_shape=(out, out, out), in_specs=[vmem,...  0.58 us
  transfers between devices with their start and end apart: 4, of which 2 were waited for; matrix products, arithmetic and copies ran while one was open for 0% of the time, Pallas kernels for 34%

profile of v6, /device:TPU:0, one launch (start us, length us, event | category | flops | bytes accessed | tf_op | source)
XLA Modules:
  0.0 28.8 jit_solution(12995202361985270252)
XLA Ops:
  0.6 1.3 %collective-permute-start = (bf16[512,512]{1,0:T(8,128)(2,1)}, bf16[512,512]{1,0:T(8,128)(2,1)S(1)}, u32[]{:S(2)}, u32[]{:S(2)}) collective-permute-start(bf16[512,512]{1,0:T(8,128)(2,1)} %bitcast.1.tile_ref), channel_id=1, source_target_pairs={{1,0},{2,1},{3,2},{4,3},{5,4},{6,5},{7,6},{8,7},{9,8},{10,9},{11,1... | collective-permute-start | bytes 1572872 | tf_op jit(solution)/shard_map/ppermute | solution.py:349
  1.9 1.3 %collective-permute-start.1 = (bf16[512,512]{1,0:T(8,128)(2,1)}, bf16[512,512]{1,0:T(8,128)(2,1)S(1)}, u32[]{:S(2)}, u32[]{:S(2)}) collective-permute-start(bf16[512,512]{1,0:T(8,128)(2,1)} %bitcast.1.tile_ref), channel_id=1, source_target_pairs={{2,0},{4,2},{6,4},{8,6},{10,8},{12,10},{14,12},{18,16},{20,18},{22... | collective-permute-start | bytes 1572872 | tf_op jit(solution)/shard_map/ppermute | solution.py:349
  3.2 0.0 copy-start
  3.2 0.0 copy-start.1
  3.3 0.0 copy-start.2
  3.3 0.0 copy-start.3
  3.3 0.0 copy-start.4
  3.3 0.0 copy-start.5
  3.3 0.0 copy-start.6
  3.3 0.0 copy-start.7
  3.3 0.0 copy-start.8
  3.3 0.0 copy-start.9
  3.3 3.4 %own_spectrum.1 = (bf16[16,128,256]{2,1,0:T(8,128)(2,1)S(1)}, bf16[16,256,256]{2,1,0:T(8,128)(2,1)S(1)}) custom-call(s32[2,32]{1,0:T(2,128)} %bitcast.2, bf16[512,512]{1,0:T(8,128)(2,1)} %bitcast.1.tile_ref, f32[768,128]{1,0:T(8,128)} %constant.14.clone.tables_ref.refs_3_), custom_call_target="tpu_custom_call" | custom-call | flops 4000000000 | bytes 3145728 | tf_op jit(solution)/shard_map/own_spectrum/pallas_call | solution.py:369
  6.7 0.7 %collective-permute-start.2 = (bf16[512,512]{1,0:T(8,128)(2,1)}, bf16[512,512]{1,0:T(8,128)(2,1)S(1)}, u32[]{:S(2)}, u32[]{:S(2)}) collective-permute-start(bf16[512,512]{1,0:T(8,128)(2,1)} %bitcast.1.tile_ref), channel_id=1, source_target_pairs={{3,1},{5,3},{7,5},{9,7},{11,9},{13,11},{15,13},{19,17},{21,19},{23... | collective-permute-start | bytes 1572872 | tf_op jit(solution)/shard_map/ppermute | solution.py:349
  7.4 0.0 collective-permute-done.refs_10_
  7.5 0.0 copy-done
  7.5 0.0 copy-done.1
  7.5 0.0 copy-done.2
  7.5 0.0 copy-done.3
  7.5 0.0 copy-done.4
  7.5 0.0 copy-done.5
  7.5 0.0 copy-done.6
  7.5 0.0 copy-done.7
  7.5 0.0 copy-done.8
  7.5 0.0 copy-done.9
  7.6 3.4 %shard_map.130 = f32[16,3,32]{2,1,0:T(4,128)} custom-call(s32[2,32]{1,0:T(2,128)S(1)} %bitcast.3, bf16[16,128,256]{2,1,0:T(8,128)(2,1)S(1)} %get-tuple-element.8.refs_1_, s32[3,32]{1,0:T(4,128)S(1)} %copy-done, f32[768,128]{1,0:T(8,128)S(1)} %copy-done.4, bf16[256,256]{1,0:T(8,128)(2,1)S(1)} %copy-done.5, bf16[256,128]{1,0:T(8,128)(2,1)S(1)} %copy-done.6, ...), custom_call_target="tpu_custom_call" | custom-call | flops 8000000000 | bytes 4194304 | tf_op jit(solution)/shard_map/pallas_call | solution.py:389
  10.9 10.6 %all-to-all-start = ((f32[16,3,32]{2,1,0:T(4,128)}), f32[16,3,32]{2,1,0:T(4,128)S(1)}, u32[]{:S(2)}, u32[]{:S(2)}) async-start(f32[16,3,32]{2,1,0:T(4,128)} %shard_map.130), calls=%async_computation | async-start | bytes 65536 | tf_op jit(solution)/shard_map/all_to_all | solution.py:410
  21.6 2.2 %collective-permute-done.1.refs_10_ = bf16[512,512]{1,0:T(8,128)(2,1)S(1)} collective-permute-done((bf16[512,512]{1,0:T(8,128)(2,1)}, bf16[512,512]{1,0:T(8,128)(2,1)S(1)}, u32[]{:S(2)}, u32[]{:S(2)}) %collective-permute-start.1) | collective-permute-done | bytes 524320 | tf_op jit(solution)/shard_map/ppermute | solution.py:349
  23.8 0.0 collective-permute-done.2.refs_11_
  23.8 3.0 %shard_map.131.skip_ref = f32[2,32]{1,0:T(2,128)S(1)} custom-call(s32[2,32]{1,0:T(2,128)S(1)} %bitcast.4, bf16[16,128,256]{2,1,0:T(8,128)(2,1)S(1)} %get-tuple-element.8.refs_1_, s32[3,32]{1,0:T(4,128)S(1)} %copy-done, f32[768,128]{1,0:T(8,128)S(1)} %copy-done.4, bf16[256,256]{1,0:T(8,128)(2,1)S(1)} %copy-done.5, bf16[256,128]{1,0:T(8,128)(2,1)S(1)} %copy-done.6, ...), custom_call_target="tpu_custom_call" | custom-call | flops 8000000000 | bytes 4194304 | tf_op jit(solution)/shard_map/pallas_call | solution.py:389
  26.8 1.4 %all-to-all-done.shared_ref = f32[16,3,32]{2,1,0:T(4,128)S(1)} async-done(((f32[16,3,32]{2,1,0:T(4,128)}), f32[16,3,32]{2,1,0:T(4,128)S(1)}, u32[]{:S(2)}, u32[]{:S(2)}) %all-to-all-start) | async-done | bytes 6176 | tf_op jit(solution)/shard_map/all_to_all | solution.py:410
  28.2 0.6 %combine.1 = (f32[1,2,32]{2,1,0:T(2,128)}, f32[1,2,32]{2,1,0:T(2,128)}, f32[1,2,32]{2,1,0:T(2,128)}) custom-call(f32[16,3,32]{2,1,0:T(4,128)S(1)} %all-to-all-done.shared_ref, f32[2,32]{1,0:T(2,128)S(1)} %shard_map.131.skip_ref), custom_call_target="tpu_custom_call" | custom-call | tf_op jit(solution)/shard_map/combine/pallas_call | solution.py:413
Async XLA Ops:
  0.6 6.8 %collective-permute-start = (bf16[512,512]{1,0:T(8,128)(2,1)}, bf16[512,512]{1,0:T(8,128)(2,1)S(1)}, u32[]{:S(2)}, u32[]{:S(2)}) collective-permute-start(bf16[512,512]{1,0:T(8,128)(2,1)} %bitcast.1.tile_ref), channel_id=1, source_target_pairs={{1,0},{2,1},{3,2},{4,3},{5,4},{6,5},{7,6},{8,7},{9,8},{10,9},{11,1... | collective-permute-start | bytes 1572872 | tf_op jit(solution)/shard_map/ppermute | solution.py:349
  1.9 21.9 %collective-permute-start.1 = (bf16[512,512]{1,0:T(8,128)(2,1)}, bf16[512,512]{1,0:T(8,128)(2,1)S(1)}, u32[]{:S(2)}, u32[]{:S(2)}) collective-permute-start(bf16[512,512]{1,0:T(8,128)(2,1)} %bitcast.1.tile_ref), channel_id=1, source_target_pairs={{2,0},{4,2},{6,4},{8,6},{10,8},{12,10},{14,12},{18,16},{20,18},{22... | collective-permute-start | bytes 1572872 | tf_op jit(solution)/shard_map/ppermute | solution.py:349
  3.2 4.2 %copy-start = (s32[3,32]{1,0:T(4,128)S(1)}, s32[3,32]{1,0:T(4,128)}, u32[]{:S(2)}) copy-start(s32[3,32]{1,0:T(4,128)} %refs_2_.3) | copy-start | bytes 1156
  3.2 4.2 %copy-start.1 = (s32[32,2]{0,1:T(2,128)S(1)}, s32[32,2]{0,1:T(2,128)}, u32[]{:S(2)}) copy-start(s32[32,2]{0,1:T(2,128)} %param.12) | copy-start | bytes 772
  3.3 4.2 %copy-start.2 = (s32[1,32]{1,0:T(1,128)S(1)}, s32[1,32]{1,0:T(1,128)}, u32[]{:S(2)}) copy-start(s32[1,32]{1,0:T(1,128)} %refs_12_.1) | copy-start | bytes 388
  3.3 4.2 %copy-start.3 = (bf16[5,256,256]{2,1,0:T(8,128)(2,1)S(1)}, bf16[5,256,256]{2,1,0:T(8,128)(2,1)}, u32[]{:S(2)}) copy-start(bf16[5,256,256]{2,1,0:T(8,128)(2,1)} %constant.18.clone.refs_7_) | copy-start | bytes 1966084
  3.3 4.2 %copy-start.4 = (f32[768,128]{1,0:T(8,128)S(1)}, f32[768,128]{1,0:T(8,128)}, u32[]{:S(2)}) copy-start(f32[768,128]{1,0:T(8,128)} %constant.14.clone.tables_ref.refs_3_) | copy-start | bytes 1179652
  3.3 4.2 %copy-start.5 = (bf16[256,256]{1,0:T(8,128)(2,1)S(1)}, bf16[256,256]{1,0:T(8,128)(2,1)}, u32[]{:S(2)}) copy-start(bf16[256,256]{1,0:T(8,128)(2,1)} %constant.15.clone.refs_4_) | copy-start | bytes 393220
  3.3 4.2 %copy-start.6 = (bf16[256,128]{1,0:T(8,128)(2,1)S(1)}, bf16[256,128]{1,0:T(8,128)(2,1)}, u32[]{:S(2)}) copy-start(bf16[256,128]{1,0:T(8,128)(2,1)} %constant.16.clone.refs_5_) | copy-start | bytes 196612
  3.3 4.2 %copy-start.7 = (bf16[128,64]{1,0:T(8,128)(2,1)S(1)}, bf16[128,64]{1,0:T(8,128)(2,1)}, u32[]{:S(2)}) copy-start(bf16[128,64]{1,0:T(8,128)(2,1)} %constant.17.clone.refs_6_) | copy-start | bytes 49156
  3.3 4.2 %copy-start.8 = (f32[64,128]{1,0:T(8,128)S(1)}, f32[64,128]{1,0:T(8,128)}, u32[]{:S(2)}) copy-start(f32[64,128]{1,0:T(8,128)} %constant.20.clone.refs_9_) | copy-start | bytes 98308
  3.3 4.2 %copy-start.9 = (f32[2,8,128]{2,1,0:T(8,128)S(1)}, f32[2,8,128]{2,1,0:T(8,128)}, u32[]{:S(2)}) copy-start(f32[2,8,128]{2,1,0:T(8,128)} %constant.19.clone.refs_8_) | copy-start | bytes 24580
  6.7 17.1 %collective-permute-start.2 = (bf16[512,512]{1,0:T(8,128)(2,1)}, bf16[512,512]{1,0:T(8,128)(2,1)S(1)}, u32[]{:S(2)}, u32[]{:S(2)}) collective-permute-start(bf16[512,512]{1,0:T(8,128)(2,1)} %bitcast.1.tile_ref), channel_id=1, source_target_pairs={{3,1},{5,3},{7,5},{9,7},{11,9},{13,11},{15,13},{19,17},{21,19},{23... | collective-permute-start | bytes 1572872 | tf_op jit(solution)/shard_map/ppermute | solution.py:349
  10.9 17.3 %all-to-all-start = ((f32[16,3,32]{2,1,0:T(4,128)}), f32[16,3,32]{2,1,0:T(4,128)S(1)}, u32[]{:S(2)}, u32[]{:S(2)}) async-start(f32[16,3,32]{2,1,0:T(4,128)} %shard_map.130), calls=%async_computation | async-start | bytes 65536 | tf_op jit(solution)/shard_map/all_to_all | solution.py:410

commit v7 on v6

--- a/solution.py
+++ b/solution.py
@@ -92,10 +92,8 @@
         panels[panel] = tile_ref[:, panel * PATCH : (panel + 1) * PATCH].astype(jnp.float32)
 
 
-def transform_of(forward_ref):
-    first = forward_ref.shape[0] - 2 * PATCH
-    parts = [forward_ref[first + turn * PATCH : first + (turn + 1) * PATCH] for turn in range(2)]
-    return jnp.concatenate(parts, axis=1).astype(jnp.bfloat16)
+def stacked_of(forward_ref):
+    return forward_ref[forward_ref.shape[0] - 2 * PATCH :].astype(jnp.bfloat16)
 
 
 class Direct:
@@ -117,7 +115,8 @@
             for order in (member, 1 - member)
         ]
         table.append(jnp.concatenate(parts, axis=1).astype(jnp.bfloat16))
-    return jnp.concatenate(table, axis=0)
+    table = jnp.concatenate(table, axis=0)
+    return table, crossed(table)
 
 
 def turned_patches(pair, place_ref, panels):
@@ -138,17 +137,12 @@
     return jnp.concatenate([-parts[:, PATCH:], parts[:, :PATCH]], axis=1)
 
 
-def spectrum_by_columns(patches, table, forward):
-    cols = product(patches, table).astype(jnp.bfloat16)
-    return product(forward, jnp.concatenate([cols, crossed(cols)], axis=0)).astype(jnp.bfloat16)
-
-
-def spectrum_by_rows(patches, table, stacked):
+def spectrum_of(patches, table, stacked):
     rows = product(stacked, patches).astype(jnp.bfloat16)
-    return (product(rows[:PATCH], table) + product(rows[PATCH:], crossed(table))).astype(jnp.bfloat16)
-
-
-def own_kernel(corners_ref, tile_ref, tables_ref, spec_ref, table_ref, held, panels, forward_ref, corners, sems):
+    return (product(rows[:PATCH], table[0]) + product(rows[PATCH:], table[1])).astype(jnp.bfloat16)
+
+
+def own_kernel(corners_ref, tile_ref, tables_ref, spec_ref, wide_ref, table_ref, held, panels, forward_ref, corners, sems):
     copies = [
         pltpu.make_async_copy(source, target, sems.at[turn])
         for turn, (source, target) in enumerate(((tile_ref, held), (tables_ref, forward_ref), (corners_ref, corners)))
@@ -158,12 +152,15 @@
     for copy in copies:
         copy.wait()
     place_ref = Direct(corners)
-    stacked = forward_ref[forward_ref.shape[0] - 2 * PATCH :].astype(jnp.bfloat16)
+    stacked = stacked_of(forward_ref)
     fill_panels(held, panels)
     for pair in range(spec_ref.shape[0]):
         table = pair_table(pair, place_ref, forward_ref)
-        table_ref[pair] = table
-        spec_ref[pair] = spectrum_by_rows(turned_patches(pair, place_ref, panels), table, stacked)
+        for turn, part in enumerate(table):
+            table_ref[turn, pair] = part
+        spec = spectrum_of(turned_patches(pair, place_ref, panels), table, stacked)
+        spec_ref[pair] = spec
+        wide_ref[pair] = spec.astype(jnp.float32)
 
 
 def estimate(
@@ -189,12 +186,15 @@
         return jnp.where((lane & (2 * width - 1)) < width, even, pltpu.roll(odd, width, 1))
 
     def cross_stage(group, slot):
-        forward = transform_of(forward_ref)
+        stacked = stacked_of(forward_ref)
         inner = []
         for pair in range(PAIRS):
             place = group * PAIRS + pair
-            table = pair_table(place, place_ref, forward_ref) if table_ref is None else table_ref[place]
-            other = spectrum_by_columns(turned_patches(place, place_ref, panels), table, forward).astype(jnp.float32)
+            if table_ref is None:
+                table = pair_table(place, place_ref, forward_ref)
+            else:
+                table = table_ref[0, place], table_ref[1, place]
+            other = spectrum_of(turned_patches(place, place_ref, panels), table, stacked).astype(jnp.float32)
             own = spec_ref[place].astype(jnp.float32)
             own_real, own_imag = own[:, :PATCH], own[:, PATCH:]
             other_real, other_imag = other[:, :PATCH], other[:, PATCH:]
@@ -366,11 +366,15 @@
 
     next_tile = moved(tile, "sec", 1)
     even_tile = moved(tile, "sec", 2, (0,))
-    own_spec, col_tables = pl.pallas_call(
+    own_spec, wide_spec, col_tables = pl.pallas_call(
         own_kernel,
-        out_shape=(spec, jax.ShapeDtypeStruct((patches // 2, 2 * PATCH, 2 * PATCH), jnp.bfloat16)),
+        out_shape=(
+            spec,
+            jax.ShapeDtypeStruct(spec.shape, jnp.float32),
+            jax.ShapeDtypeStruct((2, patches // 2, 2 * PATCH, 2 * PATCH), jnp.bfloat16),
+        ),
         in_specs=[pl.BlockSpec(memory_space=pltpu.HBM)] * 3,
-        out_specs=(vmem, vmem),
+        out_specs=(vmem, vmem, vmem),
         scratch_shapes=[
             pltpu.VMEM(tile.shape, tile.dtype),
             pltpu.VMEM(panels, jnp.float32),
@@ -385,7 +389,7 @@
     later_tile, own_spec = lax.optimization_barrier((tile, own_spec))
     odd_tile = moved(later_tile, "sec", 2, (1,))
 
-    def flow(kernel, out_shape, *more):
+    def flow(kernel, out_shape, own, *more):
         return pl.pallas_call(
             kernel,
             out_shape=jax.ShapeDtypeStruct(out_shape, jnp.float32),
@@ -404,11 +408,11 @@
             ],
             compiler_params=limit(12),
             cost_estimate=pl.CostEstimate(flops=8 * 10**9, bytes_accessed=4 * 2**20, transcendentals=0),
-        )(corners, own_spec, level_use, forward, *rest, *more)
-
-    message = flow(next_kernel, (sections, 3, patches), next_tile, col_tables, tissue_mask)
+        )(corners, own, level_use, forward, *rest, *more)
+
+    message = flow(next_kernel, (sections, 3, patches), wide_spec, next_tile, col_tables, tissue_mask)
     shared = lax.all_to_all(message, "sec", 0, 0)
-    flow_skip = flow(skip_kernel, (2, patches), even_tile, odd_tile)
+    flow_skip = flow(skip_kernel, (2, patches), own_spec, even_tile, odd_tile)
     out = jax.ShapeDtypeStruct((1, 2, patches), jnp.float32)
     return pl.pallas_call(
         combine_kernel,

time: 29 us -> 29.6 us (1.021)
  Pallas kernels: 10.4 us -> 11.5 us
  waiting for transfers between devices: 3.6 us -> 3 us
    pallas_call x2, Pallas kernels: 6.42 us -> 7.61 us  [flow(): pl.pallas_call(kernel, out_shape=jax.ShapeDtypeStruct(out_shape, jnp.floa...]
    ppermute x3, waiting for transfers between devices: 2.25 us -> 1.73 us  [moved(): return lax.ppermute(block, axis, route)]
  transfers between devices with their start and end apart: 4 -> 4, of which waited for: 2 -> 2; matrix products, arithmetic and copies ran while one was open for 0% -> 0% of each run, Pallas kernels for 34% -> 37%
where the time goes in v7:
time: 29.6 us; the launch traced here: 29.4 us
  starting transfers between devices  14 us (47%)
  Pallas kernels  11.5 us (39%)
  waiting for transfers between devices  3 us (10%)
  between operations  0.84 us (3%)
    all_to_all x1, starting transfers between devices, on_device(): shared = lax.all_to_all(message, 'sec', 0, 0)  10.7 us
    pallas_call x2, Pallas kernels, flow(): pl.pallas_call(kernel, out_shape=jax.ShapeDtypeStruct(out_shape, jnp.floa...  7.61 us
    pallas_call x1, Pallas kernels, on_device(): pl.pallas_call(own_kernel, out_shape=(spec, jax.ShapeDtypeStruct(spec.sha...  3.31 us
    ppermute x3, starting transfers between devices, moved(): return lax.ppermute(block, axis, route)  3.28 us
    ppermute x3, waiting for transfers between devices, moved(): return lax.ppermute(block, axis, route)  1.73 us
    all_to_all x1, waiting for transfers between devices, on_device(): shared = lax.all_to_all(message, 'sec', 0, 0)  1.26 us
  transfers between devices with their start and end apart: 4, of which 2 were waited for; matrix products, arithmetic and copies ran while one was open for 0% of the time, Pallas kernels for 37%

profile of v7, /device:TPU:0, one launch (start us, length us, event | category | flops | bytes accessed | tf_op | source)
XLA Modules:
  0.0 29.4 jit_solution(5116321463310220054)
XLA Ops:
  0.6 1.3 %collective-permute-start = (bf16[512,512]{1,0:T(8,128)(2,1)}, bf16[512,512]{1,0:T(8,128)(2,1)S(1)}, u32[]{:S(2)}, u32[]{:S(2)}) collective-permute-start(bf16[512,512]{1,0:T(8,128)(2,1)} %bitcast.1.tile_ref), channel_id=1, source_target_pairs={{1,0},{2,1},{3,2},{4,3},{5,4},{6,5},{7,6},{8,7},{9,8},{10,9},{11,1... | collective-permute-start | bytes 1572872 | tf_op jit(solution)/shard_map/ppermute | solution.py:349
  1.9 1.3 %collective-permute-start.1 = (bf16[512,512]{1,0:T(8,128)(2,1)}, bf16[512,512]{1,0:T(8,128)(2,1)S(1)}, u32[]{:S(2)}, u32[]{:S(2)}) collective-permute-start(bf16[512,512]{1,0:T(8,128)(2,1)} %bitcast.1.tile_ref), channel_id=1, source_target_pairs={{2,0},{4,2},{6,4},{8,6},{10,8},{12,10},{14,12},{18,16},{20,18},{22... | collective-permute-start | bytes 1572872 | tf_op jit(solution)/shard_map/ppermute | solution.py:349
  3.2 0.0 copy-start
  3.2 0.0 copy-start.1
  3.3 0.0 copy-start.2
  3.3 0.0 copy-start.3
  3.3 0.0 copy-start.4
  3.3 0.0 copy-start.5
  3.3 0.0 copy-start.6
  3.3 0.0 copy-start.7
  3.3 0.0 copy-start.8
  3.3 0.0 copy-start.9
  3.3 3.3 %own_spectrum.1 = (bf16[16,128,256]{2,1,0:T(8,128)(2,1)S(1)}, f32[16,128,256]{2,1,0:T(8,128)S(1)}, bf16[2,16,256,256]{3,2,1,0:T(8,128)(2,1)S(1)}) custom-call(s32[2,32]{1,0:T(2,128)} %bitcast.2, bf16[512,512]{1,0:T(8,128)(2,1)} %bitcast.1.tile_ref, f32[768,128]{1,0:T(8,128)} %constant.14.clone.tables_ref.refs_3_), custom_call_target="tpu_custom_call" | custom-call | flops 4000000000 | bytes 3145728 | tf_op jit(solution)/shard_map/own_spectrum/pallas_call | solution.py:369
  6.7 0.7 %collective-permute-start.2 = (bf16[512,512]{1,0:T(8,128)(2,1)}, bf16[512,512]{1,0:T(8,128)(2,1)S(1)}, u32[]{:S(2)}, u32[]{:S(2)}) collective-permute-start(bf16[512,512]{1,0:T(8,128)(2,1)} %bitcast.1.tile_ref), channel_id=1, source_target_pairs={{3,1},{5,3},{7,5},{9,7},{11,9},{13,11},{15,13},{19,17},{21,19},{23... | collective-permute-start | bytes 1572872 | tf_op jit(solution)/shard_map/ppermute | solution.py:349
  7.4 0.0 collective-permute-done.refs_10_
  7.4 0.0 copy-done
  7.4 0.0 copy-done.1
  7.4 0.0 copy-done.2
  7.4 0.0 copy-done.3
  7.4 0.0 copy-done.4
  7.4 0.0 copy-done.5
  7.4 0.0 copy-done.6
  7.5 0.0 copy-done.7
  7.5 0.0 copy-done.8
  7.5 0.0 copy-done.9
  7.5 4.0 %shard_map.130 = f32[16,3,32]{2,1,0:T(4,128)} custom-call(s32[2,32]{1,0:T(2,128)S(1)} %bitcast.3, f32[16,128,256]{2,1,0:T(8,128)S(1)} %get-tuple-element.8.refs_1_, s32[3,32]{1,0:T(4,128)S(1)} %copy-done, f32[768,128]{1,0:T(8,128)S(1)} %copy-done.4, bf16[256,256]{1,0:T(8,128)(2,1)S(1)} %copy-done.5, bf16[256,128]{1,0:T(8,128)(2,1)S(1)} %copy-done.6, ...), custom_call_target="tpu_custom_call" | custom-call | flops 8000000000 | bytes 4194304 | tf_op jit(solution)/shard_map/pallas_call | solution.py:393
  11.5 10.7 %all-to-all-start = ((f32[16,3,32]{2,1,0:T(4,128)}), f32[16,3,32]{2,1,0:T(4,128)S(1)}, u32[]{:S(2)}, u32[]{:S(2)}) async-start(f32[16,3,32]{2,1,0:T(4,128)} %shard_map.130), calls=%async_computation | async-start | bytes 65536 | tf_op jit(solution)/shard_map/all_to_all | solution.py:414
  22.1 1.7 %collective-permute-done.1.refs_10_ = bf16[512,512]{1,0:T(8,128)(2,1)S(1)} collective-permute-done((bf16[512,512]{1,0:T(8,128)(2,1)}, bf16[512,512]{1,0:T(8,128)(2,1)S(1)}, u32[]{:S(2)}, u32[]{:S(2)}) %collective-permute-start.1) | collective-permute-done | bytes 524320 | tf_op jit(solution)/shard_map/ppermute | solution.py:349
  23.9 0.0 collective-permute-done.2.refs_11_
  23.9 3.6 %shard_map.131.skip_ref = f32[2,32]{1,0:T(2,128)S(1)} custom-call(s32[2,32]{1,0:T(2,128)S(1)} %bitcast.4, bf16[16,128,256]{2,1,0:T(8,128)(2,1)S(1)} %get-tuple-element.11.refs_1_, s32[3,32]{1,0:T(4,128)S(1)} %copy-done, f32[768,128]{1,0:T(8,128)S(1)} %copy-done.4, bf16[256,256]{1,0:T(8,128)(2,1)S(1)} %copy-done.5, bf16[256,128]{1,0:T(8,128)(2,1)S(1)} %copy-done.6, ...), custom_call_target="tpu_custom_call" | custom-call | flops 8000000000 | bytes 4194304 | tf_op jit(solution)/shard_map/pallas_call | solution.py:393
  27.5 1.3 %all-to-all-done.shared_ref = f32[16,3,32]{2,1,0:T(4,128)S(1)} async-done(((f32[16,3,32]{2,1,0:T(4,128)}), f32[16,3,32]{2,1,0:T(4,128)S(1)}, u32[]{:S(2)}, u32[]{:S(2)}) %all-to-all-start) | async-done | bytes 6176 | tf_op jit(solution)/shard_map/all_to_all | solution.py:414
  28.8 0.6 %combine.1 = (f32[1,2,32]{2,1,0:T(2,128)}, f32[1,2,32]{2,1,0:T(2,128)}, f32[1,2,32]{2,1,0:T(2,128)}) custom-call(f32[16,3,32]{2,1,0:T(4,128)S(1)} %all-to-all-done.shared_ref, f32[2,32]{1,0:T(2,128)S(1)} %shard_map.131.skip_ref), custom_call_target="tpu_custom_call" | custom-call | tf_op jit(solution)/shard_map/combine/pallas_call | solution.py:417
Async XLA Ops:
  0.6 6.7 %collective-permute-start = (bf16[512,512]{1,0:T(8,128)(2,1)}, bf16[512,512]{1,0:T(8,128)(2,1)S(1)}, u32[]{:S(2)}, u32[]{:S(2)}) collective-permute-start(bf16[512,512]{1,0:T(8,128)(2,1)} %bitcast.1.tile_ref), channel_id=1, source_target_pairs={{1,0},{2,1},{3,2},{4,3},{5,4},{6,5},{7,6},{8,7},{9,8},{10,9},{11,1... | collective-permute-start | bytes 1572872 | tf_op jit(solution)/shard_map/ppermute | solution.py:349
  1.9 21.9 %collective-permute-start.1 = (bf16[512,512]{1,0:T(8,128)(2,1)}, bf16[512,512]{1,0:T(8,128)(2,1)S(1)}, u32[]{:S(2)}, u32[]{:S(2)}) collective-permute-start(bf16[512,512]{1,0:T(8,128)(2,1)} %bitcast.1.tile_ref), channel_id=1, source_target_pairs={{2,0},{4,2},{6,4},{8,6},{10,8},{12,10},{14,12},{18,16},{20,18},{22... | collective-permute-start | bytes 1572872 | tf_op jit(solution)/shard_map/ppermute | solution.py:349
  3.2 4.2 %copy-start = (s32[3,32]{1,0:T(4,128)S(1)}, s32[3,32]{1,0:T(4,128)}, u32[]{:S(2)}) copy-start(s32[3,32]{1,0:T(4,128)} %refs_2_.3) | copy-start | bytes 1156
  3.2 4.2 %copy-start.1 = (s32[32,2]{0,1:T(2,128)S(1)}, s32[32,2]{0,1:T(2,128)}, u32[]{:S(2)}) copy-start(s32[32,2]{0,1:T(2,128)} %param.12) | copy-start | bytes 772
  3.3 4.2 %copy-start.2 = (s32[1,32]{1,0:T(1,128)S(1)}, s32[1,32]{1,0:T(1,128)}, u32[]{:S(2)}) copy-start(s32[1,32]{1,0:T(1,128)} %refs_12_.1) | copy-start | bytes 388
  3.3 4.2 %copy-start.3 = (bf16[5,256,256]{2,1,0:T(8,128)(2,1)S(1)}, bf16[5,256,256]{2,1,0:T(8,128)(2,1)}, u32[]{:S(2)}) copy-start(bf16[5,256,256]{2,1,0:T(8,128)(2,1)} %constant.18.clone.refs_7_) | copy-start | bytes 1966084
  3.3 4.1 %copy-start.4 = (f32[768,128]{1,0:T(8,128)S(1)}, f32[768,128]{1,0:T(8,128)}, u32[]{:S(2)}) copy-start(f32[768,128]{1,0:T(8,128)} %constant.14.clone.tables_ref.refs_3_) | copy-start | bytes 1179652
  3.3 4.1 %copy-start.5 = (bf16[256,256]{1,0:T(8,128)(2,1)S(1)}, bf16[256,256]{1,0:T(8,128)(2,1)}, u32[]{:S(2)}) copy-start(bf16[256,256]{1,0:T(8,128)(2,1)} %constant.15.clone.refs_4_) | copy-start | bytes 393220
  3.3 4.1 %copy-start.6 = (bf16[256,128]{1,0:T(8,128)(2,1)S(1)}, bf16[256,128]{1,0:T(8,128)(2,1)}, u32[]{:S(2)}) copy-start(bf16[256,128]{1,0:T(8,128)(2,1)} %constant.16.clone.refs_5_) | copy-start | bytes 196612
  3.3 4.1 %copy-start.7 = (bf16[128,64]{1,0:T(8,128)(2,1)S(1)}, bf16[128,64]{1,0:T(8,128)(2,1)}, u32[]{:S(2)}) copy-start(bf16[128,64]{1,0:T(8,128)(2,1)} %constant.17.clone.refs_6_) | copy-start | bytes 49156
  3.3 4.1 %copy-start.8 = (f32[64,128]{1,0:T(8,128)S(1)}, f32[64,128]{1,0:T(8,128)}, u32[]{:S(2)}) copy-start(f32[64,128]{1,0:T(8,128)} %constant.20.clone.refs_9_) | copy-start | bytes 98308
  3.3 4.1 %copy-start.9 = (f32[2,8,128]{2,1,0:T(8,128)S(1)}, f32[2,8,128]{2,1,0:T(8,128)}, u32[]{:S(2)}) copy-start(f32[2,8,128]{2,1,0:T(8,128)} %constant.19.clone.refs_8_) | copy-start | bytes 24580
  6.7 17.2 %collective-permute-start.2 = (bf16[512,512]{1,0:T(8,128)(2,1)}, bf16[512,512]{1,0:T(8,128)(2,1)S(1)}, u32[]{:S(2)}, u32[]{:S(2)}) collective-permute-start(bf16[512,512]{1,0:T(8,128)(2,1)} %bitcast.1.tile_ref), channel_id=1, source_target_pairs={{3,1},{5,3},{7,5},{9,7},{11,9},{13,11},{15,13},{19,17},{21,19},{23... | collective-permute-start | bytes 1572872 | tf_op jit(solution)/shard_map/ppermute | solution.py:349
  11.5 17.3 %all-to-all-start = ((f32[16,3,32]{2,1,0:T(4,128)}), f32[16,3,32]{2,1,0:T(4,128)S(1)}, u32[]{:S(2)}, u32[]{:S(2)}) async-start(f32[16,3,32]{2,1,0:T(4,128)} %shard_map.130), calls=%async_computation | async-start | bytes 65536 | tf_op jit(solution)/shard_map/all_to_all | solution.py:414

commit v8 on v7

--- a/solution.py
+++ b/solution.py
@@ -139,7 +139,7 @@
 
 def spectrum_of(patches, table, stacked):
     rows = product(stacked, patches).astype(jnp.bfloat16)
-    return (product(rows[:PATCH], table[0]) + product(rows[PATCH:], table[1])).astype(jnp.bfloat16)
+    return (product(rows[:PATCH], table[0]) + product(rows[PATCH:], table[1]))
 
 
 def own_kernel(corners_ref, tile_ref, tables_ref, spec_ref, wide_ref, table_ref, held, panels, forward_ref, corners, sems):
@@ -158,7 +158,7 @@
         table = pair_table(pair, place_ref, forward_ref)
         for turn, part in enumerate(table):
             table_ref[turn, pair] = part
-        spec = spectrum_of(turned_patches(pair, place_ref, panels), table, stacked)
+        spec = spectrum_of(turned_patches(pair, place_ref, panels), table, stacked).astype(jnp.bfloat16)
         spec_ref[pair] = spec
         wide_ref[pair] = spec.astype(jnp.float32)
 
@@ -194,7 +194,7 @@
                 table = pair_table(place, place_ref, forward_ref)
             else:
                 table = table_ref[0, place], table_ref[1, place]
-            other = spectrum_of(turned_patches(place, place_ref, panels), table, stacked).astype(jnp.float32)
+            other = spectrum_of(turned_patches(place, place_ref, panels), table, stacked)
             own = spec_ref[place].astype(jnp.float32)
             own_real, own_imag = own[:, :PATCH], own[:, PATCH:]
             other_real, other_imag = other[:, :PATCH], other[:, PATCH:]

time: 29.6 us -> 29.6 us (level)
  no operation moved by 1% of the time
where the time goes in v8:
time: 29.6 us; the launch traced here: 29.3 us
  starting transfers between devices  14 us (47%)
  Pallas kernels  11.4 us (39%)
  waiting for transfers between devices  3.07 us (10%)
  between operations  0.84 us (3%)
    all_to_all x1, starting transfers between devices, on_device(): shared = lax.all_to_all(message, 'sec', 0, 0)  10.7 us
    pallas_call x2, Pallas kernels, flow(): pl.pallas_call(kernel, out_shape=jax.ShapeDtypeStruct(out_shape, jnp.floa...  7.49 us
    pallas_call x1, Pallas kernels, on_device(): pl.pallas_call(own_kernel, out_shape=(spec, jax.ShapeDtypeStruct(spec.sha...  3.31 us
    ppermute x3, starting transfers between devices, moved(): return lax.ppermute(block, axis, route)  3.28 us
    ppermute x3, waiting for transfers between devices, moved(): return lax.ppermute(block, axis, route)  1.78 us
    all_to_all x1, waiting for transfers between devices, on_device(): shared = lax.all_to_all(message, 'sec', 0, 0)  1.29 us
  transfers between devices with their start and end apart: 4, of which 2 were waited for; matrix products, arithmetic and copies ran while one was open for 0% of the time, Pallas kernels for 37%

profile of v8, /device:TPU:0, one launch (start us, length us, event | category | flops | bytes accessed | tf_op | source)
XLA Modules:
  0.0 29.3 jit_solution(16633484765576061200)
XLA Ops:
  0.6 1.3 %collective-permute-start = (bf16[512,512]{1,0:T(8,128)(2,1)}, bf16[512,512]{1,0:T(8,128)(2,1)S(1)}, u32[]{:S(2)}, u32[]{:S(2)}) collective-permute-start(bf16[512,512]{1,0:T(8,128)(2,1)} %bitcast.1.tile_ref), channel_id=1, source_target_pairs={{1,0},{2,1},{3,2},{4,3},{5,4},{6,5},{7,6},{8,7},{9,8},{10,9},{11,1... | collective-permute-start | bytes 1572872 | tf_op jit(solution)/shard_map/ppermute | solution.py:349
  1.9 1.3 %collective-permute-start.1 = (bf16[512,512]{1,0:T(8,128)(2,1)}, bf16[512,512]{1,0:T(8,128)(2,1)S(1)}, u32[]{:S(2)}, u32[]{:S(2)}) collective-permute-start(bf16[512,512]{1,0:T(8,128)(2,1)} %bitcast.1.tile_ref), channel_id=1, source_target_pairs={{2,0},{4,2},{6,4},{8,6},{10,8},{12,10},{14,12},{18,16},{20,18},{22... | collective-permute-start | bytes 1572872 | tf_op jit(solution)/shard_map/ppermute | solution.py:349
  3.2 0.0 copy-start
  3.2 0.0 copy-start.1
  3.3 0.0 copy-start.2
  3.3 0.0 copy-start.3
  3.3 0.0 copy-start.4
  3.3 0.0 copy-start.5
  3.3 0.0 copy-start.6
  3.3 0.0 copy-start.7
  3.3 0.0 copy-start.8
  3.3 0.0 copy-start.9
  3.3 3.3 %own_spectrum.1 = (bf16[16,128,256]{2,1,0:T(8,128)(2,1)S(1)}, f32[16,128,256]{2,1,0:T(8,128)S(1)}, bf16[2,16,256,256]{3,2,1,0:T(8,128)(2,1)S(1)}) custom-call(s32[2,32]{1,0:T(2,128)} %bitcast.2, bf16[512,512]{1,0:T(8,128)(2,1)} %bitcast.1.tile_ref, f32[768,128]{1,0:T(8,128)} %constant.14.clone.tables_ref.refs_3_), custom_call_target="tpu_custom_call" | custom-call | flops 4000000000 | bytes 3145728 | tf_op jit(solution)/shard_map/own_spectrum/pallas_call | solution.py:369
  6.7 0.7 %collective-permute-start.2 = (bf16[512,512]{1,0:T(8,128)(2,1)}, bf16[512,512]{1,0:T(8,128)(2,1)S(1)}, u32[]{:S(2)}, u32[]{:S(2)}) collective-permute-start(bf16[512,512]{1,0:T(8,128)(2,1)} %bitcast.1.tile_ref), channel_id=1, source_target_pairs={{3,1},{5,3},{7,5},{9,7},{11,9},{13,11},{15,13},{19,17},{21,19},{23... | collective-permute-start | bytes 1572872 | tf_op jit(solution)/shard_map/ppermute | solution.py:349
  7.4 0.0 collective-permute-done.refs_10_
  7.4 0.0 copy-done
  7.4 0.0 copy-done.1
  7.4 0.0 copy-done.2
  7.4 0.0 copy-done.3
  7.4 0.0 copy-done.4
  7.4 0.0 copy-done.5
  7.4 0.0 copy-done.6
  7.5 0.0 copy-done.7
  7.5 0.0 copy-done.8
  7.5 0.0 copy-done.9
  7.5 3.9 %shard_map.130 = f32[16,3,32]{2,1,0:T(4,128)} custom-call(s32[2,32]{1,0:T(2,128)S(1)} %bitcast.3, f32[16,128,256]{2,1,0:T(8,128)S(1)} %get-tuple-element.8.refs_1_, s32[3,32]{1,0:T(4,128)S(1)} %copy-done, f32[768,128]{1,0:T(8,128)S(1)} %copy-done.4, bf16[256,256]{1,0:T(8,128)(2,1)S(1)} %copy-done.5, bf16[256,128]{1,0:T(8,128)(2,1)S(1)} %copy-done.6, ...), custom_call_target="tpu_custom_call" | custom-call | flops 8000000000 | bytes 4194304 | tf_op jit(solution)/shard_map/pallas_call | solution.py:393
  11.4 10.7 %all-to-all-start = ((f32[16,3,32]{2,1,0:T(4,128)}), f32[16,3,32]{2,1,0:T(4,128)S(1)}, u32[]{:S(2)}, u32[]{:S(2)}) async-start(f32[16,3,32]{2,1,0:T(4,128)} %shard_map.130), calls=%async_computation | async-start | bytes 65536 | tf_op jit(solution)/shard_map/all_to_all | solution.py:414
  22.1 1.8 %collective-permute-done.1.refs_10_ = bf16[512,512]{1,0:T(8,128)(2,1)S(1)} collective-permute-done((bf16[512,512]{1,0:T(8,128)(2,1)}, bf16[512,512]{1,0:T(8,128)(2,1)S(1)}, u32[]{:S(2)}, u32[]{:S(2)}) %collective-permute-start.1) | collective-permute-done | bytes 524320 | tf_op jit(solution)/shard_map/ppermute | solution.py:349
  23.9 0.0 collective-permute-done.2.refs_11_
  23.9 3.6 %shard_map.131.skip_ref = f32[2,32]{1,0:T(2,128)S(1)} custom-call(s32[2,32]{1,0:T(2,128)S(1)} %bitcast.4, bf16[16,128,256]{2,1,0:T(8,128)(2,1)S(1)} %get-tuple-element.11.refs_1_, s32[3,32]{1,0:T(4,128)S(1)} %copy-done, f32[768,128]{1,0:T(8,128)S(1)} %copy-done.4, bf16[256,256]{1,0:T(8,128)(2,1)S(1)} %copy-done.5, bf16[256,128]{1,0:T(8,128)(2,1)S(1)} %copy-done.6, ...), custom_call_target="tpu_custom_call" | custom-call | flops 8000000000 | bytes 4194304 | tf_op jit(solution)/shard_map/pallas_call | solution.py:393
  27.4 1.3 %all-to-all-done.shared_ref = f32[16,3,32]{2,1,0:T(4,128)S(1)} async-done(((f32[16,3,32]{2,1,0:T(4,128)}), f32[16,3,32]{2,1,0:T(4,128)S(1)}, u32[]{:S(2)}, u32[]{:S(2)}) %all-to-all-start) | async-done | bytes 6176 | tf_op jit(solution)/shard_map/all_to_all | solution.py:414
  28.7 0.6 %combine.1 = (f32[1,2,32]{2,1,0:T(2,128)}, f32[1,2,32]{2,1,0:T(2,128)}, f32[1,2,32]{2,1,0:T(2,128)}) custom-call(f32[16,3,32]{2,1,0:T(4,128)S(1)} %all-to-all-done.shared_ref, f32[2,32]{1,0:T(2,128)S(1)} %shard_map.131.skip_ref), custom_call_target="tpu_custom_call" | custom-call | tf_op jit(solution)/shard_map/combine/pallas_call | solution.py:417
Async XLA Ops:
  0.6 6.7 %collective-permute-start = (bf16[512,512]{1,0:T(8,128)(2,1)}, bf16[512,512]{1,0:T(8,128)(2,1)S(1)}, u32[]{:S(2)}, u32[]{:S(2)}) collective-permute-start(bf16[512,512]{1,0:T(8,128)(2,1)} %bitcast.1.tile_ref), channel_id=1, source_target_pairs={{1,0},{2,1},{3,2},{4,3},{5,4},{6,5},{7,6},{8,7},{9,8},{10,9},{11,1... | collective-permute-start | bytes 1572872 | tf_op jit(solution)/shard_map/ppermute | solution.py:349
  1.9 21.9 %collective-permute-start.1 = (bf16[512,512]{1,0:T(8,128)(2,1)}, bf16[512,512]{1,0:T(8,128)(2,1)S(1)}, u32[]{:S(2)}, u32[]{:S(2)}) collective-permute-start(bf16[512,512]{1,0:T(8,128)(2,1)} %bitcast.1.tile_ref), channel_id=1, source_target_pairs={{2,0},{4,2},{6,4},{8,6},{10,8},{12,10},{14,12},{18,16},{20,18},{22... | collective-permute-start | bytes 1572872 | tf_op jit(solution)/shard_map/ppermute | solution.py:349
  3.2 4.2 %copy-start = (s32[3,32]{1,0:T(4,128)S(1)}, s32[3,32]{1,0:T(4,128)}, u32[]{:S(2)}) copy-start(s32[3,32]{1,0:T(4,128)} %refs_2_.3) | copy-start | bytes 1156
  3.2 4.2 %copy-start.1 = (s32[32,2]{0,1:T(2,128)S(1)}, s32[32,2]{0,1:T(2,128)}, u32[]{:S(2)}) copy-start(s32[32,2]{0,1:T(2,128)} %param.12) | copy-start | bytes 772
  3.3 4.2 %copy-start.2 = (s32[1,32]{1,0:T(1,128)S(1)}, s32[1,32]{1,0:T(1,128)}, u32[]{:S(2)}) copy-start(s32[1,32]{1,0:T(1,128)} %refs_12_.1) | copy-start | bytes 388
  3.3 4.2 %copy-start.3 = (bf16[5,256,256]{2,1,0:T(8,128)(2,1)S(1)}, bf16[5,256,256]{2,1,0:T(8,128)(2,1)}, u32[]{:S(2)}) copy-start(bf16[5,256,256]{2,1,0:T(8,128)(2,1)} %constant.18.clone.refs_7_) | copy-start | bytes 1966084
  3.3 4.1 %copy-start.4 = (f32[768,128]{1,0:T(8,128)S(1)}, f32[768,128]{1,0:T(8,128)}, u32[]{:S(2)}) copy-start(f32[768,128]{1,0:T(8,128)} %constant.14.clone.tables_ref.refs_3_) | copy-start | bytes 1179652
  3.3 4.1 %copy-start.5 = (bf16[256,256]{1,0:T(8,128)(2,1)S(1)}, bf16[256,256]{1,0:T(8,128)(2,1)}, u32[]{:S(2)}) copy-start(bf16[256,256]{1,0:T(8,128)(2,1)} %constant.15.clone.refs_4_) | copy-start | bytes 393220
  3.3 4.1 %copy-start.6 = (bf16[256,128]{1,0:T(8,128)(2,1)S(1)}, bf16[256,128]{1,0:T(8,128)(2,1)}, u32[]{:S(2)}) copy-start(bf16[256,128]{1,0:T(8,128)(2,1)} %constant.16.clone.refs_5_) | copy-start | bytes 196612
  3.3 4.1 %copy-start.7 = (bf16[128,64]{1,0:T(8,128)(2,1)S(1)}, bf16[128,64]{1,0:T(8,128)(2,1)}, u32[]{:S(2)}) copy-start(bf16[128,64]{1,0:T(8,128)(2,1)} %constant.17.clone.refs_6_) | copy-start | bytes 49156
  3.3 4.1 %copy-start.8 = (f32[64,128]{1,0:T(8,128)S(1)}, f32[64,128]{1,0:T(8,128)}, u32[]{:S(2)}) copy-start(f32[64,128]{1,0:T(8,128)} %constant.20.clone.refs_9_) | copy-start | bytes 98308
  3.3 4.1 %copy-start.9 = (f32[2,8,128]{2,1,0:T(8,128)S(1)}, f32[2,8,128]{2,1,0:T(8,128)}, u32[]{:S(2)}) copy-start(f32[2,8,128]{2,1,0:T(8,128)} %constant.19.clone.refs_8_) | copy-start | bytes 24580
  6.7 17.2 %collective-permute-start.2 = (bf16[512,512]{1,0:T(8,128)(2,1)}, bf16[512,512]{1,0:T(8,128)(2,1)S(1)}, u32[]{:S(2)}, u32[]{:S(2)}) collective-permute-start(bf16[512,512]{1,0:T(8,128)(2,1)} %bitcast.1.tile_ref), channel_id=1, source_target_pairs={{3,1},{5,3},{7,5},{9,7},{11,9},{13,11},{15,13},{19,17},{21,19},{23... | collective-permute-start | bytes 1572872 | tf_op jit(solution)/shard_map/ppermute | solution.py:349
  11.4 17.3 %all-to-all-start = ((f32[16,3,32]{2,1,0:T(4,128)}), f32[16,3,32]{2,1,0:T(4,128)S(1)}, u32[]{:S(2)}, u32[]{:S(2)}) async-start(f32[16,3,32]{2,1,0:T(4,128)} %shard_map.130), calls=%async_computation | async-start | bytes 65536 | tf_op jit(solution)/shard_map/all_to_all | solution.py:414

commit v9 on v6

--- a/solution.py
+++ b/solution.py
@@ -148,7 +148,7 @@
     return (product(rows[:PATCH], table) + product(rows[PATCH:], crossed(table))).astype(jnp.bfloat16)
 
 
-def own_kernel(corners_ref, tile_ref, tables_ref, spec_ref, table_ref, held, panels, forward_ref, corners, sems):
+def own_kernel(corners_ref, tile_ref, tables_ref, spec_ref, wide_ref, table_ref, held, panels, forward_ref, corners, sems):
     copies = [
         pltpu.make_async_copy(source, target, sems.at[turn])
         for turn, (source, target) in enumerate(((tile_ref, held), (tables_ref, forward_ref), (corners_ref, corners)))
@@ -163,7 +163,9 @@
     for pair in range(spec_ref.shape[0]):
         table = pair_table(pair, place_ref, forward_ref)
         table_ref[pair] = table
-        spec_ref[pair] = spectrum_by_rows(turned_patches(pair, place_ref, panels), table, stacked)
+        spec = spectrum_by_rows(turned_patches(pair, place_ref, panels), table, stacked)
+        spec_ref[pair] = spec
+        wide_ref[pair] = spec.astype(jnp.float32)
 
 
 def estimate(
@@ -366,11 +368,15 @@
 
     next_tile = moved(tile, "sec", 1)
     even_tile = moved(tile, "sec", 2, (0,))
-    own_spec, col_tables = pl.pallas_call(
+    own_spec, wide_spec, col_tables = pl.pallas_call(
         own_kernel,
-        out_shape=(spec, jax.ShapeDtypeStruct((patches // 2, 2 * PATCH, 2 * PATCH), jnp.bfloat16)),
+        out_shape=(
+            spec,
+            jax.ShapeDtypeStruct(spec.shape, jnp.float32),
+            jax.ShapeDtypeStruct((patches // 2, 2 * PATCH, 2 * PATCH), jnp.bfloat16),
+        ),
         in_specs=[pl.BlockSpec(memory_space=pltpu.HBM)] * 3,
-        out_specs=(vmem, vmem),
+        out_specs=(vmem, vmem, vmem),
         scratch_shapes=[
             pltpu.VMEM(tile.shape, tile.dtype),
             pltpu.VMEM(panels, jnp.float32),
@@ -385,7 +391,7 @@
     later_tile, own_spec = lax.optimization_barrier((tile, own_spec))
     odd_tile = moved(later_tile, "sec", 2, (1,))
 
-    def flow(kernel, out_shape, *more):
+    def flow(kernel, out_shape, own, *more):
         return pl.pallas_call(
             kernel,
             out_shape=jax.ShapeDtypeStruct(out_shape, jnp.float32),
@@ -404,11 +410,11 @@
             ],
             compiler_params=limit(12),
             cost_estimate=pl.CostEstimate(flops=8 * 10**9, bytes_accessed=4 * 2**20, transcendentals=0),
-        )(corners, own_spec, level_use, forward, *rest, *more)
-
-    message = flow(next_kernel, (sections, 3, patches), next_tile, col_tables, tissue_mask)
+        )(corners, own, level_use, forward, *rest, *more)
+
+    message = flow(next_kernel, (sections, 3, patches), wide_spec, next_tile, col_tables, tissue_mask)
     shared = lax.all_to_all(message, "sec", 0, 0)
-    flow_skip = flow(skip_kernel, (2, patches), even_tile, odd_tile)
+    flow_skip = flow(skip_kernel, (2, patches), own_spec, even_tile, odd_tile)
     out = jax.ShapeDtypeStruct((1, 2, patches), jnp.float32)
     return pl.pallas_call(
         combine_kernel,

time: 29 us -> 29 us (level)
  no operation moved by 1% of the time
where the time goes in v9:
time: 29 us; the launch traced here: 28.7 us
  starting transfers between devices  13.9 us (48%)
  Pallas kernels  10.3 us (36%)
  waiting for transfers between devices  3.6 us (12%)
  between operations  0.84 us (3%)
    all_to_all x1, starting transfers between devices, on_device(): shared = lax.all_to_all(message, 'sec', 0, 0)  10.7 us
    pallas_call x2, Pallas kernels, flow(): pl.pallas_call(kernel, out_shape=jax.ShapeDtypeStruct(out_shape, jnp.floa...  6.37 us
    pallas_call x1, Pallas kernels, on_device(): pl.pallas_call(own_kernel, out_shape=(spec, jax.ShapeDtypeStruct(spec.sha...  3.34 us
    ppermute x3, starting transfers between devices, moved(): return lax.ppermute(block, axis, route)  3.28 us
    ppermute x3, waiting for transfers between devices, moved(): return lax.ppermute(block, axis, route)  2.34 us
    all_to_all x1, waiting for transfers between devices, on_device(): shared = lax.all_to_all(message, 'sec', 0, 0)  1.26 us
    pallas_call x1, Pallas kernels, on_device(): pl.pallas_call(combine_kernel, out_shape=(out, out, out), in_specs=[vmem,...  0.58 us
  transfers between devices with their start and end apart: 4, of which 2 were waited for; matrix products, arithmetic and copies ran while one was open for 0% of the time, Pallas kernels for 34%

profile of v9, /device:TPU:0, one launch (start us, length us, event | category | flops | bytes accessed | tf_op | source)
XLA Modules:
  0.0 28.7 jit_solution(7197654521692450195)
XLA Ops:
  0.6 1.3 %collective-permute-start = (bf16[512,512]{1,0:T(8,128)(2,1)}, bf16[512,512]{1,0:T(8,128)(2,1)S(1)}, u32[]{:S(2)}, u32[]{:S(2)}) collective-permute-start(bf16[512,512]{1,0:T(8,128)(2,1)} %bitcast.1.tile_ref), channel_id=1, source_target_pairs={{1,0},{2,1},{3,2},{4,3},{5,4},{6,5},{7,6},{8,7},{9,8},{10,9},{11,1... | collective-permute-start | bytes 1572872 | tf_op jit(solution)/shard_map/ppermute | solution.py:351
  1.9 1.3 %collective-permute-start.1 = (bf16[512,512]{1,0:T(8,128)(2,1)}, bf16[512,512]{1,0:T(8,128)(2,1)S(1)}, u32[]{:S(2)}, u32[]{:S(2)}) collective-permute-start(bf16[512,512]{1,0:T(8,128)(2,1)} %bitcast.1.tile_ref), channel_id=1, source_target_pairs={{2,0},{4,2},{6,4},{8,6},{10,8},{12,10},{14,12},{18,16},{20,18},{22... | collective-permute-start | bytes 1572872 | tf_op jit(solution)/shard_map/ppermute | solution.py:351
  3.2 0.0 copy-start
  3.2 0.0 copy-start.1
  3.3 0.0 copy-start.2
  3.3 0.0 copy-start.3
  3.3 0.0 copy-start.4
  3.3 0.0 copy-start.5
  3.3 0.0 copy-start.6
  3.3 0.0 copy-start.7
  3.3 0.0 copy-start.8
  3.3 0.0 copy-start.9
  3.3 3.3 %own_spectrum.1 = (bf16[16,128,256]{2,1,0:T(8,128)(2,1)S(1)}, f32[16,128,256]{2,1,0:T(8,128)S(1)}, bf16[16,256,256]{2,1,0:T(8,128)(2,1)S(1)}) custom-call(s32[2,32]{1,0:T(2,128)} %bitcast.2, bf16[512,512]{1,0:T(8,128)(2,1)} %bitcast.1.tile_ref, f32[768,128]{1,0:T(8,128)} %constant.14.clone.tables_ref.refs_3_), custom_call_target="tpu_custom_call" | custom-call | flops 4000000000 | bytes 3145728 | tf_op jit(solution)/shard_map/own_spectrum/pallas_call | solution.py:371
  6.7 0.7 %collective-permute-start.2 = (bf16[512,512]{1,0:T(8,128)(2,1)}, bf16[512,512]{1,0:T(8,128)(2,1)S(1)}, u32[]{:S(2)}, u32[]{:S(2)}) collective-permute-start(bf16[512,512]{1,0:T(8,128)(2,1)} %bitcast.1.tile_ref), channel_id=1, source_target_pairs={{3,1},{5,3},{7,5},{9,7},{11,9},{13,11},{15,13},{19,17},{21,19},{23... | collective-permute-start | bytes 1572872 | tf_op jit(solution)/shard_map/ppermute | solution.py:351
  7.4 0.0 collective-permute-done.refs_10_
  7.4 0.0 copy-done
  7.4 0.0 copy-done.1
  7.4 0.0 copy-done.2
  7.4 0.0 copy-done.3
  7.5 0.0 copy-done.4
  7.5 0.0 copy-done.5
  7.5 0.0 copy-done.6
  7.5 0.0 copy-done.7
  7.5 0.0 copy-done.8
  7.5 0.0 copy-done.9
  7.5 3.3 %shard_map.130 = f32[16,3,32]{2,1,0:T(4,128)} custom-call(s32[2,32]{1,0:T(2,128)S(1)} %bitcast.3, f32[16,128,256]{2,1,0:T(8,128)S(1)} %get-tuple-element.8.refs_1_, s32[3,32]{1,0:T(4,128)S(1)} %copy-done, f32[768,128]{1,0:T(8,128)S(1)} %copy-done.4, bf16[256,256]{1,0:T(8,128)(2,1)S(1)} %copy-done.5, bf16[256,128]{1,0:T(8,128)(2,1)S(1)} %copy-done.6, ...), custom_call_target="tpu_custom_call" | custom-call | flops 8000000000 | bytes 4194304 | tf_op jit(solution)/shard_map/pallas_call | solution.py:395
  10.8 10.7 %all-to-all-start = ((f32[16,3,32]{2,1,0:T(4,128)}), f32[16,3,32]{2,1,0:T(4,128)S(1)}, u32[]{:S(2)}, u32[]{:S(2)}) async-start(f32[16,3,32]{2,1,0:T(4,128)} %shard_map.130), calls=%async_computation | async-start | bytes 65536 | tf_op jit(solution)/shard_map/all_to_all | solution.py:416
  21.5 2.3 %collective-permute-done.1.refs_10_ = bf16[512,512]{1,0:T(8,128)(2,1)S(1)} collective-permute-done((bf16[512,512]{1,0:T(8,128)(2,1)}, bf16[512,512]{1,0:T(8,128)(2,1)S(1)}, u32[]{:S(2)}, u32[]{:S(2)}) %collective-permute-start.1) | collective-permute-done | bytes 524320 | tf_op jit(solution)/shard_map/ppermute | solution.py:351
  23.8 0.0 collective-permute-done.2.refs_11_
  23.8 3.0 %shard_map.131.skip_ref = f32[2,32]{1,0:T(2,128)S(1)} custom-call(s32[2,32]{1,0:T(2,128)S(1)} %bitcast.4, bf16[16,128,256]{2,1,0:T(8,128)(2,1)S(1)} %get-tuple-element.11.refs_1_, s32[3,32]{1,0:T(4,128)S(1)} %copy-done, f32[768,128]{1,0:T(8,128)S(1)} %copy-done.4, bf16[256,256]{1,0:T(8,128)(2,1)S(1)} %copy-done.5, bf16[256,128]{1,0:T(8,128)(2,1)S(1)} %copy-done.6, ...), custom_call_target="tpu_custom_call" | custom-call | flops 8000000000 | bytes 4194304 | tf_op jit(solution)/shard_map/pallas_call | solution.py:395
  26.9 1.3 %all-to-all-done.shared_ref = f32[16,3,32]{2,1,0:T(4,128)S(1)} async-done(((f32[16,3,32]{2,1,0:T(4,128)}), f32[16,3,32]{2,1,0:T(4,128)S(1)}, u32[]{:S(2)}, u32[]{:S(2)}) %all-to-all-start) | async-done | bytes 6176 | tf_op jit(solution)/shard_map/all_to_all | solution.py:416
  28.1 0.6 %combine.1 = (f32[1,2,32]{2,1,0:T(2,128)}, f32[1,2,32]{2,1,0:T(2,128)}, f32[1,2,32]{2,1,0:T(2,128)}) custom-call(f32[16,3,32]{2,1,0:T(4,128)S(1)} %all-to-all-done.shared_ref, f32[2,32]{1,0:T(2,128)S(1)} %shard_map.131.skip_ref), custom_call_target="tpu_custom_call" | custom-call | tf_op jit(solution)/shard_map/combine/pallas_call | solution.py:419
Async XLA Ops:
  0.6 6.8 %collective-permute-start = (bf16[512,512]{1,0:T(8,128)(2,1)}, bf16[512,512]{1,0:T(8,128)(2,1)S(1)}, u32[]{:S(2)}, u32[]{:S(2)}) collective-permute-start(bf16[512,512]{1,0:T(8,128)(2,1)} %bitcast.1.tile_ref), channel_id=1, source_target_pairs={{1,0},{2,1},{3,2},{4,3},{5,4},{6,5},{7,6},{8,7},{9,8},{10,9},{11,1... | collective-permute-start | bytes 1572872 | tf_op jit(solution)/shard_map/ppermute | solution.py:351
  1.9 21.9 %collective-permute-start.1 = (bf16[512,512]{1,0:T(8,128)(2,1)}, bf16[512,512]{1,0:T(8,128)(2,1)S(1)}, u32[]{:S(2)}, u32[]{:S(2)}) collective-permute-start(bf16[512,512]{1,0:T(8,128)(2,1)} %bitcast.1.tile_ref), channel_id=1, source_target_pairs={{2,0},{4,2},{6,4},{8,6},{10,8},{12,10},{14,12},{18,16},{20,18},{22... | collective-permute-start | bytes 1572872 | tf_op jit(solution)/shard_map/ppermute | solution.py:351
  3.2 4.2 %copy-start = (s32[3,32]{1,0:T(4,128)S(1)}, s32[3,32]{1,0:T(4,128)}, u32[]{:S(2)}) copy-start(s32[3,32]{1,0:T(4,128)} %refs_2_.3) | copy-start | bytes 1156
  3.2 4.2 %copy-start.1 = (s32[32,2]{0,1:T(2,128)S(1)}, s32[32,2]{0,1:T(2,128)}, u32[]{:S(2)}) copy-start(s32[32,2]{0,1:T(2,128)} %param.12) | copy-start | bytes 772
  3.3 4.2 %copy-start.2 = (s32[1,32]{1,0:T(1,128)S(1)}, s32[1,32]{1,0:T(1,128)}, u32[]{:S(2)}) copy-start(s32[1,32]{1,0:T(1,128)} %refs_12_.1) | copy-start | bytes 388
  3.3 4.2 %copy-start.3 = (bf16[5,256,256]{2,1,0:T(8,128)(2,1)S(1)}, bf16[5,256,256]{2,1,0:T(8,128)(2,1)}, u32[]{:S(2)}) copy-start(bf16[5,256,256]{2,1,0:T(8,128)(2,1)} %constant.18.clone.refs_7_) | copy-start | bytes 1966084
  3.3 4.2 %copy-start.4 = (f32[768,128]{1,0:T(8,128)S(1)}, f32[768,128]{1,0:T(8,128)}, u32[]{:S(2)}) copy-start(f32[768,128]{1,0:T(8,128)} %constant.14.clone.tables_ref.refs_3_) | copy-start | bytes 1179652
  3.3 4.2 %copy-start.5 = (bf16[256,256]{1,0:T(8,128)(2,1)S(1)}, bf16[256,256]{1,0:T(8,128)(2,1)}, u32[]{:S(2)}) copy-start(bf16[256,256]{1,0:T(8,128)(2,1)} %constant.15.clone.refs_4_) | copy-start | bytes 393220
  3.3 4.2 %copy-start.6 = (bf16[256,128]{1,0:T(8,128)(2,1)S(1)}, bf16[256,128]{1,0:T(8,128)(2,1)}, u32[]{:S(2)}) copy-start(bf16[256,128]{1,0:T(8,128)(2,1)} %constant.16.clone.refs_5_) | copy-start | bytes 196612
  3.3 4.2 %copy-start.7 = (bf16[128,64]{1,0:T(8,128)(2,1)S(1)}, bf16[128,64]{1,0:T(8,128)(2,1)}, u32[]{:S(2)}) copy-start(bf16[128,64]{1,0:T(8,128)(2,1)} %constant.17.clone.refs_6_) | copy-start | bytes 49156
  3.3 4.2 %copy-start.8 = (f32[64,128]{1,0:T(8,128)S(1)}, f32[64,128]{1,0:T(8,128)}, u32[]{:S(2)}) copy-start(f32[64,128]{1,0:T(8,128)} %constant.20.clone.refs_9_) | copy-start | bytes 98308
  3.3 4.2 %copy-start.9 = (f32[2,8,128]{2,1,0:T(8,128)S(1)}, f32[2,8,128]{2,1,0:T(8,128)}, u32[]{:S(2)}) copy-start(f32[2,8,128]{2,1,0:T(8,128)} %constant.19.clone.refs_8_) | copy-start | bytes 24580
  6.7 17.1 %collective-permute-start.2 = (bf16[512,512]{1,0:T(8,128)(2,1)}, bf16[512,512]{1,0:T(8,128)(2,1)S(1)}, u32[]{:S(2)}, u32[]{:S(2)}) collective-permute-start(bf16[512,512]{1,0:T(8,128)(2,1)} %bitcast.1.tile_ref), channel_id=1, source_target_pairs={{3,1},{5,3},{7,5},{9,7},{11,9},{13,11},{15,13},{19,17},{21,19},{23... | collective-permute-start | bytes 1572872 | tf_op jit(solution)/shard_map/ppermute | solution.py:351
  10.8 17.3 %all-to-all-start = ((f32[16,3,32]{2,1,0:T(4,128)}), f32[16,3,32]{2,1,0:T(4,128)S(1)}, u32[]{:S(2)}, u32[]{:S(2)}) async-start(f32[16,3,32]{2,1,0:T(4,128)} %shard_map.130), calls=%async_computation | async-start | bytes 65536 | tf_op jit(solution)/shard_map/all_to_all | solution.py:416
